TPU v7x, 512 devices: a whole 4x8x8 slice. The times are simulated.
512 devices in a mesh: seq: 64 (over z, y_hi, core), head: 8 (over y_lo, x).
Axes of the slice: x: 4, y: 8 (y_hi: 4, y_lo: 2; y = y_hi * 2 + y_lo), z: 8, core: 2. Of those that a mesh axis runs over, the one named last changes fastest.
Arguments:
- qkv: bfloat16 [3, 8192, 4096], P(None, ('seq', 'head')), may hold values from -128 to 128
- token_rate: float32 [8192, 8], P('seq', 'head'), may hold values from 0.1 to 1
- head_rate: float32 [8], P('head'), may hold values from 0.5 to 2
- fast_state: float32 [3, 8, 512, 512], P(None, 'head', 'seq'), may hold values from -0.25 to 0.25
Outputs:
- combined: bfloat16 [8192, 4096], P(('seq', 'head'))
- new_state: float32 [3, 8, 512, 512], P(None, 'head', 'seq')
All inputs are finite; a program needn't handle non-finite values.
Results may differ from a plain program's by a relative error of at most 0.017.
Values may be sent and summed in bfloat16 or wider, within the bound.
No kernel may reach another device: no remote copies, remote signals or barrier semaphores. Data moves between devices by JAX's collectives and lax.ppermute only.
A program may use at most 64 MiB of HBM per device.

v0:
```python
import jax
import jax.numpy as jnp
from jax import lax
from jax.sharding import Mesh
from jax.sharding import PartitionSpec as P

WINDOW = 1024
NS_STEPS = 2
SEQ = ("seq_0", "seq_1", "seq_2")
SEQ_HEAD = ("seq_0", "seq_1", "seq_2", "head")


ns_first = 3.4445
ns_second = -4.775
ns_third = 2.0315
rms_eps = 1e-06
norm_eps = 1e-07
precise = lax.Precision.HIGHEST


def sent_to_all(shard, axis):
    copies = jnp.broadcast_to(shard, (lax.axis_size(axis), *shard.shape))
    return lax.all_to_all(copies, axis, split_axis=0, concat_axis=0, tiled=True)


def joined_along(pieces, dim):
    pieces = jnp.moveaxis(pieces, 0, dim)
    dims = pieces.shape
    return pieces.reshape(*dims[:dim], dims[dim] * dims[dim + 1], *dims[dim + 2 :])


def whole_of(shard, axes, dim):
    far, near = axes
    initial = sent_to_all(shard, far)
    pieces = jnp.swapaxes(sent_to_all(initial, near), 0, 1)
    return joined_along(pieces.reshape(-1, *shard.shape), dim)


def in_blocks(shard, dim, devices):
    dims = shard.shape
    pieces = shard.reshape(*dims[:dim], devices, dims[dim] // devices, *dims[dim + 1 :])
    return jnp.moveaxis(pieces, dim, 0)


def sent_and_summed(shard, axis, dim):
    devices = lax.axis_size(axis)
    pieces = lax.all_to_all(in_blocks(shard, dim, devices), axis, 0, 0, tiled=True)
    return jnp.sum(pieces.astype(jnp.float32), axis=0)


def sum_by_axis(shard, axes, dim):
    far, near = axes
    pieces = in_blocks(shard, dim, lax.axis_size(far))
    nearer = sent_and_summed(pieces, near, dim + 1)
    arrived = lax.all_to_all(
        nearer.astype(jnp.bfloat16), far, split_axis=0, concat_axis=0, tiled=True
    )
    return arrived.astype(jnp.float32).sum(axis=0)


def rows_for(lines, devices):
    spare = -lines.shape[0] % devices
    if not spare:
        return lines
    return jnp.concatenate([lines, jnp.zeros((spare, *lines.shape[1:]), lines.dtype)])


def sum_by_parts(shard, axes):
    lines = shard.reshape(-1, shard.shape[-1])
    own = sum_by_axis(rows_for(lines, lax.axis_size(axes[0]) * lax.axis_size(axes[1])), axes, 0)
    whole = whole_of(own.astype(jnp.bfloat16), axes, 0)
    return whole[: len(lines)].reshape(shard.shape).astype(jnp.float32)


def from_behind(block, axis, distance):
    devices = range(lax.axis_size(axis))
    route = [(i - distance, i) for i in devices if i - distance in devices]
    return lax.ppermute(block, axis, route)


def rms_scaled(values):
    return values * lax.rsqrt(jnp.mean(values * values, axis=-1, keepdims=True) + rms_eps)


def contract_last(left_side, right_side):
    return lax.dot_general(
        left_side, right_side, (((1,), (1,)), ((), ())), preferred_element_type=jnp.float32
    )


def contract_first(left_side, right_side):
    return lax.dot_general(
        left_side, right_side, (((0,), (0,)), ((), ())), preferred_element_type=jnp.float32
    )


def head_gradient(key_norm, signal, weight_piece):
    gate_act = contract_last(key_norm, weight_piece[0])
    up_act = contract_last(key_norm, weight_piece[1])
    active = (jax.nn.silu(gate_act) * up_act).astype(jnp.bfloat16)
    back_grad = contract_last(signal, weight_piece[2])
    sigmoid_gate = jax.nn.sigmoid(gate_act)
    grad_gate = (
        back_grad * up_act * sigmoid_gate * (1.0 + gate_act * (1.0 - sigmoid_gate))
    ).astype(jnp.bfloat16)
    grad_up = (back_grad * jax.nn.silu(gate_act)).astype(jnp.bfloat16)
    return jnp.stack(
        [
            contract_first(grad_gate, key_norm),
            contract_first(grad_up, key_norm),
            contract_first(active, signal),
        ]
    )


def gram_times(gram_matrix, section_number, row_block):
    if section_number == 0:
        return jnp.einsum("mij,mjk->mik", row_block, gram_matrix, precision=precise)
    once_moved = gram_times(gram_matrix, section_number - 1, row_block)
    return poly_times(
        gram_matrix, section_number - 1, poly_times(gram_matrix, section_number - 1, once_moved)
    )


def poly_times(gram_matrix, section_number, row_block):
    moved_once = gram_times(gram_matrix, section_number, row_block)
    moved_twice = gram_times(gram_matrix, section_number, moved_once)
    return ns_first * row_block + ns_second * moved_once + ns_third * moved_twice


def shards(qkv, token_rate, head_rate, fast_state):
    grouped = lax.all_to_all(qkv, "head", split_axis=2, concat_axis=1, tiled=True)
    tok_rows = grouped.shape[1]
    head_dim = grouped.shape[2]
    seq_index = lax.axis_index(SEQ)
    state_rows = fast_state.shape[2]
    query_norm = rms_scaled(grouped[0].astype(jnp.float32)).astype(jnp.bfloat16)
    key_norm = rms_scaled(grouped[1].astype(jnp.float32)).astype(jnp.bfloat16)
    signal = (-token_rate * grouped[2].astype(jnp.float32)).astype(jnp.bfloat16)
    old_state = fast_state[:, 0]
    old_low = old_state.astype(jnp.bfloat16)
    partial_value = head_gradient(
        key_norm, signal, whole_of(old_low, (("seq_0", "seq_1"), "seq_2"), 1)
    )
    summed = sum_by_parts(partial_value.astype(jnp.bfloat16), (("seq_0", "seq_1"), "seq_2"))
    frob_norm = jnp.sqrt(jnp.sum(summed * summed, axis=(1, 2), keepdims=True))
    normalized = summed / (frob_norm + norm_eps)
    gram_matrix = jnp.einsum("mij,mkj->mik", normalized, normalized, precision=precise)
    hidden_units = gram_matrix.shape[1]
    selector = (
        jnp.arange(hidden_units, dtype=jnp.int32)[None, :]
        == seq_index * state_rows + jnp.arange(state_rows, dtype=jnp.int32)[:, None]
    ).astype(jnp.float32)
    row_block = jnp.broadcast_to(selector, (3, state_rows, hidden_units))
    for section_number in range(NS_STEPS - 1, -1, -1):
        row_block = poly_times(gram_matrix, section_number, row_block)
    final_rows = jnp.einsum("mij,mjk->mik", row_block, normalized, precision=precise)
    new_rows = old_state - head_rate[0] * final_rows
    weight_piece = whole_of(new_rows.astype(jnp.bfloat16), (("seq_0", "seq_1"), "seq_2"), 1)
    gate_act = contract_last(query_norm, weight_piece[0])
    up_act = contract_last(query_norm, weight_piece[1])
    active = (jax.nn.silu(gate_act) * up_act).astype(jnp.bfloat16)
    fast_out = jnp.dot(active, weight_piece[2], preferred_element_type=jnp.float32)
    key_value = grouped[1:3]
    reach_blocks = WINDOW // tok_rows
    earlier = [from_behind(key_value, SEQ, distance) for distance in range(reach_blocks, 0, -1)]
    context = jnp.concatenate(earlier + [key_value], axis=1)
    scores = contract_last(grouped[0], context[0]) * head_dim ** (-0.5)
    query_pos = seq_index * tok_rows + jnp.arange(tok_rows, dtype=jnp.int32)[:, None]
    key_pos = (
        seq_index * tok_rows - WINDOW + jnp.arange(WINDOW + tok_rows, dtype=jnp.int32)[None, :]
    )
    visible = (key_pos <= query_pos) & (key_pos > query_pos - WINDOW) & (key_pos >= 0)
    scores = jnp.where(visible, scores, -jnp.inf)
    row_max = jnp.max(scores, axis=1, keepdims=True)
    exp_scores = jnp.exp(scores - row_max)
    weights = (exp_scores / jnp.sum(exp_scores, axis=1, keepdims=True)).astype(jnp.bfloat16)
    attention = jnp.dot(weights, context[1], preferred_element_type=jnp.float32)
    combined = (attention + fast_out).astype(jnp.bfloat16)
    tokens_back = lax.all_to_all(combined, "head", split_axis=0, concat_axis=1, tiled=True)
    return (tokens_back, new_rows[:, None])


def solution(mesh):
    finer = Mesh(
        mesh.devices.reshape(8, 4, 2, mesh.shape["head"]), ("seq_0", "seq_1", "seq_2", "head")
    )
    return jax.shard_map(
        shards,
        mesh=finer,
        in_specs=(P(None, SEQ_HEAD, None), P(SEQ, "head"), P("head"), P(None, "head", SEQ, None)),
        out_specs=(P(SEQ_HEAD, None), P(None, "head", SEQ, None)),
        check_vma=False,
    )
```

profile of v0, /device:TPU:64, one launch (start us, length us, event | category | flops | bytes accessed | tf_op | source)
XLA Modules:
  0.0 280.3 jit_solution(18188262417285728206)
XLA Ops:
  0.6 5.7 %copy.58 = bf16[3,16,4096]{1,0,2:T(4,128)(2,1)} copy(bf16[3,16,4096]{2,1,0:T(8,128)(2,1)} %param.4) | data formatting | bytes 786432 | tf_op args[0]
  6.3 7.4 %reshape.152 = bf16[8,2,12288]{2,1,0:T(2,128)(2,1)} reshape(bf16[4096,3,16]{2,1,0:T(4,128)(2,1)} %bitcast.124) | data formatting | bytes 786432
  13.7 5.4 %all-to-all-start = ((bf16[8,2,12288]{2,1,0:T(2,128)(2,1)}), bf16[8,2,12288]{2,1,0:T(2,128)(2,1)S(1)}, u32[]{:S(2)}, u32[]{:S(2)}) async-start(bf16[8,2,12288]{2,1,0:T(2,128)(2,1)} %reshape.152), calls=%async_computation | async-start | bytes 786432 | tf_op jit(solution)/shard_map/all_to_all | solution.py:132
  19.2 8.4 %all-to-all-done = bf16[8,2,12288]{2,1,0:T(2,128)(2,1)S(1)} async-done(((bf16[8,2,12288]{2,1,0:T(2,128)(2,1)}), bf16[8,2,12288]{2,1,0:T(2,128)(2,1)S(1)}, u32[]{:S(2)}, u32[]{:S(2)}) %all-to-all-start) | async-done | bytes 393248 | tf_op jit(solution)/shard_map/all_to_all | solution.py:132
  27.6 0.9 broadcast_in_dim.42
  28.6 14.5 %all-to-all-start.1 = ((bf16[32,3,8,512]{3,2,1,0:T(8,128)(2,1)}), bf16[32,3,8,512]{3,2,1,0:T(8,128)(2,1)S(1)}, u32[]{:S(2)}, u32[]{:S(2)}) async-start(bf16[32,3,8,512]{3,2,1,0:T(8,128)(2,1)} %broadcast_in_dim.42), calls=%async_computation.1 | async-start | bytes 1572864 | tf_op jit(solution)/shard_map/all_to_all | solution.py:23
  43.3 5.6 %reshape.153 = bf16[4096,3,16]{2,1,0:T(4,128)(2,1)} reshape(bf16[8,2,12288]{2,1,0:T(2,128)(2,1)S(1)} %all-to-all-done) | data formatting | bytes 786432
  48.8 4.2 %copy.75 = bf16[3,16,8,512]{3,2,1,0:T(8,128)(2,1)S(1)} copy(bf16[3,16,8,512]{1,0,3,2:T(4,128)(2,1)} %bitcast.123) | data formatting | bytes 786432 | tf_op jit(solution)/shard_map/all_to_all | solution.py:132
  54.1 9.4 %all-to-all-done.1 = bf16[32,3,8,512]{3,2,1,0:T(8,128)(2,1)S(1)} async-done(((bf16[32,3,8,512]{3,2,1,0:T(8,128)(2,1)}), bf16[32,3,8,512]{3,2,1,0:T(8,128)(2,1)S(1)}, u32[]{:S(2)}, u32[]{:S(2)}) %all-to-all-start.1) | async-done | bytes 786464 | tf_op jit(solution)/shard_map/all_to_all | solution.py:23
  63.7 5.0 %all_to_all.74 = bf16[2,32,3,8,512]{4,3,2,1,0:T(8,128)(2,1)S(1)} all-to-all(bf16[2,32,3,8,512]{4,3,2,1,0:T(8,128)(2,1)S(1)} %broadcast_in_dim.43), channel_id=1, replica_groups=mesh['seq_0'=8,'seq_1'=4,'seq_2'=2,'head'=8] {'seq_2'}, dimensions={0} | all-to-all | bytes 3145728 | tf_op jit(solution)/shard_map/all_to_all | solution.py:23
  71.1 5.0 %all_to_all.75 = bf16[2,32,24,512]{3,2,1,0:T(8,128)(2,1)S(1)} all-to-all(bf16[2,32,24,512]{3,2,1,0:T(8,128)(2,1)S(1)} %bitcast.133), channel_id=1, replica_groups=mesh['seq_0'=8,'seq_1'=4,'seq_2'=2,'head'=8] {'seq_2'}, dimensions={0} | all-to-all | bytes 3145728 | tf_op jit(solution)/shard_map/all_to_all | solution.py:47
  76.1 0.8 reduce_sum.72
  76.9 33.5 %all_to_all.76 = bf16[32,24,512]{2,1,0:T(8,128)(2,1)S(1)} all-to-all(bf16[32,24,512]{2,1,0:T(8,128)(2,1)S(1)} %reduce_sum.72), channel_id=1, replica_groups=mesh['seq_0'=8,'seq_1'=4,'seq_2'=2,'head'=8] {'seq_0','seq_1'}, dimensions={0} | all-to-all | bytes 1572864 | tf_op jit(solution)/shard_map/all_to_all | solution.py:55
  110.6 0.9 broadcast_in_dim.44
  111.5 8.4 %all-to-all-start.5 = ((bf16[32,24,512]{2,1,0:T(8,128)(2,1)}), bf16[32,24,512]{2,1,0:T(8,128)(2,1)S(1)}, u32[]{:S(2)}, u32[]{:S(2)}) async-start(bf16[32,24,512]{2,1,0:T(8,128)(2,1)} %broadcast_in_dim.44), calls=%async_computation.5 | async-start | bytes 1572864 | tf_op jit(solution)/shard_map/all_to_all | solution.py:23
  120.9 3.4 %collective-permute-start = (bf16[2,128,512]{2,1,0:T(8,128)(2,1)S(1)}, bf16[2,128,512]{2,1,0:T(8,128)(2,1)S(1)}, u32[]{:S(2)}, u32[]{:S(2)}) collective-permute-start(bf16[2,128,512]{2,1,0:T(8,128)(2,1)S(1)} %bitcast.140), channel_id=1, source_target_pairs={{0,64},{8,72},{16,80},{24,88},{32,96},{40,104},{48,112},{56,120},{... | collective-permute-start | bytes 786440 | tf_op jit(solution)/shard_map/ppermute | solution.py:78
  124.2 1.9 collective-permute-start.1
  126.2 5.5 %collective-permute-start.2 = (bf16[2,128,512]{2,1,0:T(8,128)(2,1)S(1)}, bf16[2,128,512]{2,1,0:T(8,128)(2,1)S(1)}, u32[]{:S(2)}, u32[]{:S(2)}) collective-permute-start(bf16[2,128,512]{2,1,0:T(8,128)(2,1)S(1)} %bitcast.142), channel_id=1, source_target_pairs={{0,48},{8,56},{16,64},{24,72},{32,80},{40,88},{48,96},{56,104},{64... | collective-permute-start | bytes 786440 | tf_op jit(solution)/shard_map/ppermute | solution.py:78
  131.7 9.4 %all-to-all-done.5 = bf16[32,24,512]{2,1,0:T(8,128)(2,1)S(1)} async-done(((bf16[32,24,512]{2,1,0:T(8,128)(2,1)}), bf16[32,24,512]{2,1,0:T(8,128)(2,1)S(1)}, u32[]{:S(2)}, u32[]{:S(2)}) %all-to-all-start.5) | async-done | bytes 786464 | tf_op jit(solution)/shard_map/all_to_all | solution.py:23
  141.2 5.0 %all_to_all.77 = bf16[2,32,24,512]{3,2,1,0:T(8,128)(2,1)S(1)} all-to-all(bf16[2,32,24,512]{3,2,1,0:T(8,128)(2,1)S(1)} %broadcast_in_dim.45), channel_id=1, replica_groups=mesh['seq_0'=8,'seq_1'=4,'seq_2'=2,'head'=8] {'seq_2'}, dimensions={0} | all-to-all | bytes 3145728 | tf_op jit(solution)/shard_map/all_to_all | solution.py:23
  147.3 5.7 %fusion.18 = f32[3,512,512]{2,1,0:T(8,128)S(1)} fusion(f32[3,512,512]{2,1,0:T(8,128)S(1)} %bitcast.134, f32[3]{0:T(128)S(1)} %sqrt_add_fusion), kind=kOutput, calls=%fused_computation.38 | convolution fusion | flops 4832624640 | bytes 6291468 | tf_op jit(solution)/shard_map/mij,mkj->mik/dot_general | solution.py:148
  152.9 1.6 fusion.40
  154.5 1.6 fusion.51
  156.1 1.6 fusion.17
  157.7 1.6 fusion.52
  159.3 1.8 fusion.16
  161.1 1.6 fusion.53
  162.7 1.6 fusion.54
  164.3 1.6 fusion.15
  165.9 1.6 fusion.55
  167.5 1.6 fusion.14
  169.1 1.6 fusion.56
  170.7 1.6 fusion.11
  172.3 2.6 fusion.49
  174.9 0.9 broadcast_in_dim.46
  175.9 11.6 %all-to-all-start.7 = ((bf16[32,3,8,512]{3,2,1,0:T(8,128)(2,1)}), bf16[32,3,8,512]{3,2,1,0:T(8,128)(2,1)S(1)}, u32[]{:S(2)}, u32[]{:S(2)}) async-start(bf16[32,3,8,512]{3,2,1,0:T(8,128)(2,1)} %broadcast_in_dim.46), calls=%async_computation.7 | async-start | bytes 1572864 | tf_op jit(solution)/shard_map/all_to_all | solution.py:23
  187.5 6.5 %collective-permute-start.3 = (bf16[2,128,512]{2,1,0:T(8,128)(2,1)S(1)}, bf16[2,128,512]{2,1,0:T(8,128)(2,1)S(1)}, u32[]{:S(2)}, u32[]{:S(2)}) collective-permute-start(bf16[2,128,512]{2,1,0:T(8,128)(2,1)S(1)} %bitcast.143), channel_id=1, source_target_pairs={{0,40},{8,48},{16,56},{24,64},{32,72},{40,80},{48,88},{56,96},{64,... | collective-permute-start | bytes 786440 | tf_op jit(solution)/shard_map/ppermute | solution.py:78
  194.0 3.4 %collective-permute-start.4 = (bf16[2,128,512]{2,1,0:T(8,128)(2,1)S(1)}, bf16[2,128,512]{2,1,0:T(8,128)(2,1)S(1)}, u32[]{:S(2)}, u32[]{:S(2)}) collective-permute-start(bf16[2,128,512]{2,1,0:T(8,128)(2,1)S(1)} %bitcast.144), channel_id=1, source_target_pairs={{0,32},{8,40},{16,48},{24,56},{32,64},{40,72},{48,80},{56,88},{64,... | collective-permute-start | bytes 786440 | tf_op jit(solution)/shard_map/ppermute | solution.py:78
  197.5 4.5 %collective-permute-start.5 = (bf16[2,128,512]{2,1,0:T(8,128)(2,1)S(1)}, bf16[2,128,512]{2,1,0:T(8,128)(2,1)S(1)}, u32[]{:S(2)}, u32[]{:S(2)}) collective-permute-start(bf16[2,128,512]{2,1,0:T(8,128)(2,1)S(1)} %bitcast.145), channel_id=1, source_target_pairs={{0,24},{8,32},{16,40},{24,48},{32,56},{40,64},{48,72},{56,80},{64,... | collective-permute-start | bytes 786440 | tf_op jit(solution)/shard_map/ppermute | solution.py:78
  202.1 3.7 %collective-permute-start.6 = (bf16[2,128,512]{2,1,0:T(8,128)(2,1)S(1)}, bf16[2,128,512]{2,1,0:T(8,128)(2,1)S(1)}, u32[]{:S(2)}, u32[]{:S(2)}) collective-permute-start(bf16[2,128,512]{2,1,0:T(8,128)(2,1)S(1)} %bitcast.146), channel_id=1, source_target_pairs={{0,16},{8,24},{16,32},{24,40},{32,48},{40,56},{48,64},{56,72},{64,... | collective-permute-start | bytes 786440 | tf_op jit(solution)/shard_map/ppermute | solution.py:78
  205.8 3.3 %collective-permute-start.7 = (bf16[2,128,512]{2,1,0:T(8,128)(2,1)S(1)}, bf16[2,128,512]{2,1,0:T(8,128)(2,1)S(1)}, u32[]{:S(2)}, u32[]{:S(2)}) collective-permute-start(bf16[2,128,512]{2,1,0:T(8,128)(2,1)S(1)} %bitcast.147), channel_id=1, source_target_pairs={{0,8},{8,16},{16,24},{24,32},{32,40},{40,48},{48,56},{56,64},{64,7... | collective-permute-start | bytes 786440 | tf_op jit(solution)/shard_map/ppermute | solution.py:78
  209.1 5.0 %collective-permute-done.3 = bf16[2,128,512]{2,1,0:T(8,128)(2,1)S(1)} collective-permute-done((bf16[2,128,512]{2,1,0:T(8,128)(2,1)S(1)}, bf16[2,128,512]{2,1,0:T(8,128)(2,1)S(1)}, u32[]{:S(2)}, u32[]{:S(2)}) %collective-permute-start.3) | collective-permute-done | bytes 262176 | tf_op jit(solution)/shard_map/ppermute | solution.py:78
  214.2 21.4 %collective-permute-done.4 = bf16[2,128,512]{2,1,0:T(8,128)(2,1)S(1)} collective-permute-done((bf16[2,128,512]{2,1,0:T(8,128)(2,1)S(1)}, bf16[2,128,512]{2,1,0:T(8,128)(2,1)S(1)}, u32[]{:S(2)}, u32[]{:S(2)}) %collective-permute-start.4) | collective-permute-done | bytes 262176 | tf_op jit(solution)/shard_map/ppermute | solution.py:78
  235.7 10.4 %collective-permute-done.6 = bf16[2,128,512]{2,1,0:T(8,128)(2,1)S(1)} collective-permute-done((bf16[2,128,512]{2,1,0:T(8,128)(2,1)S(1)}, bf16[2,128,512]{2,1,0:T(8,128)(2,1)S(1)}, u32[]{:S(2)}, u32[]{:S(2)}) %collective-permute-start.6) | collective-permute-done | bytes 262176 | tf_op jit(solution)/shard_map/ppermute | solution.py:78
  246.7 0.9 copy-done.2
  247.9 5.0 %all_to_all.78 = bf16[2,32,3,8,512]{4,3,2,1,0:T(8,128)(2,1)S(1)} all-to-all(bf16[2,32,3,8,512]{4,3,2,1,0:T(8,128)(2,1)S(1)} %broadcast_in_dim.47), channel_id=1, replica_groups=mesh['seq_0'=8,'seq_1'=4,'seq_2'=2,'head'=8] {'seq_2'}, dimensions={0} | all-to-all | bytes 3145728 | tf_op jit(solution)/shard_map/all_to_all | solution.py:23
  253.9 1.7 fusion.8
  255.6 24.1 %all_to_all.79 = bf16[8,16,512]{2,1,0:T(8,128)(2,1)S(1)} all-to-all(bf16[8,16,512]{2,1,0:T(8,128)(2,1)S(1)} %bitcast.156), channel_id=1, replica_groups=mesh['seq_0'=8,'seq_1'=4,'seq_2'=2,'head'=8] {'head'}, dimensions={0} | all-to-all | bytes 262144 | tf_op jit(solution)/shard_map/all_to_all | solution.py:180
  (72 shorter events, 8.1 us)
Async XLA Ops:
  6.3 12.8 %copy-start = (f32[3,1,8,512]{3,2,1,0:T(8,128)S(1)}, f32[3,1,8,512]{3,2,1,0:T(8,128)}, u32[]{:S(2)}) copy-start(f32[3,1,8,512]{3,2,1,0:T(8,128)} %param.7) | copy-start | bytes 147460
  13.7 29.3 %copy-start.3 = (f32[128,1]{0,1:T(1,128)S(1)}, f32[128,1]{0,1:T(1,128)}, u32[]{:S(2)}) copy-start(f32[128,1]{0,1:T(1,128)} %param.5) | copy-start | bytes 1540
  13.7 13.9 %all-to-all-start = ((bf16[8,2,12288]{2,1,0:T(2,128)(2,1)}), bf16[8,2,12288]{2,1,0:T(2,128)(2,1)S(1)}, u32[]{:S(2)}, u32[]{:S(2)}) async-start(bf16[8,2,12288]{2,1,0:T(2,128)(2,1)} %reshape.152), calls=%async_computation | async-start | bytes 786432 | tf_op jit(solution)/shard_map/all_to_all | solution.py:132
  28.6 35.0 %all-to-all-start.1 = ((bf16[32,3,8,512]{3,2,1,0:T(8,128)(2,1)}), bf16[32,3,8,512]{3,2,1,0:T(8,128)(2,1)S(1)}, u32[]{:S(2)}, u32[]{:S(2)}) async-start(bf16[32,3,8,512]{3,2,1,0:T(8,128)(2,1)} %broadcast_in_dim.42), calls=%async_computation.1 | async-start | bytes 1572864 | tf_op jit(solution)/shard_map/all_to_all | solution.py:23
  111.5 29.6 %all-to-all-start.5 = ((bf16[32,24,512]{2,1,0:T(8,128)(2,1)}), bf16[32,24,512]{2,1,0:T(8,128)(2,1)S(1)}, u32[]{:S(2)}, u32[]{:S(2)}) async-start(bf16[32,24,512]{2,1,0:T(8,128)(2,1)} %broadcast_in_dim.44), calls=%async_computation.5 | async-start | bytes 1572864 | tf_op jit(solution)/shard_map/all_to_all | solution.py:23
  120.9 76.6 %collective-permute-start = (bf16[2,128,512]{2,1,0:T(8,128)(2,1)S(1)}, bf16[2,128,512]{2,1,0:T(8,128)(2,1)S(1)}, u32[]{:S(2)}, u32[]{:S(2)}) collective-permute-start(bf16[2,128,512]{2,1,0:T(8,128)(2,1)S(1)} %bitcast.140), channel_id=1, source_target_pairs={{0,64},{8,72},{16,80},{24,88},{32,96},{40,104},{48,112},{56,120},{... | collective-permute-start | bytes 786440 | tf_op jit(solution)/shard_map/ppermute | solution.py:78
  124.2 77.8 %collective-permute-start.1 = (bf16[2,128,512]{2,1,0:T(8,128)(2,1)S(1)}, bf16[2,128,512]{2,1,0:T(8,128)(2,1)S(1)}, u32[]{:S(2)}, u32[]{:S(2)}) collective-permute-start(bf16[2,128,512]{2,1,0:T(8,128)(2,1)S(1)} %bitcast.141), channel_id=1, source_target_pairs={{0,56},{8,64},{16,72},{24,80},{32,88},{40,96},{48,104},{56,112},{6... | collective-permute-start | bytes 786440 | tf_op jit(solution)/shard_map/ppermute | solution.py:78
  126.2 79.6 %collective-permute-start.2 = (bf16[2,128,512]{2,1,0:T(8,128)(2,1)S(1)}, bf16[2,128,512]{2,1,0:T(8,128)(2,1)S(1)}, u32[]{:S(2)}, u32[]{:S(2)}) collective-permute-start(bf16[2,128,512]{2,1,0:T(8,128)(2,1)S(1)} %bitcast.142), channel_id=1, source_target_pairs={{0,48},{8,56},{16,64},{24,72},{32,80},{40,88},{48,96},{56,104},{64... | collective-permute-start | bytes 786440 | tf_op jit(solution)/shard_map/ppermute | solution.py:78
  170.7 1.6 copy-start.1
  175.9 71.9 %all-to-all-start.7 = ((bf16[32,3,8,512]{3,2,1,0:T(8,128)(2,1)}), bf16[32,3,8,512]{3,2,1,0:T(8,128)(2,1)S(1)}, u32[]{:S(2)}, u32[]{:S(2)}) async-start(bf16[32,3,8,512]{3,2,1,0:T(8,128)(2,1)} %broadcast_in_dim.46), calls=%async_computation.7 | async-start | bytes 1572864 | tf_op jit(solution)/shard_map/all_to_all | solution.py:23
  187.5 26.6 %collective-permute-start.3 = (bf16[2,128,512]{2,1,0:T(8,128)(2,1)S(1)}, bf16[2,128,512]{2,1,0:T(8,128)(2,1)S(1)}, u32[]{:S(2)}, u32[]{:S(2)}) collective-permute-start(bf16[2,128,512]{2,1,0:T(8,128)(2,1)S(1)} %bitcast.143), channel_id=1, source_target_pairs={{0,40},{8,48},{16,56},{24,64},{32,72},{40,80},{48,88},{56,96},{64,... | collective-permute-start | bytes 786440 | tf_op jit(solution)/shard_map/ppermute | solution.py:78
  194.0 41.6 %collective-permute-start.4 = (bf16[2,128,512]{2,1,0:T(8,128)(2,1)S(1)}, bf16[2,128,512]{2,1,0:T(8,128)(2,1)S(1)}, u32[]{:S(2)}, u32[]{:S(2)}) collective-permute-start(bf16[2,128,512]{2,1,0:T(8,128)(2,1)S(1)} %bitcast.144), channel_id=1, source_target_pairs={{0,32},{8,40},{16,48},{24,56},{32,64},{40,72},{48,80},{56,88},{64,... | collective-permute-start | bytes 786440 | tf_op jit(solution)/shard_map/ppermute | solution.py:78
  197.5 38.2 %collective-permute-start.5 = (bf16[2,128,512]{2,1,0:T(8,128)(2,1)S(1)}, bf16[2,128,512]{2,1,0:T(8,128)(2,1)S(1)}, u32[]{:S(2)}, u32[]{:S(2)}) collective-permute-start(bf16[2,128,512]{2,1,0:T(8,128)(2,1)S(1)} %bitcast.145), channel_id=1, source_target_pairs={{0,24},{8,32},{16,40},{24,48},{32,56},{40,64},{48,72},{56,80},{64,... | collective-permute-start | bytes 786440 | tf_op jit(solution)/shard_map/ppermute | solution.py:78
  202.1 44.1 %collective-permute-start.6 = (bf16[2,128,512]{2,1,0:T(8,128)(2,1)S(1)}, bf16[2,128,512]{2,1,0:T(8,128)(2,1)S(1)}, u32[]{:S(2)}, u32[]{:S(2)}) collective-permute-start(bf16[2,128,512]{2,1,0:T(8,128)(2,1)S(1)} %bitcast.146), channel_id=1, source_target_pairs={{0,16},{8,24},{16,32},{24,40},{32,48},{40,56},{48,64},{56,72},{64,... | collective-permute-start | bytes 786440 | tf_op jit(solution)/shard_map/ppermute | solution.py:78
  205.8 40.4 %collective-permute-start.7 = (bf16[2,128,512]{2,1,0:T(8,128)(2,1)S(1)}, bf16[2,128,512]{2,1,0:T(8,128)(2,1)S(1)}, u32[]{:S(2)}, u32[]{:S(2)}) collective-permute-start(bf16[2,128,512]{2,1,0:T(8,128)(2,1)S(1)} %bitcast.147), channel_id=1, source_target_pairs={{0,8},{8,16},{16,24},{24,32},{32,40},{40,48},{48,56},{56,64},{64,7... | collective-permute-start | bytes 786440 | tf_op jit(solution)/shard_map/ppermute | solution.py:78
  246.2 1.4 copy-start.2
where the time goes:
time: 282 us; the launch traced here: 280 us
  blocking collectives  77.6 us (28%)
  starting transfers between devices  72.1 us (26%)
  waiting for transfers between devices  64.2 us (23%)
  matrix products  32.5 us (12%)
  local copies, waits for them, and re-layouts  29.2 us (10%)
  other arithmetic  2.9 us (1%)
    ppermute x8, waiting for transfers between devices, from_behind(): return lax.ppermute(block, axis, route)  37 us
    all_to_all x3, starting transfers between devices, sent_to_all(): return lax.all_to_all(copies, axis, split_axis=0, concat_axis=0, tiled=True)  34.5 us
    all_to_all x1, blocking collectives, sum_by_axis(): lax.all_to_all(nearer.astype(jnp.bfloat16), far, split_axis=0, concat_axi...  33.5 us
    ppermute x8, starting transfers between devices, from_behind(): return lax.ppermute(block, axis, route)  32.1 us
    all_to_all x1, blocking collectives, shards(): lax.all_to_all(combined, 'head', split_axis=0, concat_axis=1, tiled=True)  24.1 us
    unnamed x19, local copies, waits for them, and re-layouts  19.8 us
    dot_general x12, matrix products, gram_times(): return jnp.einsum('mij,mjk->mik', row_block, gram_matrix, precision=precise)  19.3 us
    all_to_all x3, waiting for transfers between devices, sent_to_all(): return lax.all_to_all(copies, axis, split_axis=0, concat_axis=0, tiled=True)  18.8 us
  transfers between devices with their start and end apart: 12, of which 7 were waited for; matrix products, arithmetic and copies ran while one was open for 15% of the time, Pallas kernels for 0%

commit v1 on v0

v1 whole, which is shorter than its diff:
```python
import jax
import jax.numpy as jnp
from jax import lax
from jax.experimental import pallas as pl
from jax.experimental.pallas import tpu as pltpu
from jax.sharding import Mesh
from jax.sharding import PartitionSpec as P

WINDOW = 1024
NS_STEPS = 2
NS_1, NS_2, NS_3 = 3.4445, -4.775, 2.0315
RMS_EPS = 1e-06
NORM_EPS = 1e-07

SEQ = ("z", "y", "core")
SEQ_HEAD = ("z", "y", "core", "head")
CHIPS = ("z", "y")
F32, BF16 = jnp.float32, jnp.bfloat16


def dot_nt(a, b):
    return lax.dot_general(a, b, (((1,), (1,)), ((), ())), preferred_element_type=F32)


def dot_nn(a, b):
    return lax.dot_general(a, b, (((1,), (0,)), ((), ())), preferred_element_type=F32)


def local_call(body, outs, args, smem=(), scratch=()):
    specs = [
        pl.BlockSpec(memory_space=pltpu.SMEM if i in smem else pltpu.VMEM) for i in range(len(args))
    ]
    single = not isinstance(outs, (list, tuple))
    out_list = [outs] if single else list(outs)
    out_specs = [pl.BlockSpec(memory_space=pltpu.VMEM) for _ in out_list]
    return pl.pallas_call(
        body,
        in_specs=specs,
        out_specs=out_specs[0] if single else out_specs,
        out_shape=outs if single else out_list,
        scratch_shapes=list(scratch),
        name=body.__name__,
    )(*args)


def split_heads(qkv_ref, out_ref):
    for h in range(out_ref.shape[0]):
        hd = out_ref.shape[3]
        for j in range(3):
            out_ref[h, j] = qkv_ref[j, :, h * hd : (h + 1) * hd]


def rms_scaled(x):
    return x * lax.rsqrt(jnp.mean(x * x, axis=-1, keepdims=True) + RMS_EPS)


def prepare(arr_ref, rate_ref, q_ref, kv_ref, qn_ref, ks_ref):
    n, _, t, _ = arr_ref.shape
    for j in range(n):
        rows = slice(j * t, (j + 1) * t)
        q, k, v = arr_ref[j, 0], arr_ref[j, 1], arr_ref[j, 2]
        q_ref[rows] = q
        kv_ref[0, rows] = k
        kv_ref[1, rows] = v
        qn_ref[rows] = rms_scaled(q.astype(F32)).astype(BF16)
        ks_ref[0, rows] = rms_scaled(k.astype(F32)).astype(BF16)
        ks_ref[1, rows] = (-rate_ref[rows] * v.astype(F32)).astype(BF16)


def copies_of(rows_ref, out_ref):
    rows = rows_ref[...].astype(BF16)
    for d in range(out_ref.shape[0]):
        out_ref[d] = rows


def merged_rows(ref, m):
    n, _, r, w = ref.shape
    return ref[:, m].astype(F32).reshape(n * r, w)


def gradient(own_ref, other_ref, w_ref, out_ref):
    n, _, r, w = w_ref.shape
    key_norm = jnp.concatenate([own_ref[0], other_ref[0]], axis=0)
    signal = jnp.concatenate([own_ref[1], other_ref[1]], axis=0)
    gate = dot_nt(merged_rows(w_ref, 0).astype(BF16), key_norm)
    up = dot_nt(merged_rows(w_ref, 1).astype(BF16), key_norm)
    back = dot_nt(merged_rows(w_ref, 2).astype(BF16), signal)
    s = jax.nn.sigmoid(gate)
    silu = gate * s
    grads = (
        ((back * up * s * (1.0 + gate * (1.0 - s))).astype(BF16), key_norm),
        ((back * silu).astype(BF16), key_norm),
        ((silu * up).astype(BF16), signal),
    )
    for m, (left, right) in enumerate(grads):
        out_ref[:, m] = dot_nn(left, right).reshape(n, r, w).astype(BF16)


def sum_and_copy(arr_ref, out_ref):
    total = arr_ref[0].astype(F32)
    for d in range(1, arr_ref.shape[0]):
        total = total + arr_ref[d].astype(F32)
    total = total.astype(BF16)
    for d in range(out_ref.shape[0]):
        out_ref[d] = total


def attend(where_ref, q_ref, own_ref, other_ref, out_ref):
    blocks, _, t, w = own_ref.shape
    chip, core = where_ref[0], where_ref[1]
    q = q_ref[...]
    q_pos = (2 * chip + core) * t + lax.broadcasted_iota(jnp.int32, (t, t), 0)
    lane = lax.broadcasted_iota(jnp.int32, (t, t), 1)
    parts = []
    for b in range(blocks):
        for ref, c in ((own_ref, core), (other_ref, 1 - core)):
            k_pos = (2 * (chip - b) + c) * t + lane
            seen = (k_pos <= q_pos) & (k_pos > q_pos - WINDOW) & (k_pos >= 0)
            scores = dot_nt(q, ref[b, 0]) * (w ** (-0.5))
            parts.append(jnp.where(seen, scores, -jnp.inf))
    top = parts[0]
    for p in parts[1:]:
        top = jnp.maximum(top, p)
    top = jnp.max(top, axis=1, keepdims=True)
    parts = [jnp.exp(p - top) for p in parts]
    total = parts[0]
    for p in parts[1:]:
        total = total + p
    inverse = 1.0 / jnp.sum(total, axis=1, keepdims=True)
    out = jnp.zeros((t, w), F32)
    for b in range(blocks):
        for i, ref in enumerate((own_ref, other_ref)):
            out = out + dot_nn((parts[2 * b + i] * inverse).astype(BF16), ref[b, 1])
    out_ref[...] = out


def finish(
    where_ref, rate_ref, g_own, g_other, old_own, old_other, state_ref, qn_ref, att_ref,
    rows_ref, out_ref, x_ref, fresh_ref,
):
    n, _, r, _ = g_own.shape
    half = n * r
    rate = rate_ref[0]
    chip = where_ref[0]

    def one_matrix(m, carry):
        g = jnp.concatenate([merged_rows(g_own, m), merged_rows(g_other, m)], axis=0)
        norm = jnp.sqrt(jnp.sum(g * g, keepdims=True))
        x = g / (norm + NORM_EPS)
        for _ in range(NS_STEPS):
            low = x.astype(BF16)
            gram = dot_nt(low, low)
            gram_low = gram.astype(BF16)
            poly = NS_2 * gram + NS_3 * dot_nn(gram_low, gram_low)
            x = NS_1 * x + dot_nn(poly.astype(BF16), low)
        x_ref[...] = x
        fresh_ref[m, :half] = (merged_rows(old_own, m) - rate * x[:half]).astype(BF16)
        fresh_ref[m, half:] = (merged_rows(old_other, m) - rate * x[half:]).astype(BF16)
        rows_ref[m] = state_ref[m] - rate * x_ref[pl.ds(pl.multiple_of(chip * r, r), r)]
        return carry

    lax.fori_loop(0, 3, one_matrix, 0)
    gate = dot_nt(qn_ref[...], fresh_ref[0])
    up = dot_nt(qn_ref[...], fresh_ref[1])
    active = (jax.nn.silu(gate) * up).astype(BF16)
    out_ref[...] = (att_ref[...] + dot_nn(active, fresh_ref[2])).astype(BF16)


def join_heads(arr_ref, out_ref):
    for h in range(arr_ref.shape[0]):
        hd = arr_ref.shape[2]
        out_ref[:, h * hd : (h + 1) * hd] = arr_ref[h]


def shards(qkv, token_rate, head_rate, fast_state):
    heads = lax.axis_size("head")
    chips = lax.axis_size("z") * lax.axis_size("y")
    _, tok_part, width = qkv.shape
    hd = width // heads
    tok = tok_part * heads
    rows = fast_state.shape[2]
    chip = lax.axis_index(CHIPS)
    core = lax.axis_index("core")
    where = jnp.stack([chip, core]).astype(jnp.int32)
    state = fast_state[:, 0]
    swap = [(0, 1), (1, 0)]

    def shape(dims, dtype=BF16):
        return jax.ShapeDtypeStruct(dims, dtype)

    def exchanged(pieces, axis):
        return lax.all_to_all(pieces, axis, 0, 0, tiled=True)

    old_copies = local_call(copies_of, shape((chips, 3, rows, hd)), (state,))
    split = local_call(split_heads, shape((heads, 3, tok_part, hd)), (qkv,))
    arrived = exchanged(split, "head")
    old_own = exchanged(old_copies, CHIPS)
    q, kv, q_norm, ks = local_call(
        prepare,
        [shape((tok, hd)), shape((2, tok, hd)), shape((tok, hd)), shape((2, tok, hd))],
        (arrived, token_rate),
    )
    ks_other = lax.ppermute(ks, "core", swap)
    before = WINDOW // (2 * tok)
    own_blocks = [kv] + [
        lax.ppermute(kv, CHIPS, [(i - d, i) for i in range(d, chips)]) for d in range(1, before + 1)
    ]
    own_kv = jnp.stack(own_blocks)
    partial = local_call(gradient, shape((chips, 3, rows, hd)), (ks, ks_other, old_own))
    parts = exchanged(partial, CHIPS)
    g_copies = local_call(sum_and_copy, shape((chips, 3, rows, hd)), (parts,))
    g_own = exchanged(g_copies, CHIPS)
    other_kv = lax.ppermute(own_kv, "core", swap)
    attention = local_call(attend, shape((tok, hd), F32), (where, q, own_kv, other_kv), smem=(0,))
    old_other = lax.ppermute(old_own, "core", swap)
    g_other = lax.ppermute(g_own, "core", swap)
    new_rows, combined = local_call(
        finish,
        [shape((3, rows, hd), F32), shape((tok, hd))],
        (where, head_rate, g_own, g_other, old_own, old_other, state, q_norm, attention),
        smem=(0, 1),
        scratch=[
            pltpu.VMEM((2 * chips * rows, hd), F32),
            pltpu.VMEM((3, 2 * chips * rows, hd), BF16),
        ],
    )
    back = exchanged(combined.reshape(heads, tok_part, hd), "head")
    return (
        local_call(join_heads, shape((tok_part, width)), (back,)),
        new_rows[:, None],
    )


def solution(mesh):
    finer = Mesh(mesh.devices.reshape(8, 4, 2, mesh.shape["head"]), SEQ_HEAD)
    return jax.shard_map(
        shards,
        mesh=finer,
        in_specs=(P(None, SEQ_HEAD, None), P(SEQ, "head"), P("head"), P(None, "head", SEQ, None)),
        out_specs=(P(SEQ_HEAD, None), P(None, "head", SEQ, None)),
        check_vma=False,
    )
```

time: 282 us -> 187 us (0.66)
  the two profiles are of different devices: /device:TPU:64 before, /device:TPU:104 now
where the time goes in v1:
time: 187 us; the launch traced here: 186 us
  waiting for transfers between devices  66 us (35%)
  starting transfers between devices  65.2 us (35%)
  Pallas kernels  26.7 us (14%)
  blocking collectives  22.6 us (12%)
  local copies, waits for them, and re-layouts  3.57 us (2%)
    all_to_all x4, waiting for transfers between devices, exchanged(): return lax.all_to_all(pieces, axis, 0, 0, tiled=True)  43.4 us
    all_to_all x4, starting transfers between devices, exchanged(): return lax.all_to_all(pieces, axis, 0, 0, tiled=True)  42.5 us
    pallas_call x8, Pallas kernels, local_call(): pl.pallas_call(body, in_specs=specs, out_specs=out_specs[0] if single els...  26.7 us
    all_to_all x1, blocking collectives, exchanged(): return lax.all_to_all(pieces, axis, 0, 0, tiled=True)  22.6 us
    ppermute x4, waiting for transfers between devices, shards(): lax.ppermute(kv, CHIPS, [(i - d, i) for i in range(d, chips)])  21 us
    ppermute x4, starting transfers between devices, shards(): lax.ppermute(kv, CHIPS, [(i - d, i) for i in range(d, chips)])  14.5 us
  transfers between devices with their start and end apart: 12, of which 6 were waited for; matrix products, arithmetic and copies ran while one was open for 1% of the time, Pallas kernels for 5%

profile of v1, /device:TPU:104, one launch (start us, length us, event | category | flops | bytes accessed | tf_op | source)
XLA Modules:
  0.0 186.2 jit_solution(6633263925868242419)
XLA Ops:
  0.6 1.8 split_heads.1
  2.4 5.8 %all-to-all-start = ((bf16[8,3,16,512]{3,2,1,0:T(8,128)(2,1)}), bf16[8,3,16,512]{3,2,1,0:T(8,128)(2,1)S(1)}, u32[]{:S(2)}, u32[]{:S(2)}) async-start(bf16[8,3,16,512]{3,2,1,0:T(8,128)(2,1)} %split_heads.1), calls=%async_computation | async-start | bytes 786432 | tf_op jit(solution)/shard_map/all_to_all | solution.py:192
  8.2 1.8 copies_of.1
  9.9 5.5 %all-to-all-done.arr_ref = bf16[8,3,16,512]{3,2,1,0:T(8,128)(2,1)S(1)} async-done(((bf16[8,3,16,512]{3,2,1,0:T(8,128)(2,1)}), bf16[8,3,16,512]{3,2,1,0:T(8,128)(2,1)S(1)}, u32[]{:S(2)}, u32[]{:S(2)}) %all-to-all-start) | async-done | bytes 393248 | tf_op jit(solution)/shard_map/all_to_all | solution.py:192
  15.4 14.9 %all-to-all-start.1 = ((bf16[32,3,8,512]{3,2,1,0:T(8,128)(2,1)}), bf16[32,3,8,512]{3,2,1,0:T(8,128)(2,1)S(1)}, u32[]{:S(2)}, u32[]{:S(2)}) async-start(bf16[32,3,8,512]{3,2,1,0:T(8,128)(2,1)} %copies_of.1), calls=%async_computation.1 | async-start | bytes 1572864 | tf_op jit(solution)/shard_map/all_to_all | solution.py:192
  30.3 0.0 copy-done.8
  30.3 0.7 copy.6.rate_ref
  31.1 0.0 copy-done.5
  31.1 1.9 %prepare.1 = (bf16[128,512]{1,0:T(8,128)(2,1)}, bf16[2,128,512]{2,1,0:T(8,128)(2,1)}, bf16[128,512]{1,0:T(8,128)(2,1)}, bf16[2,128,512]{2,1,0:T(8,128)(2,1)}) custom-call(bf16[8,3,16,512]{3,2,1,0:T(8,128)(2,1)} %copy-done.5, f32[128,1]{1,0:T(8,128)} %copy.6.rate_ref), custom_call_target="tpu_custom_call" | custom-call | tf_op jit(solution)/shard_map/prepare/pallas_call | solution.py:36
  33.0 1.9 %collective-permute-start = (bf16[2,128,512]{2,1,0:T(8,128)(2,1)}, bf16[2,128,512]{2,1,0:T(8,128)(2,1)S(1)}, u32[]{:S(2)}, u32[]{:S(2)}) collective-permute-start(bf16[2,128,512]{2,1,0:T(8,128)(2,1)} %get-tuple-element.8.own_ref), channel_id=1, source_target_pairs={{0,8},{8,0},{1,9},{9,1},{2,10},{10,2},{3,11},{11,3},{4,12},{12,4},... | collective-permute-start | bytes 786440 | tf_op jit(solution)/shard_map/ppermute | solution.py:203
  34.9 1.7 collective-permute-done.other_ref
  36.6 15.0 %all-to-all-done.1.w_ref.old_own = bf16[32,3,8,512]{3,2,1,0:T(8,128)(2,1)S(1)} async-done(((bf16[32,3,8,512]{3,2,1,0:T(8,128)(2,1)}), bf16[32,3,8,512]{3,2,1,0:T(8,128)(2,1)S(1)}, u32[]{:S(2)}, u32[]{:S(2)}) %all-to-all-start.1) | async-done | bytes 786464 | tf_op jit(solution)/shard_map/all_to_all | solution.py:192
  51.7 0.0 copy-done.7
  51.7 0.9 copy-done
  52.6 3.0 %gradient.1 = bf16[32,3,8,512]{3,2,1,0:T(8,128)(2,1)} custom-call(bf16[2,128,512]{2,1,0:T(8,128)(2,1)} %get-tuple-element.8.own_ref, bf16[2,128,512]{2,1,0:T(8,128)(2,1)} %copy-done.7, bf16[32,3,8,512]{3,2,1,0:T(8,128)(2,1)} %copy-done), custom_call_target="tpu_custom_call" | custom-call | tf_op jit(solution)/shard_map/gradient/pallas_call | solution.py:36
  55.6 9.1 %all-to-all-start.2 = ((bf16[32,3,8,512]{3,2,1,0:T(8,128)(2,1)}), bf16[32,3,8,512]{3,2,1,0:T(8,128)(2,1)S(1)}, u32[]{:S(2)}, u32[]{:S(2)}) async-start(bf16[32,3,8,512]{3,2,1,0:T(8,128)(2,1)} %gradient.1), calls=%async_computation.2 | async-start | bytes 1572864 | tf_op jit(solution)/shard_map/all_to_all | solution.py:192
  64.7 0.0 copy-done.6
  64.7 2.5 %collective-permute-start.3 = (bf16[2,128,512]{2,1,0:T(8,128)(2,1)S(1)}, bf16[2,128,512]{2,1,0:T(8,128)(2,1)}, u32[]{:S(2)}, u32[]{:S(2)}) collective-permute-start(bf16[2,128,512]{2,1,0:T(8,128)(2,1)S(1)} %copy-done.6), channel_id=1, source_target_pairs={{0,16},{16,32},{32,48},{48,64},{64,80},{80,96},{96,112},{112,128},... | collective-permute-start | bytes 786440 | tf_op jit(solution)/shard_map/ppermute | solution.py:206
  67.2 5.2 %collective-permute-start.4 = (bf16[2,128,512]{2,1,0:T(8,128)(2,1)S(1)}, bf16[2,128,512]{2,1,0:T(8,128)(2,1)S(1)}, u32[]{:S(2)}, u32[]{:S(2)}) collective-permute-start(bf16[2,128,512]{2,1,0:T(8,128)(2,1)S(1)} %copy-done.6), channel_id=1, source_target_pairs={{0,32},{16,48},{32,64},{48,80},{64,96},{80,112},{96,128},{112,144}... | collective-permute-start | bytes 786440 | tf_op jit(solution)/shard_map/ppermute | solution.py:206
  72.3 22.9 %all-to-all-done.2.arr_ref = bf16[32,3,8,512]{3,2,1,0:T(8,128)(2,1)S(1)} async-done(((bf16[32,3,8,512]{3,2,1,0:T(8,128)(2,1)}), bf16[32,3,8,512]{3,2,1,0:T(8,128)(2,1)S(1)}, u32[]{:S(2)}, u32[]{:S(2)}) %all-to-all-start.2) | async-done | bytes 786464 | tf_op jit(solution)/shard_map/all_to_all | solution.py:192
  95.2 0.9 copy-done.2
  96.1 2.1 %sum_and_copy.1 = bf16[32,3,8,512]{3,2,1,0:T(8,128)(2,1)} custom-call(bf16[32,3,8,512]{3,2,1,0:T(8,128)(2,1)} %copy-done.2), custom_call_target="tpu_custom_call" | custom-call | tf_op jit(solution)/shard_map/sum_and_copy/pallas_call | solution.py:36
  98.2 12.7 %all-to-all-start.3 = ((bf16[32,3,8,512]{3,2,1,0:T(8,128)(2,1)}), bf16[32,3,8,512]{3,2,1,0:T(8,128)(2,1)S(1)}, u32[]{:S(2)}, u32[]{:S(2)}) async-start(bf16[32,3,8,512]{3,2,1,0:T(8,128)(2,1)} %sum_and_copy.1), calls=%async_computation.3 | async-start | bytes 1572864 | tf_op jit(solution)/shard_map/all_to_all | solution.py:192
  110.9 0.0 copy-start.1
  110.9 3.5 %collective-permute-start.5 = (bf16[2,128,512]{2,1,0:T(8,128)(2,1)S(1)}, bf16[2,128,512]{2,1,0:T(8,128)(2,1)S(1)}, u32[]{:S(2)}, u32[]{:S(2)}) collective-permute-start(bf16[2,128,512]{2,1,0:T(8,128)(2,1)S(1)} %copy-done.6), channel_id=1, source_target_pairs={{0,48},{16,64},{32,80},{48,96},{64,112},{80,128},{96,144},{112,160... | collective-permute-start | bytes 786440 | tf_op jit(solution)/shard_map/ppermute | solution.py:206
  114.5 3.4 %collective-permute-start.6 = (bf16[2,128,512]{2,1,0:T(8,128)(2,1)S(1)}, bf16[2,128,512]{2,1,0:T(8,128)(2,1)S(1)}, u32[]{:S(2)}, u32[]{:S(2)}) collective-permute-start(bf16[2,128,512]{2,1,0:T(8,128)(2,1)S(1)} %copy-done.6), channel_id=1, source_target_pairs={{0,64},{16,80},{32,96},{48,112},{64,128},{80,144},{96,160},{112,17... | collective-permute-start | bytes 786440 | tf_op jit(solution)/shard_map/ppermute | solution.py:206
  117.8 0.0 collective-permute-done.3
  117.8 1.0 bitcast_dynamic-update-slice_fusion.3
  118.8 0.0 collective-permute-done.4
  118.9 15.9 %collective-permute-done.5 = bf16[2,128,512]{2,1,0:T(8,128)(2,1)S(1)} collective-permute-done((bf16[2,128,512]{2,1,0:T(8,128)(2,1)S(1)}, bf16[2,128,512]{2,1,0:T(8,128)(2,1)S(1)}, u32[]{:S(2)}, u32[]{:S(2)}) %collective-permute-start.5) | collective-permute-done | bytes 262176 | tf_op jit(solution)/shard_map/ppermute | solution.py:206
  134.8 5.1 %collective-permute-done.6 = bf16[2,128,512]{2,1,0:T(8,128)(2,1)S(1)} collective-permute-done((bf16[2,128,512]{2,1,0:T(8,128)(2,1)S(1)}, bf16[2,128,512]{2,1,0:T(8,128)(2,1)S(1)}, u32[]{:S(2)}, u32[]{:S(2)}) %collective-permute-start.6) | collective-permute-done | bytes 262176 | tf_op jit(solution)/shard_map/ppermute | solution.py:206
  139.9 0.0 copy-start.4
  139.9 2.0 %collective-permute-start.7 = (bf16[5,2,128,512]{3,2,1,0:T(8,128)(2,1)S(1)}, bf16[5,2,128,512]{3,2,1,0:T(8,128)(2,1)}, u32[]{:S(2)}, u32[]{:S(2)}) collective-permute-start(bf16[5,2,128,512]{3,2,1,0:T(8,128)(2,1)S(1)} %bitcast_dynamic-update-slice_fusion.own_ref), channel_id=1, source_target_pairs={{0,8},{8,0},{1,9},{9,1},{2,10},{10,2},{3,11},{11,3},{4,12},{12,4},... | collective-permute-start | bytes 3932168 | tf_op jit(solution)/shard_map/ppermute | solution.py:213
  141.9 0.0 copy-done.1
  141.9 2.3 %collective-permute-start.2 = (bf16[32,3,8,512]{3,2,1,0:T(8,128)(2,1)S(1)}, bf16[32,3,8,512]{3,2,1,0:T(8,128)(2,1)}, u32[]{:S(2)}, u32[]{:S(2)}) collective-permute-start(bf16[32,3,8,512]{3,2,1,0:T(8,128)(2,1)S(1)} %copy-done.1), channel_id=1, source_target_pairs={{0,8},{8,0},{1,9},{9,1},{2,10},{10,2},{3,11},{11,3},{4,12},{12,4},... | collective-permute-start | bytes 2359304 | tf_op jit(solution)/shard_map/ppermute | solution.py:215
  144.2 0.0 all-to-all-done.3.g_own
  144.2 0.0 copy-start.3
  144.2 2.0 %collective-permute-start.1 = (bf16[32,3,8,512]{3,2,1,0:T(8,128)(2,1)S(1)}, bf16[32,3,8,512]{3,2,1,0:T(8,128)(2,1)}, u32[]{:S(2)}, u32[]{:S(2)}) collective-permute-start(bf16[32,3,8,512]{3,2,1,0:T(8,128)(2,1)S(1)} %all-to-all-done.3.g_own), channel_id=1, source_target_pairs={{0,8},{8,0},{1,9},{9,1},{2,10},{10,2},{3,11},{11,3},{4,12},{12,4},... | collective-permute-start | bytes 2359304 | tf_op jit(solution)/shard_map/ppermute | solution.py:216
  146.9 0.6 pad_add_fusion.where_ref
  147.5 0.0 collective-permute-done.7.other_ref
  147.5 0.0 copy-done.4
  147.5 3.7 %attend.1.att_ref = f32[128,512]{1,0:T(8,128)} custom-call(s32[2]{0:T(128)} %pad_add_fusion.where_ref, bf16[128,512]{1,0:T(8,128)(2,1)} %get-tuple-element.10.q_ref, bf16[5,2,128,512]{3,2,1,0:T(8,128)(2,1)} %copy-done.4, bf16[5,2,128,512]{3,2,1,0:T(8,128)(2,1)} %collective-permute-done.7.other_ref), custom_call_target="tpu_custom_call" | custom-call | tf_op jit(solution)/shard_map/attend/pallas_call | solution.py:36
  151.2 0.0 copy-done.3
  151.2 0.0 collective-permute-done.2.old_other
  151.2 0.0 collective-permute-done.1.g_other
  151.2 10.8 %finish.1 = (f32[3,8,512]{2,1,0:T(8,128)}, bf16[128,512]{1,0:T(8,128)(2,1)}) custom-call(s32[2]{0:T(128)} %pad_add_fusion.where_ref, f32[1]{0:T(128)S(6)} %copy.12.rate_ref, bf16[32,3,8,512]{3,2,1,0:T(8,128)(2,1)} %copy-done.3, bf16[32,3,8,512]{3,2,1,0:T(8,128)(2,1)} %collective-permute-done.1.g_other, bf16[32,3,8,512]{3,2,1,0:T(8,128)(2,1)} %copy-done, ...), custom_call_target="tpu_custom_call" | custom-call | tf_op jit(solution)/shard_map/finish/pallas_call | solution.py:36
  162.0 22.6 %all_to_all.25.arr_ref = bf16[8,16,512]{2,1,0:T(8,128)(2,1)} all-to-all(bf16[8,16,512]{2,1,0:T(8,128)(2,1)} %bitcast.19), channel_id=1, replica_groups=mesh['z'=8,'y'=4,'core'=2,'head'=8] {'head'}, dimensions={0} | all-to-all | bytes 262144 | tf_op jit(solution)/shard_map/all_to_all | solution.py:192
  184.6 1.6 join_heads.1
  (10 shorter events, 0.1 us)
Async XLA Ops:
  2.4 13.0 %all-to-all-start = ((bf16[8,3,16,512]{3,2,1,0:T(8,128)(2,1)}), bf16[8,3,16,512]{3,2,1,0:T(8,128)(2,1)S(1)}, u32[]{:S(2)}, u32[]{:S(2)}) async-start(bf16[8,3,16,512]{3,2,1,0:T(8,128)(2,1)} %split_heads.1), calls=%async_computation | async-start | bytes 786432 | tf_op jit(solution)/shard_map/all_to_all | solution.py:192
  8.2 22.2 %copy-start.8 = (f32[128,1]{0,1:T(1,128)S(1)}, f32[128,1]{0,1:T(1,128)}, u32[]{:S(2)}) copy-start(f32[128,1]{0,1:T(1,128)} %param.5) | copy-start | bytes 1540
  15.4 15.7 %copy-start.5 = (bf16[8,3,16,512]{3,2,1,0:T(8,128)(2,1)}, bf16[8,3,16,512]{3,2,1,0:T(8,128)(2,1)S(1)}, u32[]{:S(2)}) copy-start(bf16[8,3,16,512]{3,2,1,0:T(8,128)(2,1)S(1)} %all-to-all-done.arr_ref) | copy-start | bytes 1179652
  15.4 36.3 %all-to-all-start.1 = ((bf16[32,3,8,512]{3,2,1,0:T(8,128)(2,1)}), bf16[32,3,8,512]{3,2,1,0:T(8,128)(2,1)S(1)}, u32[]{:S(2)}, u32[]{:S(2)}) async-start(bf16[32,3,8,512]{3,2,1,0:T(8,128)(2,1)} %copies_of.1), calls=%async_computation.1 | async-start | bytes 1572864 | tf_op jit(solution)/shard_map/all_to_all | solution.py:192
  33.0 3.6 %collective-permute-start = (bf16[2,128,512]{2,1,0:T(8,128)(2,1)}, bf16[2,128,512]{2,1,0:T(8,128)(2,1)S(1)}, u32[]{:S(2)}, u32[]{:S(2)}) collective-permute-start(bf16[2,128,512]{2,1,0:T(8,128)(2,1)} %get-tuple-element.8.own_ref), channel_id=1, source_target_pairs={{0,8},{8,0},{1,9},{9,1},{2,10},{10,2},{3,11},{11,3},{4,12},{12,4},... | collective-permute-start | bytes 786440 | tf_op jit(solution)/shard_map/ppermute | solution.py:203
  36.6 15.0 %copy-start.7 = (bf16[2,128,512]{2,1,0:T(8,128)(2,1)}, bf16[2,128,512]{2,1,0:T(8,128)(2,1)S(1)}, u32[]{:S(2)}) copy-start(bf16[2,128,512]{2,1,0:T(8,128)(2,1)S(1)} %collective-permute-done.other_ref) | copy-start | bytes 786436
  51.7 0.9 copy-start
  55.6 9.1 %copy-start.6 = (bf16[2,128,512]{2,1,0:T(8,128)(2,1)S(1)}, bf16[2,128,512]{2,1,0:T(8,128)(2,1)}, u32[]{:S(2)}) copy-start(bf16[2,128,512]{2,1,0:T(8,128)(2,1)} %get-tuple-element.11) | copy-start | bytes 786436
  55.6 39.6 %all-to-all-start.2 = ((bf16[32,3,8,512]{3,2,1,0:T(8,128)(2,1)}), bf16[32,3,8,512]{3,2,1,0:T(8,128)(2,1)S(1)}, u32[]{:S(2)}, u32[]{:S(2)}) async-start(bf16[32,3,8,512]{3,2,1,0:T(8,128)(2,1)} %gradient.1), calls=%async_computation.2 | async-start | bytes 1572864 | tf_op jit(solution)/shard_map/all_to_all | solution.py:192
  64.7 53.2 %collective-permute-start.3 = (bf16[2,128,512]{2,1,0:T(8,128)(2,1)S(1)}, bf16[2,128,512]{2,1,0:T(8,128)(2,1)}, u32[]{:S(2)}, u32[]{:S(2)}) collective-permute-start(bf16[2,128,512]{2,1,0:T(8,128)(2,1)S(1)} %copy-done.6), channel_id=1, source_target_pairs={{0,16},{16,32},{32,48},{48,64},{64,80},{80,96},{96,112},{112,128},... | collective-permute-start | bytes 786440 | tf_op jit(solution)/shard_map/ppermute | solution.py:206
  67.2 51.7 %collective-permute-start.4 = (bf16[2,128,512]{2,1,0:T(8,128)(2,1)S(1)}, bf16[2,128,512]{2,1,0:T(8,128)(2,1)S(1)}, u32[]{:S(2)}, u32[]{:S(2)}) collective-permute-start(bf16[2,128,512]{2,1,0:T(8,128)(2,1)S(1)} %copy-done.6), channel_id=1, source_target_pairs={{0,32},{16,48},{32,64},{48,80},{64,96},{80,112},{96,128},{112,144}... | collective-permute-start | bytes 786440 | tf_op jit(solution)/shard_map/ppermute | solution.py:206
  95.2 0.9 copy-start.2
  98.2 46.0 %all-to-all-start.3 = ((bf16[32,3,8,512]{3,2,1,0:T(8,128)(2,1)}), bf16[32,3,8,512]{3,2,1,0:T(8,128)(2,1)S(1)}, u32[]{:S(2)}, u32[]{:S(2)}) async-start(bf16[32,3,8,512]{3,2,1,0:T(8,128)(2,1)} %sum_and_copy.1), calls=%async_computation.3 | async-start | bytes 1572864 | tf_op jit(solution)/shard_map/all_to_all | solution.py:192
  110.9 31.0 %copy-start.1 = (bf16[32,3,8,512]{3,2,1,0:T(8,128)(2,1)S(1)}, bf16[32,3,8,512]{3,2,1,0:T(8,128)(2,1)}, u32[]{:S(2)}) copy-start(bf16[32,3,8,512]{3,2,1,0:T(8,128)(2,1)} %copy-done) | copy-start | bytes 2359300
  110.9 23.8 %collective-permute-start.5 = (bf16[2,128,512]{2,1,0:T(8,128)(2,1)S(1)}, bf16[2,128,512]{2,1,0:T(8,128)(2,1)S(1)}, u32[]{:S(2)}, u32[]{:S(2)}) collective-permute-start(bf16[2,128,512]{2,1,0:T(8,128)(2,1)S(1)} %copy-done.6), channel_id=1, source_target_pairs={{0,48},{16,64},{32,80},{48,96},{64,112},{80,128},{96,144},{112,160... | collective-permute-start | bytes 786440 | tf_op jit(solution)/shard_map/ppermute | solution.py:206
  114.5 25.4 %collective-permute-start.6 = (bf16[2,128,512]{2,1,0:T(8,128)(2,1)S(1)}, bf16[2,128,512]{2,1,0:T(8,128)(2,1)S(1)}, u32[]{:S(2)}, u32[]{:S(2)}) collective-permute-start(bf16[2,128,512]{2,1,0:T(8,128)(2,1)S(1)} %copy-done.6), channel_id=1, source_target_pairs={{0,64},{16,80},{32,96},{48,112},{64,128},{80,144},{96,160},{112,17... | collective-permute-start | bytes 786440 | tf_op jit(solution)/shard_map/ppermute | solution.py:206
  139.9 7.7 %copy-start.4 = (bf16[5,2,128,512]{3,2,1,0:T(8,128)(2,1)}, bf16[5,2,128,512]{3,2,1,0:T(8,128)(2,1)S(1)}, u32[]{:S(2)}) copy-start(bf16[5,2,128,512]{3,2,1,0:T(8,128)(2,1)S(1)} %bitcast_dynamic-update-slice_fusion.own_ref) | copy-start | bytes 3932164
  139.9 7.7 %collective-permute-start.7 = (bf16[5,2,128,512]{3,2,1,0:T(8,128)(2,1)S(1)}, bf16[5,2,128,512]{3,2,1,0:T(8,128)(2,1)}, u32[]{:S(2)}, u32[]{:S(2)}) collective-permute-start(bf16[5,2,128,512]{3,2,1,0:T(8,128)(2,1)S(1)} %bitcast_dynamic-update-slice_fusion.own_ref), channel_id=1, source_target_pairs={{0,8},{8,0},{1,9},{9,1},{2,10},{10,2},{3,11},{11,3},{4,12},{12,4},... | collective-permute-start | bytes 3932168 | tf_op jit(solution)/shard_map/ppermute | solution.py:213
  141.9 9.3 %collective-permute-start.2 = (bf16[32,3,8,512]{3,2,1,0:T(8,128)(2,1)S(1)}, bf16[32,3,8,512]{3,2,1,0:T(8,128)(2,1)}, u32[]{:S(2)}, u32[]{:S(2)}) collective-permute-start(bf16[32,3,8,512]{3,2,1,0:T(8,128)(2,1)S(1)} %copy-done.1), channel_id=1, source_target_pairs={{0,8},{8,0},{1,9},{9,1},{2,10},{10,2},{3,11},{11,3},{4,12},{12,4},... | collective-permute-start | bytes 2359304 | tf_op jit(solution)/shard_map/ppermute | solution.py:215
  144.2 7.0 %copy-start.3 = (bf16[32,3,8,512]{3,2,1,0:T(8,128)(2,1)}, bf16[32,3,8,512]{3,2,1,0:T(8,128)(2,1)S(1)}, u32[]{:S(2)}) copy-start(bf16[32,3,8,512]{3,2,1,0:T(8,128)(2,1)S(1)} %all-to-all-done.3.g_own) | copy-start | bytes 2359300
  144.2 7.0 %collective-permute-start.1 = (bf16[32,3,8,512]{3,2,1,0:T(8,128)(2,1)S(1)}, bf16[32,3,8,512]{3,2,1,0:T(8,128)(2,1)}, u32[]{:S(2)}, u32[]{:S(2)}) collective-permute-start(bf16[32,3,8,512]{3,2,1,0:T(8,128)(2,1)S(1)} %all-to-all-done.3.g_own), channel_id=1, source_target_pairs={{0,8},{8,0},{1,9},{9,1},{2,10},{10,2},{3,11},{11,3},{4,12},{12,4},... | collective-permute-start | bytes 2359304 | tf_op jit(solution)/shard_map/ppermute | solution.py:216

commit v2 on v1

--- a/solution.py
+++ b/solution.py
@@ -16,6 +16,7 @@
 SEQ_HEAD = ("z", "y", "core", "head")
 CHIPS = ("z", "y")
 F32, BF16 = jnp.float32, jnp.bfloat16
+KERNEL_VMEM = 20 * 1024 * 1024
 
 
 def dot_nt(a, b):
@@ -26,39 +27,48 @@
     return lax.dot_general(a, b, (((1,), (0,)), ((), ())), preferred_element_type=F32)
 
 
-def local_call(body, outs, args, smem=(), scratch=()):
+def local_call(body, outs, args, smem=(), scratch=(), hbm_in=(), hbm_out=()):
     specs = [
         pl.BlockSpec(memory_space=pltpu.SMEM if i in smem else pltpu.VMEM) for i in range(len(args))
     ]
     single = not isinstance(outs, (list, tuple))
     out_list = [outs] if single else list(outs)
+    out_list = [
+        o if i in hbm_out else pltpu.VMEM(o.shape, o.dtype) for i, o in enumerate(out_list)
+    ]
+    args = [
+        a if i in smem or i in hbm_in else pltpu.with_memory_space_constraint(a, pltpu.VMEM)
+        for i, a in enumerate(args)
+    ]
     out_specs = [pl.BlockSpec(memory_space=pltpu.VMEM) for _ in out_list]
     return pl.pallas_call(
         body,
         in_specs=specs,
         out_specs=out_specs[0] if single else out_specs,
-        out_shape=outs if single else out_list,
+        out_shape=out_list[0] if single else out_list,
         scratch_shapes=list(scratch),
-        name=body.__name__,
+        compiler_params=pltpu.CompilerParams(vmem_limit_bytes=KERNEL_VMEM),
     )(*args)
 
 
-def split_heads(qkv_ref, out_ref):
-    for h in range(out_ref.shape[0]):
-        hd = out_ref.shape[3]
+def split_heads(where_ref, qkv_ref, *out_refs):
+    hd = out_refs[0].shape[2]
+    for d, out_ref in enumerate(out_refs):
+        start = pl.multiple_of((where_ref[2] ^ d) * hd, hd)
         for j in range(3):
-            out_ref[h, j] = qkv_ref[j, :, h * hd : (h + 1) * hd]
+            out_ref[j] = qkv_ref[j, :, pl.ds(start, hd)]
 
 
 def rms_scaled(x):
     return x * lax.rsqrt(jnp.mean(x * x, axis=-1, keepdims=True) + RMS_EPS)
 
 
-def prepare(arr_ref, rate_ref, q_ref, kv_ref, qn_ref, ks_ref):
-    n, _, t, _ = arr_ref.shape
-    for j in range(n):
-        rows = slice(j * t, (j + 1) * t)
-        q, k, v = arr_ref[j, 0], arr_ref[j, 1], arr_ref[j, 2]
+def prepare(where_ref, rate_ref, *refs):
+    pieces, (q_ref, kv_ref, qn_ref, ks_ref) = refs[:-4], refs[-4:]
+    t = pieces[0].shape[1]
+    for d, piece in enumerate(pieces):
+        rows = pl.ds(pl.multiple_of((where_ref[2] ^ d) * t, t), t)
+        q, k, v = piece[0], piece[1], piece[2]
         q_ref[rows] = q
         kv_ref[0, rows] = k
         kv_ref[1, rows] = v
@@ -143,23 +153,23 @@
     rate = rate_ref[0]
     chip = where_ref[0]
 
-    def one_matrix(m, carry):
+    xs = []
+    for m in range(3):
         g = jnp.concatenate([merged_rows(g_own, m), merged_rows(g_other, m)], axis=0)
-        norm = jnp.sqrt(jnp.sum(g * g, keepdims=True))
-        x = g / (norm + NORM_EPS)
-        for _ in range(NS_STEPS):
-            low = x.astype(BF16)
-            gram = dot_nt(low, low)
-            gram_low = gram.astype(BF16)
-            poly = NS_2 * gram + NS_3 * dot_nn(gram_low, gram_low)
-            x = NS_1 * x + dot_nn(poly.astype(BF16), low)
-        x_ref[...] = x
+        xs.append(g / (jnp.sqrt(jnp.sum(g * g, keepdims=True)) + NORM_EPS))
+    for _ in range(NS_STEPS):
+        lows = [x.astype(BF16) for x in xs]
+        grams = [dot_nt(low, low) for low in lows]
+        gram_lows = [gram.astype(BF16) for gram in grams]
+        squares = [dot_nn(gram, gram) for gram in gram_lows]
+        polys = [(NS_2 * gram + NS_3 * sq).astype(BF16) for gram, sq in zip(grams, squares)]
+        moved = [dot_nn(poly, low) for poly, low in zip(polys, lows)]
+        xs = [NS_1 * x + move for x, move in zip(xs, moved)]
+    for m, x in enumerate(xs):
         fresh_ref[m, :half] = (merged_rows(old_own, m) - rate * x[:half]).astype(BF16)
         fresh_ref[m, half:] = (merged_rows(old_other, m) - rate * x[half:]).astype(BF16)
-        rows_ref[m] = state_ref[m] - rate * x_ref[pl.ds(pl.multiple_of(chip * r, r), r)]
-        return carry
-
-    lax.fori_loop(0, 3, one_matrix, 0)
+        x_ref[m] = x[:half]
+        rows_ref[m] = state_ref[m] - rate * x_ref[m, pl.ds(pl.multiple_of(chip * r, r), r)]
     gate = dot_nt(qn_ref[...], fresh_ref[0])
     up = dot_nt(qn_ref[...], fresh_ref[1])
     active = (jax.nn.silu(gate) * up).astype(BF16)
@@ -181,7 +191,7 @@
     rows = fast_state.shape[2]
     chip = lax.axis_index(CHIPS)
     core = lax.axis_index("core")
-    where = jnp.stack([chip, core]).astype(jnp.int32)
+    where = jnp.stack([chip, core, lax.axis_index("head")]).astype(jnp.int32)
     state = fast_state[:, 0]
     swap = [(0, 1), (1, 0)]
 
@@ -191,24 +201,33 @@
     def exchanged(pieces, axis):
         return lax.all_to_all(pieces, axis, 0, 0, tiled=True)
 
-    old_copies = local_call(copies_of, shape((chips, 3, rows, hd)), (state,))
-    split = local_call(split_heads, shape((heads, 3, tok_part, hd)), (qkv,))
-    arrived = exchanged(split, "head")
+    def behind(distance):
+        return [(i, (i + distance) % chips) for i in range(chips)]
+
+    old_copies = local_call(copies_of, shape((chips, 3, rows, hd)), (state,), hbm_out=(0,))
+    split = local_call(
+        split_heads, [shape((3, tok_part, hd))] * heads, (where, qkv), smem=(0,), hbm_in=(1,)
+    )
     old_own = exchanged(old_copies, CHIPS)
+    pieces = [split[0]] + [
+        lax.ppermute(split[d], "head", [(i, i ^ d) for i in range(heads)])
+        for d in range(1, heads)
+    ]
     q, kv, q_norm, ks = local_call(
         prepare,
         [shape((tok, hd)), shape((2, tok, hd)), shape((tok, hd)), shape((2, tok, hd))],
-        (arrived, token_rate),
+        (where, token_rate, *pieces),
+        smem=(0,),
     )
     ks_other = lax.ppermute(ks, "core", swap)
-    before = WINDOW // (2 * tok)
-    own_blocks = [kv] + [
-        lax.ppermute(kv, CHIPS, [(i - d, i) for i in range(d, chips)]) for d in range(1, before + 1)
-    ]
-    own_kv = jnp.stack(own_blocks)
-    partial = local_call(gradient, shape((chips, 3, rows, hd)), (ks, ks_other, old_own))
+    one = lax.ppermute(kv, CHIPS, behind(1))
+    three = lax.ppermute(kv, CHIPS, behind(3))
+    four = lax.ppermute(kv, CHIPS, behind(4))
+    two = lax.ppermute(one, CHIPS, behind(1))
+    own_kv = jnp.stack([kv, one, two, three, four])
+    partial = local_call(gradient, shape((chips, 3, rows, hd)), (ks, ks_other, old_own), hbm_out=(0,))
     parts = exchanged(partial, CHIPS)
-    g_copies = local_call(sum_and_copy, shape((chips, 3, rows, hd)), (parts,))
+    g_copies = local_call(sum_and_copy, shape((chips, 3, rows, hd)), (parts,), hbm_out=(0,))
     g_own = exchanged(g_copies, CHIPS)
     other_kv = lax.ppermute(own_kv, "core", swap)
     attention = local_call(attend, shape((tok, hd), F32), (where, q, own_kv, other_kv), smem=(0,))
@@ -219,14 +238,15 @@
         [shape((3, rows, hd), F32), shape((tok, hd))],
         (where, head_rate, g_own, g_other, old_own, old_other, state, q_norm, attention),
         smem=(0, 1),
+        hbm_out=(0, 1),
         scratch=[
-            pltpu.VMEM((2 * chips * rows, hd), F32),
+            pltpu.VMEM((3, chips * rows, hd), F32),
             pltpu.VMEM((3, 2 * chips * rows, hd), BF16),
         ],
     )
     back = exchanged(combined.reshape(heads, tok_part, hd), "head")
     return (
-        local_call(join_heads, shape((tok_part, width)), (back,)),
+        local_call(join_heads, shape((tok_part, width)), (back,), hbm_out=(0,)),
         new_rows[:, None],
     )
 

time: 187 us -> 176 us (0.941)
  the two profiles are of different devices: /device:TPU:104 before, /device:TPU:1 now
where the time goes in v2:
time: 176 us; the launch traced here: 175 us
  starting transfers between devices  89.7 us (51%)
  waiting for transfers between devices  48.2 us (27%)
  blocking collectives  16.9 us (10%)
  Pallas kernels  15.9 us (9%)
  local copies, waits for them, and re-layouts  2.96 us (2%)
    all_to_all x3, starting transfers between devices, exchanged(): return lax.all_to_all(pieces, axis, 0, 0, tiled=True)  39.2 us
    ppermute x7, starting transfers between devices, shards(): lax.ppermute(split[d], 'head', [(i, i ^ d) for i in range(heads)])  23.2 us
    ppermute x1, waiting for transfers between devices, shards(): one = lax.ppermute(kv, CHIPS, behind(1))  21.4 us
    ppermute x1, waiting for transfers between devices, shards(): four = lax.ppermute(kv, CHIPS, behind(4))  17.5 us
    all_to_all x1, blocking collectives, exchanged(): return lax.all_to_all(pieces, axis, 0, 0, tiled=True)  16.9 us
    pallas_call x8, Pallas kernels, local_call(): pl.pallas_call(body, in_specs=specs, out_specs=out_specs[0] if single els...  15.9 us
    ppermute x1, starting transfers between devices, shards(): ks_other = lax.ppermute(ks, 'core', swap)  5.69 us
    ppermute x1, starting transfers between devices, shards(): three = lax.ppermute(kv, CHIPS, behind(3))  5.25 us
  transfers between devices with their start and end apart: 18, of which 5 were waited for; matrix products, arithmetic and copies ran while one was open for 1% of the time, Pallas kernels for 3%

profile of v2, /device:TPU:1, one launch (start us, length us, event | category | flops | bytes accessed | tf_op | source)
XLA Modules:
  0.0 175.3 jit_solution(17129063522710359982)
XLA Ops:
  0.6 0.0 copy-start.1
  0.7 0.8 copy-done.1
  1.5 0.9 shard_map.61
  2.4 16.5 %all-to-all-start = ((bf16[32,3,8,512]{3,2,1,0:T(8,128)(2,1)}), bf16[32,3,8,512]{3,2,1,0:T(8,128)(2,1)S(1)}, u32[]{:S(2)}, u32[]{:S(2)}) async-start(bf16[32,3,8,512]{3,2,1,0:T(8,128)(2,1)} %shard_map.61), calls=%async_computation | async-start | bytes 1572864 | tf_op jit(solution)/shard_map/all_to_all | solution.py:202
  18.9 0.1 pad_add_fusion.where_ref
  19.0 0.6 shard_map.59
  19.6 3.1 %collective-permute-start = (bf16[3,16,512]{2,1,0:T(8,128)(2,1)S(1)}, bf16[3,16,512]{2,1,0:T(8,128)(2,1)S(1)}, u32[]{:S(2)}, u32[]{:S(2)}) collective-permute-start(bf16[3,16,512]{2,1,0:T(8,128)(2,1)S(1)} %get-tuple-element.17), channel_id=1, source_target_pairs={{0,1},{1,0},{2,3},{3,2},{4,5},{5,4},{6,7},{7,6},{8,9},{9,8},{10,11... | collective-permute-start | bytes 147464 | tf_op jit(solution)/shard_map/ppermute | solution.py:213
  22.7 4.4 %collective-permute-start.1 = (bf16[3,16,512]{2,1,0:T(8,128)(2,1)S(1)}, bf16[3,16,512]{2,1,0:T(8,128)(2,1)S(1)}, u32[]{:S(2)}, u32[]{:S(2)}) collective-permute-start(bf16[3,16,512]{2,1,0:T(8,128)(2,1)S(1)} %get-tuple-element.18), channel_id=1, source_target_pairs={{0,2},{1,3},{2,0},{3,1},{4,6},{5,7},{6,4},{7,5},{8,10},{9,11},{10,... | collective-permute-start | bytes 147464 | tf_op jit(solution)/shard_map/ppermute | solution.py:213
  27.1 2.1 %collective-permute-start.2 = (bf16[3,16,512]{2,1,0:T(8,128)(2,1)S(1)}, bf16[3,16,512]{2,1,0:T(8,128)(2,1)S(1)}, u32[]{:S(2)}, u32[]{:S(2)}) collective-permute-start(bf16[3,16,512]{2,1,0:T(8,128)(2,1)S(1)} %get-tuple-element.19), channel_id=1, source_target_pairs={{0,3},{1,2},{2,1},{3,0},{4,7},{5,6},{6,5},{7,4},{8,11},{9,10},{10,... | collective-permute-start | bytes 147464 | tf_op jit(solution)/shard_map/ppermute | solution.py:213
  29.2 2.3 %collective-permute-start.3 = (bf16[3,16,512]{2,1,0:T(8,128)(2,1)S(1)}, bf16[3,16,512]{2,1,0:T(8,128)(2,1)S(1)}, u32[]{:S(2)}, u32[]{:S(2)}) collective-permute-start(bf16[3,16,512]{2,1,0:T(8,128)(2,1)S(1)} %get-tuple-element.20), channel_id=1, source_target_pairs={{0,4},{1,5},{2,6},{3,7},{4,0},{5,1},{6,2},{7,3},{8,12},{9,13},{10,... | collective-permute-start | bytes 147464 | tf_op jit(solution)/shard_map/ppermute | solution.py:213
  31.5 2.7 %collective-permute-start.4 = (bf16[3,16,512]{2,1,0:T(8,128)(2,1)S(1)}, bf16[3,16,512]{2,1,0:T(8,128)(2,1)S(1)}, u32[]{:S(2)}, u32[]{:S(2)}) collective-permute-start(bf16[3,16,512]{2,1,0:T(8,128)(2,1)S(1)} %get-tuple-element.21), channel_id=1, source_target_pairs={{0,5},{1,4},{2,7},{3,6},{4,1},{5,0},{6,3},{7,2},{8,13},{9,12},{10,... | collective-permute-start | bytes 147464 | tf_op jit(solution)/shard_map/ppermute | solution.py:213
  34.2 0.0 collective-permute-done.refs_1_
  34.2 5.7 %collective-permute-start.5 = (bf16[3,16,512]{2,1,0:T(8,128)(2,1)S(1)}, bf16[3,16,512]{2,1,0:T(8,128)(2,1)S(1)}, u32[]{:S(2)}, u32[]{:S(2)}) collective-permute-start(bf16[3,16,512]{2,1,0:T(8,128)(2,1)S(1)} %get-tuple-element.22), channel_id=1, source_target_pairs={{0,6},{1,7},{2,4},{3,5},{4,2},{5,3},{6,0},{7,1},{8,14},{9,15},{10,... | collective-permute-start | bytes 147464 | tf_op jit(solution)/shard_map/ppermute | solution.py:213
  39.9 0.0 collective-permute-done.1.refs_2_
  39.9 2.9 %collective-permute-start.6 = (bf16[3,16,512]{2,1,0:T(8,128)(2,1)S(1)}, bf16[3,16,512]{2,1,0:T(8,128)(2,1)S(1)}, u32[]{:S(2)}, u32[]{:S(2)}) collective-permute-start(bf16[3,16,512]{2,1,0:T(8,128)(2,1)S(1)} %get-tuple-element.23), channel_id=1, source_target_pairs={{0,7},{1,6},{2,5},{3,4},{4,3},{5,2},{6,1},{7,0},{8,15},{9,14},{10,... | collective-permute-start | bytes 147464 | tf_op jit(solution)/shard_map/ppermute | solution.py:213
  42.9 0.1 copy.6.rate_ref
  43.0 0.0 collective-permute-done.2.refs_3_
  43.0 0.0 collective-permute-done.3.refs_4_
  43.0 0.0 collective-permute-done.5.refs_6_
  43.0 3.9 %collective-permute-done.6.refs_7_ = bf16[3,16,512]{2,1,0:T(8,128)(2,1)S(1)} collective-permute-done((bf16[3,16,512]{2,1,0:T(8,128)(2,1)S(1)}, bf16[3,16,512]{2,1,0:T(8,128)(2,1)S(1)}, u32[]{:S(2)}, u32[]{:S(2)}) %collective-permute-start.6) | collective-permute-done | bytes 49184 | tf_op jit(solution)/shard_map/ppermute | solution.py:213
  46.9 0.7 shard_map.60
  47.6 5.7 %collective-permute-start.7 = (bf16[2,128,512]{2,1,0:T(8,128)(2,1)S(1)}, bf16[2,128,512]{2,1,0:T(8,128)(2,1)S(1)}, u32[]{:S(2)}, u32[]{:S(2)}) collective-permute-start(bf16[2,128,512]{2,1,0:T(8,128)(2,1)S(1)} %get-tuple-element.24.own_ref), channel_id=1, source_target_pairs={{0,8},{8,0},{1,9},{9,1},{2,10},{10,2},{3,11},{11,3},{4,12},{12,4},... | collective-permute-start | bytes 786440 | tf_op jit(solution)/shard_map/ppermute | solution.py:222
  53.3 1.1 collective-permute-done.7.other_ref
  54.4 0.0 all-to-all-done.w_ref.old_own
  54.4 1.7 shard_map.62
  56.2 11.9 %all-to-all-start.1 = ((bf16[32,3,8,512]{3,2,1,0:T(8,128)(2,1)}), bf16[32,3,8,512]{3,2,1,0:T(8,128)(2,1)S(1)}, u32[]{:S(2)}, u32[]{:S(2)}) async-start(bf16[32,3,8,512]{3,2,1,0:T(8,128)(2,1)} %shard_map.62), calls=%async_computation.1 | async-start | bytes 1572864 | tf_op jit(solution)/shard_map/all_to_all | solution.py:202
  68.1 4.0 %collective-permute-start.10 = (bf16[2,128,512]{2,1,0:T(8,128)(2,1)S(1)}, bf16[2,128,512]{2,1,0:T(8,128)(2,1)}, u32[]{:S(2)}, u32[]{:S(2)}) collective-permute-start(bf16[2,128,512]{2,1,0:T(8,128)(2,1)S(1)} %get-tuple-element.27), channel_id=1, source_target_pairs={{0,16},{16,32},{32,48},{48,64},{64,80},{80,96},{96,112},{112,128},... | collective-permute-start | bytes 786440 | tf_op jit(solution)/shard_map/ppermute | solution.py:223
  72.1 21.4 %collective-permute-done.10 = bf16[2,128,512]{2,1,0:T(8,128)(2,1)} collective-permute-done((bf16[2,128,512]{2,1,0:T(8,128)(2,1)S(1)}, bf16[2,128,512]{2,1,0:T(8,128)(2,1)}, u32[]{:S(2)}, u32[]{:S(2)}) %collective-permute-start.10) | collective-permute-done | bytes 262176 | tf_op jit(solution)/shard_map/ppermute | solution.py:223
  93.5 1.9 %collective-permute-start.11 = (bf16[2,128,512]{2,1,0:T(8,128)(2,1)}, bf16[2,128,512]{2,1,0:T(8,128)(2,1)}, u32[]{:S(2)}, u32[]{:S(2)}) collective-permute-start(bf16[2,128,512]{2,1,0:T(8,128)(2,1)} %collective-permute-done.10), channel_id=1, source_target_pairs={{0,16},{16,32},{32,48},{48,64},{64,80},{80,96},{96,112},{112,128},... | collective-permute-start | bytes 786440 | tf_op jit(solution)/shard_map/ppermute | solution.py:226
  95.4 0.0 all-to-all-done.1.arr_ref
  95.5 1.0 shard_map.63
  96.5 10.9 %all-to-all-start.2 = ((bf16[32,3,8,512]{3,2,1,0:T(8,128)(2,1)}), bf16[32,3,8,512]{3,2,1,0:T(8,128)(2,1)S(1)}, u32[]{:S(2)}, u32[]{:S(2)}) async-start(bf16[32,3,8,512]{3,2,1,0:T(8,128)(2,1)} %shard_map.63), calls=%async_computation.2 | async-start | bytes 1572864 | tf_op jit(solution)/shard_map/all_to_all | solution.py:202
  107.3 5.2 %collective-permute-start.12 = (bf16[2,128,512]{2,1,0:T(8,128)(2,1)S(1)}, bf16[2,128,512]{2,1,0:T(8,128)(2,1)S(1)}, u32[]{:S(2)}, u32[]{:S(2)}) collective-permute-start(bf16[2,128,512]{2,1,0:T(8,128)(2,1)S(1)} %get-tuple-element.27), channel_id=1, source_target_pairs={{0,48},{16,64},{32,80},{48,96},{64,112},{80,128},{96,144},{112,160... | collective-permute-start | bytes 786440 | tf_op jit(solution)/shard_map/ppermute | solution.py:224
  112.6 3.1 %collective-permute-start.13 = (bf16[2,128,512]{2,1,0:T(8,128)(2,1)S(1)}, bf16[2,128,512]{2,1,0:T(8,128)(2,1)S(1)}, u32[]{:S(2)}, u32[]{:S(2)}) collective-permute-start(bf16[2,128,512]{2,1,0:T(8,128)(2,1)S(1)} %get-tuple-element.27), channel_id=1, source_target_pairs={{0,64},{16,80},{32,96},{48,112},{64,128},{80,144},{96,160},{112,17... | collective-permute-start | bytes 786440 | tf_op jit(solution)/shard_map/ppermute | solution.py:225
  115.7 1.0 bitcast_dynamic-update-slice_fusion.3
  116.7 1.0 bitcast_dynamic-update-slice_fusion.2
  117.7 4.2 %collective-permute-done.12 = bf16[2,128,512]{2,1,0:T(8,128)(2,1)S(1)} collective-permute-done((bf16[2,128,512]{2,1,0:T(8,128)(2,1)S(1)}, bf16[2,128,512]{2,1,0:T(8,128)(2,1)S(1)}, u32[]{:S(2)}, u32[]{:S(2)}) %collective-permute-start.12) | collective-permute-done | bytes 262176 | tf_op jit(solution)/shard_map/ppermute | solution.py:224
  121.9 17.5 %collective-permute-done.13 = bf16[2,128,512]{2,1,0:T(8,128)(2,1)S(1)} collective-permute-done((bf16[2,128,512]{2,1,0:T(8,128)(2,1)S(1)}, bf16[2,128,512]{2,1,0:T(8,128)(2,1)S(1)}, u32[]{:S(2)}, u32[]{:S(2)}) %collective-permute-start.13) | collective-permute-done | bytes 262176 | tf_op jit(solution)/shard_map/ppermute | solution.py:225
  139.4 3.0 %collective-permute-start.14 = (bf16[5,2,128,512]{3,2,1,0:T(8,128)(2,1)S(1)}, bf16[5,2,128,512]{3,2,1,0:T(8,128)(2,1)}, u32[]{:S(2)}, u32[]{:S(2)}) collective-permute-start(bf16[5,2,128,512]{3,2,1,0:T(8,128)(2,1)S(1)} %bitcast_dynamic-update-slice_fusion.own_ref), channel_id=1, source_target_pairs={{0,8},{8,0},{1,9},{9,1},{2,10},{10,2},{3,11},{11,3},{4,12},{12,4},... | collective-permute-start | bytes 3932168 | tf_op jit(solution)/shard_map/ppermute | solution.py:232
  142.4 1.9 %collective-permute-start.9 = (bf16[32,3,8,512]{3,2,1,0:T(8,128)(2,1)S(1)}, bf16[32,3,8,512]{3,2,1,0:T(8,128)(2,1)}, u32[]{:S(2)}, u32[]{:S(2)}) collective-permute-start(bf16[32,3,8,512]{3,2,1,0:T(8,128)(2,1)S(1)} %all-to-all-done.w_ref.old_own), channel_id=1, source_target_pairs={{0,8},{8,0},{1,9},{9,1},{2,10},{10,2},{3,11},{11,3},{4,12},{12,4},... | collective-permute-start | bytes 2359304 | tf_op jit(solution)/shard_map/ppermute | solution.py:234
  144.3 0.0 all-to-all-done.2.g_own
  144.4 2.4 %collective-permute-start.8 = (bf16[32,3,8,512]{3,2,1,0:T(8,128)(2,1)S(1)}, bf16[32,3,8,512]{3,2,1,0:T(8,128)(2,1)S(1)}, u32[]{:S(2)}, u32[]{:S(2)}) collective-permute-start(bf16[32,3,8,512]{3,2,1,0:T(8,128)(2,1)S(1)} %all-to-all-done.2.g_own), channel_id=1, source_target_pairs={{0,8},{8,0},{1,9},{9,1},{2,10},{10,2},{3,11},{11,3},{4,12},{12,4},... | collective-permute-start | bytes 2359304 | tf_op jit(solution)/shard_map/ppermute | solution.py:235
  147.4 0.0 collective-permute-done.14.other_ref
  147.4 0.0 copy-start.2
  147.4 2.5 %shard_map.64.att_ref = f32[128,512]{1,0:T(8,128)S(1)} custom-call(s32[3]{0:T(128)S(1)} %pad_add_fusion.where_ref, bf16[128,512]{1,0:T(8,128)(2,1)S(1)} %get-tuple-element.26.q_ref, bf16[5,2,128,512]{3,2,1,0:T(8,128)(2,1)S(1)} %bitcast_dynamic-update-slice_fusion.own_ref, bf16[5,2,128,512]{3,2,1,0:T(8,128)(2,1)} %collective-permute-done.14.other_ref), custom_call_target="tpu_custom_call" | custom-call | tf_op jit(solution)/shard_map/pallas_call | solution.py:44
  150.0 7.7 %shard_map.65 = (f32[3,8,512]{2,1,0:T(8,128)}, bf16[128,512]{1,0:T(8,128)(2,1)S(1)}) custom-call(s32[3]{0:T(128)S(1)} %pad_add_fusion.where_ref, f32[1]{0:T(128)S(6)} %copy.12.rate_ref, bf16[32,3,8,512]{3,2,1,0:T(8,128)(2,1)S(1)} %all-to-all-done.2.g_own, bf16[32,3,8,512]{3,2,1,0:T(8,128)(2,1)S(1)} %collective-permute-done.8.g_other, ...), custom_call_target="tpu_custom_call" | custom-call | tf_op jit(solution)/shard_map/pallas_call | solution.py:44
  157.7 16.9 %all_to_all.20.arr_ref = bf16[8,16,512]{2,1,0:T(8,128)(2,1)S(1)} all-to-all(bf16[8,16,512]{2,1,0:T(8,128)(2,1)S(1)} %bitcast.20), channel_id=1, replica_groups=mesh['z'=8,'y'=4,'core'=2,'head'=8] {'head'}, dimensions={0} | all-to-all | bytes 262144 | tf_op jit(solution)/shard_map/all_to_all | solution.py:202
  174.6 0.7 shard_map.66
  (12 shorter events, 0.1 us)
Async XLA Ops:
  0.6 18.4 %copy-start = (bf16[3,16,4096]{2,1,0:T(8,128)(2,1)S(1)}, bf16[3,16,4096]{2,1,0:T(8,128)(2,1)}, u32[]{:S(2)}) copy-start(bf16[3,16,4096]{2,1,0:T(8,128)(2,1)} %qkv_ref.1) | copy-start | bytes 1179652
  0.6 0.9 copy-start.1
  1.5 41.4 %copy-start.3 = (f32[128,1]{0,1:T(1,128)S(1)}, f32[128,1]{0,1:T(1,128)}, u32[]{:S(2)}) copy-start(f32[128,1]{0,1:T(1,128)} %param.5) | copy-start | bytes 1540
  2.4 52.0 %all-to-all-start = ((bf16[32,3,8,512]{3,2,1,0:T(8,128)(2,1)}), bf16[32,3,8,512]{3,2,1,0:T(8,128)(2,1)S(1)}, u32[]{:S(2)}, u32[]{:S(2)}) async-start(bf16[32,3,8,512]{3,2,1,0:T(8,128)(2,1)} %shard_map.61), calls=%async_computation | async-start | bytes 1572864 | tf_op jit(solution)/shard_map/all_to_all | solution.py:202
  19.6 14.6 %collective-permute-start = (bf16[3,16,512]{2,1,0:T(8,128)(2,1)S(1)}, bf16[3,16,512]{2,1,0:T(8,128)(2,1)S(1)}, u32[]{:S(2)}, u32[]{:S(2)}) collective-permute-start(bf16[3,16,512]{2,1,0:T(8,128)(2,1)S(1)} %get-tuple-element.17), channel_id=1, source_target_pairs={{0,1},{1,0},{2,3},{3,2},{4,5},{5,4},{6,7},{7,6},{8,9},{9,8},{10,11... | collective-permute-start | bytes 147464 | tf_op jit(solution)/shard_map/ppermute | solution.py:213
  22.7 17.2 %collective-permute-start.1 = (bf16[3,16,512]{2,1,0:T(8,128)(2,1)S(1)}, bf16[3,16,512]{2,1,0:T(8,128)(2,1)S(1)}, u32[]{:S(2)}, u32[]{:S(2)}) collective-permute-start(bf16[3,16,512]{2,1,0:T(8,128)(2,1)S(1)} %get-tuple-element.18), channel_id=1, source_target_pairs={{0,2},{1,3},{2,0},{3,1},{4,6},{5,7},{6,4},{7,5},{8,10},{9,11},{10,... | collective-permute-start | bytes 147464 | tf_op jit(solution)/shard_map/ppermute | solution.py:213
  27.1 15.9 %collective-permute-start.2 = (bf16[3,16,512]{2,1,0:T(8,128)(2,1)S(1)}, bf16[3,16,512]{2,1,0:T(8,128)(2,1)S(1)}, u32[]{:S(2)}, u32[]{:S(2)}) collective-permute-start(bf16[3,16,512]{2,1,0:T(8,128)(2,1)S(1)} %get-tuple-element.19), channel_id=1, source_target_pairs={{0,3},{1,2},{2,1},{3,0},{4,7},{5,6},{6,5},{7,4},{8,11},{9,10},{10,... | collective-permute-start | bytes 147464 | tf_op jit(solution)/shard_map/ppermute | solution.py:213
  29.2 13.8 %collective-permute-start.3 = (bf16[3,16,512]{2,1,0:T(8,128)(2,1)S(1)}, bf16[3,16,512]{2,1,0:T(8,128)(2,1)S(1)}, u32[]{:S(2)}, u32[]{:S(2)}) collective-permute-start(bf16[3,16,512]{2,1,0:T(8,128)(2,1)S(1)} %get-tuple-element.20), channel_id=1, source_target_pairs={{0,4},{1,5},{2,6},{3,7},{4,0},{5,1},{6,2},{7,3},{8,12},{9,13},{10,... | collective-permute-start | bytes 147464 | tf_op jit(solution)/shard_map/ppermute | solution.py:213
  31.5 11.5 %collective-permute-start.4 = (bf16[3,16,512]{2,1,0:T(8,128)(2,1)S(1)}, bf16[3,16,512]{2,1,0:T(8,128)(2,1)S(1)}, u32[]{:S(2)}, u32[]{:S(2)}) collective-permute-start(bf16[3,16,512]{2,1,0:T(8,128)(2,1)S(1)} %get-tuple-element.21), channel_id=1, source_target_pairs={{0,5},{1,4},{2,7},{3,6},{4,1},{5,0},{6,3},{7,2},{8,13},{9,12},{10,... | collective-permute-start | bytes 147464 | tf_op jit(solution)/shard_map/ppermute | solution.py:213
  34.2 8.8 %collective-permute-start.5 = (bf16[3,16,512]{2,1,0:T(8,128)(2,1)S(1)}, bf16[3,16,512]{2,1,0:T(8,128)(2,1)S(1)}, u32[]{:S(2)}, u32[]{:S(2)}) collective-permute-start(bf16[3,16,512]{2,1,0:T(8,128)(2,1)S(1)} %get-tuple-element.22), channel_id=1, source_target_pairs={{0,6},{1,7},{2,4},{3,5},{4,2},{5,3},{6,0},{7,1},{8,14},{9,15},{10,... | collective-permute-start | bytes 147464 | tf_op jit(solution)/shard_map/ppermute | solution.py:213
  39.9 6.9 %collective-permute-start.6 = (bf16[3,16,512]{2,1,0:T(8,128)(2,1)S(1)}, bf16[3,16,512]{2,1,0:T(8,128)(2,1)S(1)}, u32[]{:S(2)}, u32[]{:S(2)}) collective-permute-start(bf16[3,16,512]{2,1,0:T(8,128)(2,1)S(1)} %get-tuple-element.23), channel_id=1, source_target_pairs={{0,7},{1,6},{2,5},{3,4},{4,3},{5,2},{6,1},{7,0},{8,15},{9,14},{10,... | collective-permute-start | bytes 147464 | tf_op jit(solution)/shard_map/ppermute | solution.py:213
  47.6 6.8 %collective-permute-start.7 = (bf16[2,128,512]{2,1,0:T(8,128)(2,1)S(1)}, bf16[2,128,512]{2,1,0:T(8,128)(2,1)S(1)}, u32[]{:S(2)}, u32[]{:S(2)}) collective-permute-start(bf16[2,128,512]{2,1,0:T(8,128)(2,1)S(1)} %get-tuple-element.24.own_ref), channel_id=1, source_target_pairs={{0,8},{8,0},{1,9},{9,1},{2,10},{10,2},{3,11},{11,3},{4,12},{12,4},... | collective-permute-start | bytes 786440 | tf_op jit(solution)/shard_map/ppermute | solution.py:222
  56.2 39.3 %all-to-all-start.1 = ((bf16[32,3,8,512]{3,2,1,0:T(8,128)(2,1)}), bf16[32,3,8,512]{3,2,1,0:T(8,128)(2,1)S(1)}, u32[]{:S(2)}, u32[]{:S(2)}) async-start(bf16[32,3,8,512]{3,2,1,0:T(8,128)(2,1)} %shard_map.62), calls=%async_computation.1 | async-start | bytes 1572864 | tf_op jit(solution)/shard_map/all_to_all | solution.py:202
  68.1 25.5 %collective-permute-start.10 = (bf16[2,128,512]{2,1,0:T(8,128)(2,1)S(1)}, bf16[2,128,512]{2,1,0:T(8,128)(2,1)}, u32[]{:S(2)}, u32[]{:S(2)}) collective-permute-start(bf16[2,128,512]{2,1,0:T(8,128)(2,1)S(1)} %get-tuple-element.27), channel_id=1, source_target_pairs={{0,16},{16,32},{32,48},{48,64},{64,80},{80,96},{96,112},{112,128},... | collective-permute-start | bytes 786440 | tf_op jit(solution)/shard_map/ppermute | solution.py:223
  93.5 23.1 %collective-permute-start.11 = (bf16[2,128,512]{2,1,0:T(8,128)(2,1)}, bf16[2,128,512]{2,1,0:T(8,128)(2,1)}, u32[]{:S(2)}, u32[]{:S(2)}) collective-permute-start(bf16[2,128,512]{2,1,0:T(8,128)(2,1)} %collective-permute-done.10), channel_id=1, source_target_pairs={{0,16},{16,32},{32,48},{48,64},{64,80},{80,96},{96,112},{112,128},... | collective-permute-start | bytes 786440 | tf_op jit(solution)/shard_map/ppermute | solution.py:226
  96.5 47.9 %all-to-all-start.2 = ((bf16[32,3,8,512]{3,2,1,0:T(8,128)(2,1)}), bf16[32,3,8,512]{3,2,1,0:T(8,128)(2,1)S(1)}, u32[]{:S(2)}, u32[]{:S(2)}) async-start(bf16[32,3,8,512]{3,2,1,0:T(8,128)(2,1)} %shard_map.63), calls=%async_computation.2 | async-start | bytes 1572864 | tf_op jit(solution)/shard_map/all_to_all | solution.py:202
  107.3 14.6 %collective-permute-start.12 = (bf16[2,128,512]{2,1,0:T(8,128)(2,1)S(1)}, bf16[2,128,512]{2,1,0:T(8,128)(2,1)S(1)}, u32[]{:S(2)}, u32[]{:S(2)}) collective-permute-start(bf16[2,128,512]{2,1,0:T(8,128)(2,1)S(1)} %get-tuple-element.27), channel_id=1, source_target_pairs={{0,48},{16,64},{32,80},{48,96},{64,112},{80,128},{96,144},{112,160... | collective-permute-start | bytes 786440 | tf_op jit(solution)/shard_map/ppermute | solution.py:224
  112.6 26.8 %collective-permute-start.13 = (bf16[2,128,512]{2,1,0:T(8,128)(2,1)S(1)}, bf16[2,128,512]{2,1,0:T(8,128)(2,1)S(1)}, u32[]{:S(2)}, u32[]{:S(2)}) collective-permute-start(bf16[2,128,512]{2,1,0:T(8,128)(2,1)S(1)} %get-tuple-element.27), channel_id=1, source_target_pairs={{0,64},{16,80},{32,96},{48,112},{64,128},{80,144},{96,160},{112,17... | collective-permute-start | bytes 786440 | tf_op jit(solution)/shard_map/ppermute | solution.py:225
  139.4 8.0 %collective-permute-start.14 = (bf16[5,2,128,512]{3,2,1,0:T(8,128)(2,1)S(1)}, bf16[5,2,128,512]{3,2,1,0:T(8,128)(2,1)}, u32[]{:S(2)}, u32[]{:S(2)}) collective-permute-start(bf16[5,2,128,512]{3,2,1,0:T(8,128)(2,1)S(1)} %bitcast_dynamic-update-slice_fusion.own_ref), channel_id=1, source_target_pairs={{0,8},{8,0},{1,9},{9,1},{2,10},{10,2},{3,11},{11,3},{4,12},{12,4},... | collective-permute-start | bytes 3932168 | tf_op jit(solution)/shard_map/ppermute | solution.py:232
  142.4 7.6 %collective-permute-start.9 = (bf16[32,3,8,512]{3,2,1,0:T(8,128)(2,1)S(1)}, bf16[32,3,8,512]{3,2,1,0:T(8,128)(2,1)}, u32[]{:S(2)}, u32[]{:S(2)}) collective-permute-start(bf16[32,3,8,512]{3,2,1,0:T(8,128)(2,1)S(1)} %all-to-all-done.w_ref.old_own), channel_id=1, source_target_pairs={{0,8},{8,0},{1,9},{9,1},{2,10},{10,2},{3,11},{11,3},{4,12},{12,4},... | collective-permute-start | bytes 2359304 | tf_op jit(solution)/shard_map/ppermute | solution.py:234
  144.4 5.6 %collective-permute-start.8 = (bf16[32,3,8,512]{3,2,1,0:T(8,128)(2,1)S(1)}, bf16[32,3,8,512]{3,2,1,0:T(8,128)(2,1)S(1)}, u32[]{:S(2)}, u32[]{:S(2)}) collective-permute-start(bf16[32,3,8,512]{3,2,1,0:T(8,128)(2,1)S(1)} %all-to-all-done.2.g_own), channel_id=1, source_target_pairs={{0,8},{8,0},{1,9},{9,1},{2,10},{10,2},{3,11},{11,3},{4,12},{12,4},... | collective-permute-start | bytes 2359304 | tf_op jit(solution)/shard_map/ppermute | solution.py:235
  147.4 2.6 %copy-start.2 = (f32[3,1,8,512]{3,2,1,0:T(8,128)S(1)}, f32[3,1,8,512]{3,2,1,0:T(8,128)}, u32[]{:S(2)}) copy-start(f32[3,1,8,512]{3,2,1,0:T(8,128)} %param.7) | copy-start | bytes 147460

commit v3 on v2

--- a/solution.py
+++ b/solution.py
@@ -51,24 +51,22 @@
     )(*args)
 
 
-def split_heads(where_ref, qkv_ref, *out_refs):
-    hd = out_refs[0].shape[2]
-    for d, out_ref in enumerate(out_refs):
-        start = pl.multiple_of((where_ref[2] ^ d) * hd, hd)
+def split_heads(qkv_ref, out_ref):
+    for h in range(out_ref.shape[0]):
+        hd = out_ref.shape[3]
         for j in range(3):
-            out_ref[j] = qkv_ref[j, :, pl.ds(start, hd)]
+            out_ref[h, j] = qkv_ref[j, :, h * hd : (h + 1) * hd]
 
 
 def rms_scaled(x):
     return x * lax.rsqrt(jnp.mean(x * x, axis=-1, keepdims=True) + RMS_EPS)
 
 
-def prepare(where_ref, rate_ref, *refs):
-    pieces, (q_ref, kv_ref, qn_ref, ks_ref) = refs[:-4], refs[-4:]
-    t = pieces[0].shape[1]
-    for d, piece in enumerate(pieces):
-        rows = pl.ds(pl.multiple_of((where_ref[2] ^ d) * t, t), t)
-        q, k, v = piece[0], piece[1], piece[2]
+def prepare(arr_ref, rate_ref, q_ref, kv_ref, qn_ref, ks_ref):
+    n, _, t, _ = arr_ref.shape
+    for j in range(n):
+        rows = slice(j * t, (j + 1) * t)
+        q, k, v = arr_ref[j, 0], arr_ref[j, 1], arr_ref[j, 2]
         q_ref[rows] = q
         kv_ref[0, rows] = k
         kv_ref[1, rows] = v
@@ -191,7 +189,7 @@
     rows = fast_state.shape[2]
     chip = lax.axis_index(CHIPS)
     core = lax.axis_index("core")
-    where = jnp.stack([chip, core, lax.axis_index("head")]).astype(jnp.int32)
+    where = jnp.stack([chip, core]).astype(jnp.int32)
     state = fast_state[:, 0]
     swap = [(0, 1), (1, 0)]
 
@@ -206,24 +204,21 @@
 
     old_copies = local_call(copies_of, shape((chips, 3, rows, hd)), (state,), hbm_out=(0,))
     split = local_call(
-        split_heads, [shape((3, tok_part, hd))] * heads, (where, qkv), smem=(0,), hbm_in=(1,)
+        split_heads, shape((heads, 3, tok_part, hd)), (qkv,), hbm_in=(0,), hbm_out=(0,)
     )
     old_own = exchanged(old_copies, CHIPS)
-    pieces = [split[0]] + [
-        lax.ppermute(split[d], "head", [(i, i ^ d) for i in range(heads)])
-        for d in range(1, heads)
-    ]
+    arrived = exchanged(split, "head")
     q, kv, q_norm, ks = local_call(
         prepare,
         [shape((tok, hd)), shape((2, tok, hd)), shape((tok, hd)), shape((2, tok, hd))],
-        (where, token_rate, *pieces),
-        smem=(0,),
+        (arrived, token_rate),
     )
     ks_other = lax.ppermute(ks, "core", swap)
     one = lax.ppermute(kv, CHIPS, behind(1))
     three = lax.ppermute(kv, CHIPS, behind(3))
     four = lax.ppermute(kv, CHIPS, behind(4))
-    two = lax.ppermute(one, CHIPS, behind(1))
+    relay = [(2 * i, 2 * j) for i, j in behind(1)] + [(2 * j + 1, 2 * i + 1) for i, j in behind(1)]
+    two = lax.ppermute(jnp.where(core == 0, one, three), SEQ, relay)
     own_kv = jnp.stack([kv, one, two, three, four])
     partial = local_call(gradient, shape((chips, 3, rows, hd)), (ks, ks_other, old_own), hbm_out=(0,))
     parts = exchanged(partial, CHIPS)

time: 176 us -> 166 us (0.943)
  starting transfers between devices: 89.7 us -> 66.5 us
  waiting for transfers between devices: 48.2 us -> 67 us
  blocking collectives: 16.9 us -> 10.4 us
    ppermute x8 -> x1, starting transfers between devices: 25.1 us -> 4.5 us  [shards(): two = lax.ppermute(jnp.where(core == 0, one, three), SEQ, relay)]
    all_to_all x3 -> x4, waiting for transfers between devices: 0.01 us -> 19.2 us  [exchanged(): return lax.all_to_all(pieces, axis, 0, 0, tiled=True)]
    all_to_all x1, blocking collectives: 16.9 us -> 10.4 us  [exchanged(): return lax.all_to_all(pieces, axis, 0, 0, tiled=True)]
    ppermute x8 -> x1, waiting for transfers between devices: 3.9 us -> 0.01 us  [shards(): two = lax.ppermute(jnp.where(core == 0, one, three), SEQ, relay)]
    ppermute x1, waiting for transfers between devices: 17.5 us -> 20.7 us  [shards(): four = lax.ppermute(kv, CHIPS, behind(4))]
    all_to_all x3 -> x4, starting transfers between devices: 39.2 us -> 38.3 us  [exchanged(): return lax.all_to_all(pieces, axis, 0, 0, tiled=True)]
  transfers between devices with their start and end apart: 18 -> 12, of which waited for: 5 -> 6; matrix products, arithmetic and copies ran while one was open for 1% -> 2% of each run, Pallas kernels for 3% -> 3%
where the time goes in v3:
time: 166 us; the launch traced here: 165 us
  waiting for transfers between devices  67 us (40%)
  starting transfers between devices  66.5 us (40%)
  Pallas kernels  15.8 us (10%)
  blocking collectives  10.4 us (6%)
  local copies, waits for them, and re-layouts  3.12 us (2%)
    all_to_all x4, starting transfers between devices, exchanged(): return lax.all_to_all(pieces, axis, 0, 0, tiled=True)  38.3 us
    ppermute x1, waiting for transfers between devices, shards(): four = lax.ppermute(kv, CHIPS, behind(4))  20.7 us
    ppermute x1, waiting for transfers between devices, shards(): one = lax.ppermute(kv, CHIPS, behind(1))  20.3 us
    all_to_all x4, waiting for transfers between devices, exchanged(): return lax.all_to_all(pieces, axis, 0, 0, tiled=True)  19.2 us
    pallas_call x8, Pallas kernels, local_call(): pl.pallas_call(body, in_specs=specs, out_specs=out_specs[0] if single els...  15.8 us
    all_to_all x1, blocking collectives, exchanged(): return lax.all_to_all(pieces, axis, 0, 0, tiled=True)  10.4 us
    ppermute x1, waiting for transfers between devices, shards(): three = lax.ppermute(kv, CHIPS, behind(3))  5.75 us
    ppermute x1, starting transfers between devices, shards(): ks_other = lax.ppermute(ks, 'core', swap)  4.73 us
  transfers between devices with their start and end apart: 12, of which 6 were waited for; matrix products, arithmetic and copies ran while one was open for 2% of the time, Pallas kernels for 3%

profile of v3, /device:TPU:1, one launch (start us, length us, event | category | flops | bytes accessed | tf_op | source)
XLA Modules:
  0.0 165.2 jit_solution(10572524014717580438)
XLA Ops:
  0.6 0.0 copy-start
  0.6 1.0 copy-done
  1.6 0.0 copy-start.1
  1.6 0.8 shard_map.59
  2.4 5.9 %all-to-all-start = ((bf16[8,3,16,512]{3,2,1,0:T(8,128)(2,1)}), bf16[8,3,16,512]{3,2,1,0:T(8,128)(2,1)S(1)}, u32[]{:S(2)}, u32[]{:S(2)}) async-start(bf16[8,3,16,512]{3,2,1,0:T(8,128)(2,1)} %shard_map.59), calls=%async_computation | async-start | bytes 786432 | tf_op jit(solution)/shard_map/all_to_all | solution.py:200
  8.3 0.0 copy-start.5
  8.3 0.0 copy-done.1
  8.3 0.9 shard_map.61
  9.2 5.6 %all-to-all-done.arr_ref = bf16[8,3,16,512]{3,2,1,0:T(8,128)(2,1)S(1)} async-done(((bf16[8,3,16,512]{3,2,1,0:T(8,128)(2,1)}), bf16[8,3,16,512]{3,2,1,0:T(8,128)(2,1)S(1)}, u32[]{:S(2)}, u32[]{:S(2)}) %all-to-all-start) | async-done | bytes 393248 | tf_op jit(solution)/shard_map/all_to_all | solution.py:200
  14.9 15.0 %all-to-all-start.1 = ((bf16[32,3,8,512]{3,2,1,0:T(8,128)(2,1)}), bf16[32,3,8,512]{3,2,1,0:T(8,128)(2,1)S(1)}, u32[]{:S(2)}, u32[]{:S(2)}) async-start(bf16[32,3,8,512]{3,2,1,0:T(8,128)(2,1)} %shard_map.61), calls=%async_computation.1 | async-start | bytes 1572864 | tf_op jit(solution)/shard_map/all_to_all | solution.py:200
  29.9 0.0 copy-done.5
  29.9 0.1 copy.6.rate_ref
  30.1 0.2 shard_map.60
  30.2 4.7 %collective-permute-start = (bf16[2,128,512]{2,1,0:T(8,128)(2,1)S(1)}, bf16[2,128,512]{2,1,0:T(8,128)(2,1)S(1)}, u32[]{:S(2)}, u32[]{:S(2)}) collective-permute-start(bf16[2,128,512]{2,1,0:T(8,128)(2,1)S(1)} %get-tuple-element.8.own_ref), channel_id=1, source_target_pairs={{0,8},{8,0},{1,9},{9,1},{2,10},{10,2},{3,11},{11,3},{4,12},{12,4},... | collective-permute-start | bytes 786440 | tf_op jit(solution)/shard_map/ppermute | solution.py:216
  35.0 1.1 collective-permute-done.other_ref
  36.1 13.6 %all-to-all-done.1.w_ref.old_own = bf16[32,3,8,512]{3,2,1,0:T(8,128)(2,1)S(1)} async-done(((bf16[32,3,8,512]{3,2,1,0:T(8,128)(2,1)}), bf16[32,3,8,512]{3,2,1,0:T(8,128)(2,1)S(1)}, u32[]{:S(2)}, u32[]{:S(2)}) %all-to-all-start.1) | async-done | bytes 786464 | tf_op jit(solution)/shard_map/all_to_all | solution.py:200
  49.7 1.7 %shard_map.62 = bf16[32,3,8,512]{3,2,1,0:T(8,128)(2,1)} custom-call(bf16[2,128,512]{2,1,0:T(8,128)(2,1)S(1)} %get-tuple-element.8.own_ref, bf16[2,128,512]{2,1,0:T(8,128)(2,1)S(1)} %collective-permute-done.other_ref, bf16[32,3,8,512]{3,2,1,0:T(8,128)(2,1)S(1)} %all-to-all-done.1.w_ref.old_own), custom_call_target="tpu_custom_call" | custom-call | tf_op jit(solution)/shard_map/pallas_call | solution.py:44
  51.4 10.2 %all-to-all-start.2 = ((bf16[32,3,8,512]{3,2,1,0:T(8,128)(2,1)}), bf16[32,3,8,512]{3,2,1,0:T(8,128)(2,1)S(1)}, u32[]{:S(2)}, u32[]{:S(2)}) async-start(bf16[32,3,8,512]{3,2,1,0:T(8,128)(2,1)} %shard_map.62), calls=%async_computation.2 | async-start | bytes 1572864 | tf_op jit(solution)/shard_map/all_to_all | solution.py:200
  61.7 4.0 %collective-permute-start.3 = (bf16[2,128,512]{2,1,0:T(8,128)(2,1)S(1)}, bf16[2,128,512]{2,1,0:T(8,128)(2,1)S(1)}, u32[]{:S(2)}, u32[]{:S(2)}) collective-permute-start(bf16[2,128,512]{2,1,0:T(8,128)(2,1)S(1)} %get-tuple-element.11), channel_id=1, source_target_pairs={{0,16},{16,32},{32,48},{48,64},{64,80},{80,96},{96,112},{112,128},... | collective-permute-start | bytes 786440 | tf_op jit(solution)/shard_map/ppermute | solution.py:217
  65.7 4.3 %collective-permute-start.4 = (bf16[2,128,512]{2,1,0:T(8,128)(2,1)S(1)}, bf16[2,128,512]{2,1,0:T(8,128)(2,1)S(1)}, u32[]{:S(2)}, u32[]{:S(2)}) collective-permute-start(bf16[2,128,512]{2,1,0:T(8,128)(2,1)S(1)} %get-tuple-element.11), channel_id=1, source_target_pairs={{0,48},{16,64},{32,80},{48,96},{64,112},{80,128},{96,144},{112,160... | collective-permute-start | bytes 786440 | tf_op jit(solution)/shard_map/ppermute | solution.py:218
  70.0 20.3 %collective-permute-done.3 = bf16[2,128,512]{2,1,0:T(8,128)(2,1)S(1)} collective-permute-done((bf16[2,128,512]{2,1,0:T(8,128)(2,1)S(1)}, bf16[2,128,512]{2,1,0:T(8,128)(2,1)S(1)}, u32[]{:S(2)}, u32[]{:S(2)}) %collective-permute-start.3) | collective-permute-done | bytes 262176 | tf_op jit(solution)/shard_map/ppermute | solution.py:217
  90.3 5.8 %collective-permute-done.4 = bf16[2,128,512]{2,1,0:T(8,128)(2,1)S(1)} collective-permute-done((bf16[2,128,512]{2,1,0:T(8,128)(2,1)S(1)}, bf16[2,128,512]{2,1,0:T(8,128)(2,1)S(1)}, u32[]{:S(2)}, u32[]{:S(2)}) %collective-permute-start.4) | collective-permute-done | bytes 262176 | tf_op jit(solution)/shard_map/ppermute | solution.py:218
  96.0 0.8 broadcast_select_fusion
  96.8 4.5 %collective-permute-start.5 = (bf16[2,128,512]{2,1,0:T(8,128)(2,1)}, bf16[2,128,512]{2,1,0:T(8,128)(2,1)}, u32[]{:S(2)}, u32[]{:S(2)}) collective-permute-start(bf16[2,128,512]{2,1,0:T(8,128)(2,1)} %broadcast_select_fusion), channel_id=1, source_target_pairs={{0,16},{16,32},{32,48},{48,64},{64,80},{80,96},{96,112},{112,128},... | collective-permute-start | bytes 786440 | tf_op jit(solution)/shard_map/ppermute | solution.py:221
  101.4 0.0 all-to-all-done.2.arr_ref
  101.4 1.0 shard_map.63
  102.4 0.0 copy-done.4
  102.4 0.0 copy-done.2
  102.4 7.2 %all-to-all-start.3 = ((bf16[32,3,8,512]{3,2,1,0:T(8,128)(2,1)}), bf16[32,3,8,512]{3,2,1,0:T(8,128)(2,1)S(1)}, u32[]{:S(2)}, u32[]{:S(2)}) async-start(bf16[32,3,8,512]{3,2,1,0:T(8,128)(2,1)} %shard_map.63), calls=%async_computation.3 | async-start | bytes 1572864 | tf_op jit(solution)/shard_map/all_to_all | solution.py:200
  109.5 0.0 copy-start.3
  109.6 3.3 %collective-permute-start.6 = (bf16[2,128,512]{2,1,0:T(8,128)(2,1)S(1)}, bf16[2,128,512]{2,1,0:T(8,128)(2,1)S(1)}, u32[]{:S(2)}, u32[]{:S(2)}) collective-permute-start(bf16[2,128,512]{2,1,0:T(8,128)(2,1)S(1)} %get-tuple-element.11), channel_id=1, source_target_pairs={{0,64},{16,80},{32,96},{48,112},{64,128},{80,144},{96,160},{112,17... | collective-permute-start | bytes 786440 | tf_op jit(solution)/shard_map/ppermute | solution.py:219
  112.9 1.0 bitcast_dynamic-update-slice_fusion.3
  113.8 0.0 collective-permute-done.5
  113.8 1.0 bitcast_dynamic-update-slice_fusion.2
  114.8 0.0 copy-done.3
  114.8 20.7 %collective-permute-done.6 = bf16[2,128,512]{2,1,0:T(8,128)(2,1)S(1)} collective-permute-done((bf16[2,128,512]{2,1,0:T(8,128)(2,1)S(1)}, bf16[2,128,512]{2,1,0:T(8,128)(2,1)S(1)}, u32[]{:S(2)}, u32[]{:S(2)}) %collective-permute-start.6) | collective-permute-done | bytes 262176 | tf_op jit(solution)/shard_map/ppermute | solution.py:219
  135.5 3.0 %collective-permute-start.7 = (bf16[5,2,128,512]{3,2,1,0:T(8,128)(2,1)S(1)}, bf16[5,2,128,512]{3,2,1,0:T(8,128)(2,1)}, u32[]{:S(2)}, u32[]{:S(2)}) collective-permute-start(bf16[5,2,128,512]{3,2,1,0:T(8,128)(2,1)S(1)} %bitcast_dynamic-update-slice_fusion.own_ref), channel_id=1, source_target_pairs={{0,8},{8,0},{1,9},{9,1},{2,10},{10,2},{3,11},{11,3},{4,12},{12,4},... | collective-permute-start | bytes 3932168 | tf_op jit(solution)/shard_map/ppermute | solution.py:227
  138.5 1.9 %collective-permute-start.2 = (bf16[32,3,8,512]{3,2,1,0:T(8,128)(2,1)S(1)}, bf16[32,3,8,512]{3,2,1,0:T(8,128)(2,1)}, u32[]{:S(2)}, u32[]{:S(2)}) collective-permute-start(bf16[32,3,8,512]{3,2,1,0:T(8,128)(2,1)S(1)} %all-to-all-done.1.w_ref.old_own), channel_id=1, source_target_pairs={{0,8},{8,0},{1,9},{9,1},{2,10},{10,2},{3,11},{11,3},{4,12},{12,4},... | collective-permute-start | bytes 2359304 | tf_op jit(solution)/shard_map/ppermute | solution.py:229
  140.5 0.0 all-to-all-done.3.g_own
  140.5 2.4 %collective-permute-start.1 = (bf16[32,3,8,512]{3,2,1,0:T(8,128)(2,1)S(1)}, bf16[32,3,8,512]{3,2,1,0:T(8,128)(2,1)}, u32[]{:S(2)}, u32[]{:S(2)}) collective-permute-start(bf16[32,3,8,512]{3,2,1,0:T(8,128)(2,1)S(1)} %all-to-all-done.3.g_own), channel_id=1, source_target_pairs={{0,8},{8,0},{1,9},{9,1},{2,10},{10,2},{3,11},{11,3},{4,12},{12,4},... | collective-permute-start | bytes 2359304 | tf_op jit(solution)/shard_map/ppermute | solution.py:230
  143.6 0.1 pad_add_fusion.where_ref
  143.6 0.0 collective-permute-done.7.other_ref
  143.6 2.5 %shard_map.64.att_ref = f32[128,512]{1,0:T(8,128)S(1)} custom-call(s32[2]{0:T(128)S(1)} %pad_add_fusion.where_ref, bf16[128,512]{1,0:T(8,128)(2,1)S(1)} %get-tuple-element.10.q_ref, bf16[5,2,128,512]{3,2,1,0:T(8,128)(2,1)S(1)} %bitcast_dynamic-update-slice_fusion.own_ref, bf16[5,2,128,512]{3,2,1,0:T(8,128)(2,1)} %collective-permute-done.7.other_ref), custom_call_target="tpu_custom_call" | custom-call | tf_op jit(solution)/shard_map/pallas_call | solution.py:44
  146.2 0.0 collective-permute-done.2.old_other
  146.2 0.0 collective-permute-done.1.g_other
  146.2 8.0 %shard_map.65 = (f32[3,8,512]{2,1,0:T(8,128)}, bf16[128,512]{1,0:T(8,128)(2,1)S(1)}) custom-call(s32[2]{0:T(128)S(1)} %pad_add_fusion.where_ref, f32[1]{0:T(128)S(6)} %copy.12.rate_ref, bf16[32,3,8,512]{3,2,1,0:T(8,128)(2,1)S(1)} %all-to-all-done.3.g_own, bf16[32,3,8,512]{3,2,1,0:T(8,128)(2,1)} %collective-permute-done.1.g_other, ...), custom_call_target="tpu_custom_call" | custom-call | tf_op jit(solution)/shard_map/pallas_call | solution.py:44
  154.2 10.4 %all_to_all.25.arr_ref = bf16[8,16,512]{2,1,0:T(8,128)(2,1)S(1)} all-to-all(bf16[8,16,512]{2,1,0:T(8,128)(2,1)S(1)} %bitcast.19), channel_id=1, replica_groups=mesh['z'=8,'y'=4,'core'=2,'head'=8] {'head'}, dimensions={0} | all-to-all | bytes 262144 | tf_op jit(solution)/shard_map/all_to_all | solution.py:200
  164.5 0.7 shard_map.66
  (5 shorter events, 0.1 us)
Async XLA Ops:
  0.6 1.0 copy-start
  1.6 6.7 %copy-start.1 = (f32[3,1,8,512]{3,2,1,0:T(8,128)S(1)}, f32[3,1,8,512]{3,2,1,0:T(8,128)}, u32[]{:S(2)}) copy-start(f32[3,1,8,512]{3,2,1,0:T(8,128)} %param.7) | copy-start | bytes 147460
  2.4 12.5 %all-to-all-start = ((bf16[8,3,16,512]{3,2,1,0:T(8,128)(2,1)}), bf16[8,3,16,512]{3,2,1,0:T(8,128)(2,1)S(1)}, u32[]{:S(2)}, u32[]{:S(2)}) async-start(bf16[8,3,16,512]{3,2,1,0:T(8,128)(2,1)} %shard_map.59), calls=%async_computation | async-start | bytes 786432 | tf_op jit(solution)/shard_map/all_to_all | solution.py:200
  8.3 21.7 %copy-start.5 = (f32[128,1]{0,1:T(1,128)S(1)}, f32[128,1]{0,1:T(1,128)}, u32[]{:S(2)}) copy-start(f32[128,1]{0,1:T(1,128)} %param.5) | copy-start | bytes 1540
  14.9 34.8 %all-to-all-start.1 = ((bf16[32,3,8,512]{3,2,1,0:T(8,128)(2,1)}), bf16[32,3,8,512]{3,2,1,0:T(8,128)(2,1)S(1)}, u32[]{:S(2)}, u32[]{:S(2)}) async-start(bf16[32,3,8,512]{3,2,1,0:T(8,128)(2,1)} %shard_map.61), calls=%async_computation.1 | async-start | bytes 1572864 | tf_op jit(solution)/shard_map/all_to_all | solution.py:200
  30.2 5.9 %collective-permute-start = (bf16[2,128,512]{2,1,0:T(8,128)(2,1)S(1)}, bf16[2,128,512]{2,1,0:T(8,128)(2,1)S(1)}, u32[]{:S(2)}, u32[]{:S(2)}) collective-permute-start(bf16[2,128,512]{2,1,0:T(8,128)(2,1)S(1)} %get-tuple-element.8.own_ref), channel_id=1, source_target_pairs={{0,8},{8,0},{1,9},{9,1},{2,10},{10,2},{3,11},{11,3},{4,12},{12,4},... | collective-permute-start | bytes 786440 | tf_op jit(solution)/shard_map/ppermute | solution.py:216
  51.4 50.0 %all-to-all-start.2 = ((bf16[32,3,8,512]{3,2,1,0:T(8,128)(2,1)}), bf16[32,3,8,512]{3,2,1,0:T(8,128)(2,1)S(1)}, u32[]{:S(2)}, u32[]{:S(2)}) async-start(bf16[32,3,8,512]{3,2,1,0:T(8,128)(2,1)} %shard_map.62), calls=%async_computation.2 | async-start | bytes 1572864 | tf_op jit(solution)/shard_map/all_to_all | solution.py:200
  61.7 28.6 %collective-permute-start.3 = (bf16[2,128,512]{2,1,0:T(8,128)(2,1)S(1)}, bf16[2,128,512]{2,1,0:T(8,128)(2,1)S(1)}, u32[]{:S(2)}, u32[]{:S(2)}) collective-permute-start(bf16[2,128,512]{2,1,0:T(8,128)(2,1)S(1)} %get-tuple-element.11), channel_id=1, source_target_pairs={{0,16},{16,32},{32,48},{48,64},{64,80},{80,96},{96,112},{112,128},... | collective-permute-start | bytes 786440 | tf_op jit(solution)/shard_map/ppermute | solution.py:217
  65.7 30.3 %collective-permute-start.4 = (bf16[2,128,512]{2,1,0:T(8,128)(2,1)S(1)}, bf16[2,128,512]{2,1,0:T(8,128)(2,1)S(1)}, u32[]{:S(2)}, u32[]{:S(2)}) collective-permute-start(bf16[2,128,512]{2,1,0:T(8,128)(2,1)S(1)} %get-tuple-element.11), channel_id=1, source_target_pairs={{0,48},{16,64},{32,80},{48,96},{64,112},{80,128},{96,144},{112,160... | collective-permute-start | bytes 786440 | tf_op jit(solution)/shard_map/ppermute | solution.py:218
  90.3 12.1 %copy-start.4 = (bf16[2,128,512]{2,1,0:T(8,128)(2,1)}, bf16[2,128,512]{2,1,0:T(8,128)(2,1)S(1)}, u32[]{:S(2)}) copy-start(bf16[2,128,512]{2,1,0:T(8,128)(2,1)S(1)} %collective-permute-done.3) | copy-start | bytes 786436
  96.0 6.3 %copy-start.2 = (bf16[2,128,512]{2,1,0:T(8,128)(2,1)}, bf16[2,128,512]{2,1,0:T(8,128)(2,1)S(1)}, u32[]{:S(2)}) copy-start(bf16[2,128,512]{2,1,0:T(8,128)(2,1)S(1)} %collective-permute-done.4) | copy-start | bytes 786436
  96.8 17.0 %collective-permute-start.5 = (bf16[2,128,512]{2,1,0:T(8,128)(2,1)}, bf16[2,128,512]{2,1,0:T(8,128)(2,1)}, u32[]{:S(2)}, u32[]{:S(2)}) collective-permute-start(bf16[2,128,512]{2,1,0:T(8,128)(2,1)} %broadcast_select_fusion), channel_id=1, source_target_pairs={{0,16},{16,32},{32,48},{48,64},{64,80},{80,96},{96,112},{112,128},... | collective-permute-start | bytes 786440 | tf_op jit(solution)/shard_map/ppermute | solution.py:221
  102.4 38.1 %all-to-all-start.3 = ((bf16[32,3,8,512]{3,2,1,0:T(8,128)(2,1)}), bf16[32,3,8,512]{3,2,1,0:T(8,128)(2,1)S(1)}, u32[]{:S(2)}, u32[]{:S(2)}) async-start(bf16[32,3,8,512]{3,2,1,0:T(8,128)(2,1)} %shard_map.63), calls=%async_computation.3 | async-start | bytes 1572864 | tf_op jit(solution)/shard_map/all_to_all | solution.py:200
  109.5 5.3 %copy-start.3 = (bf16[2,128,512]{2,1,0:T(8,128)(2,1)S(1)}, bf16[2,128,512]{2,1,0:T(8,128)(2,1)}, u32[]{:S(2)}) copy-start(bf16[2,128,512]{2,1,0:T(8,128)(2,1)} %copy-done.2) | copy-start | bytes 786436
  109.6 25.9 %collective-permute-start.6 = (bf16[2,128,512]{2,1,0:T(8,128)(2,1)S(1)}, bf16[2,128,512]{2,1,0:T(8,128)(2,1)S(1)}, u32[]{:S(2)}, u32[]{:S(2)}) collective-permute-start(bf16[2,128,512]{2,1,0:T(8,128)(2,1)S(1)} %get-tuple-element.11), channel_id=1, source_target_pairs={{0,64},{16,80},{32,96},{48,112},{64,128},{80,144},{96,160},{112,17... | collective-permute-start | bytes 786440 | tf_op jit(solution)/shard_map/ppermute | solution.py:219
  135.5 8.1 %collective-permute-start.7 = (bf16[5,2,128,512]{3,2,1,0:T(8,128)(2,1)S(1)}, bf16[5,2,128,512]{3,2,1,0:T(8,128)(2,1)}, u32[]{:S(2)}, u32[]{:S(2)}) collective-permute-start(bf16[5,2,128,512]{3,2,1,0:T(8,128)(2,1)S(1)} %bitcast_dynamic-update-slice_fusion.own_ref), channel_id=1, source_target_pairs={{0,8},{8,0},{1,9},{9,1},{2,10},{10,2},{3,11},{11,3},{4,12},{12,4},... | collective-permute-start | bytes 3932168 | tf_op jit(solution)/shard_map/ppermute | solution.py:227
  138.5 7.6 %collective-permute-start.2 = (bf16[32,3,8,512]{3,2,1,0:T(8,128)(2,1)S(1)}, bf16[32,3,8,512]{3,2,1,0:T(8,128)(2,1)}, u32[]{:S(2)}, u32[]{:S(2)}) collective-permute-start(bf16[32,3,8,512]{3,2,1,0:T(8,128)(2,1)S(1)} %all-to-all-done.1.w_ref.old_own), channel_id=1, source_target_pairs={{0,8},{8,0},{1,9},{9,1},{2,10},{10,2},{3,11},{11,3},{4,12},{12,4},... | collective-permute-start | bytes 2359304 | tf_op jit(solution)/shard_map/ppermute | solution.py:229
  140.5 5.7 %collective-permute-start.1 = (bf16[32,3,8,512]{3,2,1,0:T(8,128)(2,1)S(1)}, bf16[32,3,8,512]{3,2,1,0:T(8,128)(2,1)}, u32[]{:S(2)}, u32[]{:S(2)}) collective-permute-start(bf16[32,3,8,512]{3,2,1,0:T(8,128)(2,1)S(1)} %all-to-all-done.3.g_own), channel_id=1, source_target_pairs={{0,8},{8,0},{1,9},{9,1},{2,10},{10,2},{3,11},{11,3},{4,12},{12,4},... | collective-permute-start | bytes 2359304 | tf_op jit(solution)/shard_map/ppermute | solution.py:230

commit v4 on v3

--- a/solution.py
+++ b/solution.py
@@ -16,6 +16,8 @@
 SEQ_HEAD = ("z", "y", "core", "head")
 CHIPS = ("z", "y")
 F32, BF16 = jnp.float32, jnp.bfloat16
+CHIPS_Z, CHIPS_Y = 8, 4
+RATE_ROWS = 8
 KERNEL_VMEM = 20 * 1024 * 1024
 
 
@@ -62,17 +64,28 @@
     return x * lax.rsqrt(jnp.mean(x * x, axis=-1, keepdims=True) + RMS_EPS)
 
 
-def prepare(arr_ref, rate_ref, q_ref, kv_ref, qn_ref, ks_ref):
+def prepare(arr_ref, rate_ref, q_ref, qn_ref, sent_ref):
     n, _, t, _ = arr_ref.shape
+    copies, lines, w = sent_ref.shape
+    tok = n * t
+    rate = rate_ref[...]
+    high = rate.astype(BF16).astype(F32)
+    middle = (rate - high).astype(BF16).astype(F32)
+    low = rate - high - middle
+    spare = jnp.zeros((1, w - 3 * tok), F32)
+    rate_rows = jnp.broadcast_to(
+        jnp.concatenate([high, middle, low, spare], axis=1), (lines - 2 * tok, w)
+    ).astype(BF16)
     for j in range(n):
         rows = slice(j * t, (j + 1) * t)
-        q, k, v = arr_ref[j, 0], arr_ref[j, 1], arr_ref[j, 2]
+        q = arr_ref[j, 0]
         q_ref[rows] = q
-        kv_ref[0, rows] = k
-        kv_ref[1, rows] = v
         qn_ref[rows] = rms_scaled(q.astype(F32)).astype(BF16)
-        ks_ref[0, rows] = rms_scaled(k.astype(F32)).astype(BF16)
-        ks_ref[1, rows] = (-rate_ref[rows] * v.astype(F32)).astype(BF16)
+    for d in range(copies):
+        for j in range(n):
+            sent_ref[d, j * t : (j + 1) * t] = arr_ref[j, 1]
+            sent_ref[d, tok + j * t : tok + (j + 1) * t] = arr_ref[j, 2]
+        sent_ref[d, 2 * tok :] = rate_rows
 
 
 def copies_of(rows_ref, out_ref):
@@ -88,20 +101,34 @@
 
 def gradient(own_ref, other_ref, w_ref, out_ref):
     n, _, r, w = w_ref.shape
-    key_norm = jnp.concatenate([own_ref[0], other_ref[0]], axis=0)
-    signal = jnp.concatenate([own_ref[1], other_ref[1]], axis=0)
-    gate = dot_nt(merged_rows(w_ref, 0).astype(BF16), key_norm)
-    up = dot_nt(merged_rows(w_ref, 1).astype(BF16), key_norm)
-    back = dot_nt(merged_rows(w_ref, 2).astype(BF16), signal)
-    s = jax.nn.sigmoid(gate)
-    silu = gate * s
-    grads = (
-        ((back * up * s * (1.0 + gate * (1.0 - s))).astype(BF16), key_norm),
-        ((back * silu).astype(BF16), key_norm),
-        ((silu * up).astype(BF16), signal),
-    )
-    for m, (left, right) in enumerate(grads):
-        out_ref[:, m] = dot_nn(left, right).reshape(n, r, w).astype(BF16)
+    weights = [merged_rows(w_ref, m).astype(BF16) for m in range(3)]
+    chips, lines, _ = own_ref.shape
+    tok = (lines - RATE_ROWS) // 2
+    sums = [None, None, None]
+    for ref in (own_ref, other_ref):
+        keys = ref[:, :tok].reshape(chips * tok, w)
+        values = ref[:, tok : 2 * tok].reshape(chips * tok, w)
+        rates = []
+        for i in range(chips):
+            parts = ref[i, 2 * tok :].astype(F32)[:1]
+            rates.append(parts[:, :tok] + parts[:, tok : 2 * tok] + parts[:, 2 * tok : 3 * tok])
+        minus_rate = -jnp.concatenate(rates, axis=1)
+        key_norm = rms_scaled(keys.astype(F32)).astype(BF16)
+        gate = dot_nt(weights[0], key_norm)
+        up = dot_nt(weights[1], key_norm)
+        back = dot_nt(weights[2], values) * minus_rate
+        s = jax.nn.sigmoid(gate)
+        silu = gate * s
+        lefts = (
+            (back * up * s * (1.0 + gate * (1.0 - s)), key_norm),
+            (back * silu, key_norm),
+            (silu * up * minus_rate, values),
+        )
+        for m, (left, right) in enumerate(lefts):
+            part = dot_nn(left.astype(BF16), right)
+            sums[m] = part if sums[m] is None else sums[m] + part
+    for m in range(3):
+        out_ref[:, m] = sums[m].reshape(n, r, w).astype(BF16)
 
 
 def sum_and_copy(arr_ref, out_ref):
@@ -113,32 +140,42 @@
         out_ref[d] = total
 
 
-def attend(where_ref, q_ref, own_ref, other_ref, out_ref):
-    blocks, _, t, w = own_ref.shape
-    chip, core = where_ref[0], where_ref[1]
+def arrange(where_ref, *refs):
+    pieces, out_ref = refs[:-1], refs[-1]
+    planes = pieces[0].shape[0]
+    for d, piece in enumerate(pieces):
+        for z in range(planes):
+            out_ref[z * len(pieces) + (where_ref[1] ^ d)] = piece[z]
+
+
+def attend(where_ref, q_ref, own_ref, other_ref, own_before_ref, other_before_ref, out_ref):
     q = q_ref[...]
-    q_pos = (2 * chip + core) * t + lax.broadcasted_iota(jnp.int32, (t, t), 0)
-    lane = lax.broadcasted_iota(jnp.int32, (t, t), 1)
+    t, w = q.shape
+    chips = own_ref.shape[0]
+    z, y, core = where_ref[0], where_ref[1], where_ref[2]
+    plane = 2 * chips * t
+    q_pos = z * plane + (2 * y + core) * t + lax.broadcasted_iota(jnp.int32, (t, chips * t), 0)
+    lane = lax.broadcasted_iota(jnp.int32, (t, chips * t), 1)
+    lane = lane + lane // t * t
+    sides = (
+        (own_ref, z, core),
+        (other_ref, z, 1 - core),
+        (own_before_ref, z - 1, core),
+        (other_before_ref, z - 1, 1 - core),
+    )
     parts = []
-    for b in range(blocks):
-        for ref, c in ((own_ref, core), (other_ref, 1 - core)):
-            k_pos = (2 * (chip - b) + c) * t + lane
-            seen = (k_pos <= q_pos) & (k_pos > q_pos - WINDOW) & (k_pos >= 0)
-            scores = dot_nt(q, ref[b, 0]) * (w ** (-0.5))
-            parts.append(jnp.where(seen, scores, -jnp.inf))
-    top = parts[0]
-    for p in parts[1:]:
-        top = jnp.maximum(top, p)
+    for ref, k_plane, k_core in sides:
+        k_pos = k_plane * plane + k_core * t + lane
+        seen = (k_pos <= q_pos) & (k_pos > q_pos - WINDOW) & (k_pos >= 0)
+        scores = dot_nt(q, ref[:, :t].reshape(chips * t, w)) * (w ** (-0.5))
+        parts.append(jnp.where(seen, scores, -jnp.inf))
+    top = jnp.maximum(jnp.maximum(parts[0], parts[1]), jnp.maximum(parts[2], parts[3]))
     top = jnp.max(top, axis=1, keepdims=True)
     parts = [jnp.exp(p - top) for p in parts]
-    total = parts[0]
-    for p in parts[1:]:
-        total = total + p
-    inverse = 1.0 / jnp.sum(total, axis=1, keepdims=True)
+    inverse = 1.0 / jnp.sum(parts[0] + parts[1] + parts[2] + parts[3], axis=1, keepdims=True)
     out = jnp.zeros((t, w), F32)
-    for b in range(blocks):
-        for i, ref in enumerate((own_ref, other_ref)):
-            out = out + dot_nn((parts[2 * b + i] * inverse).astype(BF16), ref[b, 1])
+    for p, (ref, _, _) in zip(parts, sides):
+        out = out + dot_nn((p * inverse).astype(BF16), ref[:, t : 2 * t].reshape(chips * t, w))
     out_ref[...] = out
 
 
@@ -149,7 +186,7 @@
     n, _, r, _ = g_own.shape
     half = n * r
     rate = rate_ref[0]
-    chip = where_ref[0]
+    chip = where_ref[0] * CHIPS_Y + where_ref[1]
 
     xs = []
     for m in range(3):
@@ -182,14 +219,12 @@
 
 def shards(qkv, token_rate, head_rate, fast_state):
     heads = lax.axis_size("head")
-    chips = lax.axis_size("z") * lax.axis_size("y")
+    chips = CHIPS_Z * CHIPS_Y
     _, tok_part, width = qkv.shape
     hd = width // heads
     tok = tok_part * heads
     rows = fast_state.shape[2]
-    chip = lax.axis_index(CHIPS)
-    core = lax.axis_index("core")
-    where = jnp.stack([chip, core]).astype(jnp.int32)
+    where = jnp.stack([lax.axis_index(a) for a in SEQ]).astype(jnp.int32)
     state = fast_state[:, 0]
     swap = [(0, 1), (1, 0)]
 
@@ -199,33 +234,40 @@
     def exchanged(pieces, axis):
         return lax.all_to_all(pieces, axis, 0, 0, tiled=True)
 
-    def behind(distance):
-        return [(i, (i + distance) % chips) for i in range(chips)]
-
-    old_copies = local_call(copies_of, shape((chips, 3, rows, hd)), (state,), hbm_out=(0,))
     split = local_call(
         split_heads, shape((heads, 3, tok_part, hd)), (qkv,), hbm_in=(0,), hbm_out=(0,)
     )
-    old_own = exchanged(old_copies, CHIPS)
     arrived = exchanged(split, "head")
-    q, kv, q_norm, ks = local_call(
+    old_copies = local_call(copies_of, shape((CHIPS_Z, 3, rows, hd)), (state,), hbm_out=(0,))
+    old_slice = exchanged(old_copies, "z")
+    q, q_norm, sent = local_call(
         prepare,
-        [shape((tok, hd)), shape((2, tok, hd)), shape((tok, hd)), shape((2, tok, hd))],
-        (arrived, token_rate),
-    )
-    ks_other = lax.ppermute(ks, "core", swap)
-    one = lax.ppermute(kv, CHIPS, behind(1))
-    three = lax.ppermute(kv, CHIPS, behind(3))
-    four = lax.ppermute(kv, CHIPS, behind(4))
-    relay = [(2 * i, 2 * j) for i, j in behind(1)] + [(2 * j + 1, 2 * i + 1) for i, j in behind(1)]
-    two = lax.ppermute(jnp.where(core == 0, one, three), SEQ, relay)
-    own_kv = jnp.stack([kv, one, two, three, four])
-    partial = local_call(gradient, shape((chips, 3, rows, hd)), (ks, ks_other, old_own), hbm_out=(0,))
-    parts = exchanged(partial, CHIPS)
+        [shape((tok, hd)), shape((tok, hd)), shape((CHIPS_Y, 2 * tok + RATE_ROWS, hd))],
+        (arrived, token_rate.reshape(1, tok)),
+        hbm_out=(2,),
+    )
+    kv_own = exchanged(sent, "y")
+    kv_other = lax.ppermute(kv_own, "core", swap)
+    partial = local_call(
+        gradient, shape((CHIPS_Z, 3, rows, hd)), (kv_own, kv_other, old_slice), hbm_out=(0,)
+    )
+    parts = exchanged(partial, "z")
     g_copies = local_call(sum_and_copy, shape((chips, 3, rows, hd)), (parts,), hbm_out=(0,))
     g_own = exchanged(g_copies, CHIPS)
-    other_kv = lax.ppermute(own_kv, "core", swap)
-    attention = local_call(attend, shape((tok, hd), F32), (where, q, own_kv, other_kv), smem=(0,))
+    ring = [(i, (i + 1) % CHIPS_Z) for i in range(CHIPS_Z)]
+    kv_own_before = lax.ppermute(kv_own, "z", ring)
+    kv_other_before = lax.ppermute(kv_own_before, "core", swap)
+    attention = local_call(
+        attend,
+        shape((tok, hd), F32),
+        (where, q, kv_own, kv_other, kv_own_before, kv_other_before),
+        smem=(0,),
+    )
+    olds = [old_slice] + [
+        lax.ppermute(old_slice, "y", [(i, i ^ d) for i in range(CHIPS_Y)])
+        for d in range(1, CHIPS_Y)
+    ]
+    old_own = local_call(arrange, shape((chips, 3, rows, hd)), (where, *olds), smem=(0,))
     old_other = lax.ppermute(old_own, "core", swap)
     g_other = lax.ppermute(g_own, "core", swap)
     new_rows, combined = local_call(
@@ -247,7 +289,7 @@
 
 
 def solution(mesh):
-    finer = Mesh(mesh.devices.reshape(8, 4, 2, mesh.shape["head"]), SEQ_HEAD)
+    finer = Mesh(mesh.devices.reshape(CHIPS_Z, CHIPS_Y, 2, mesh.shape["head"]), SEQ_HEAD)
     return jax.shard_map(
         shards,
         mesh=finer,

time: 166 us -> 195 us (1.17)
  the two profiles are of different devices: /device:TPU:1 before, /device:TPU:56 now
where the time goes in v4:
time: 195 us; the launch traced here: 194 us
  blocking collectives  91.1 us (47%)
  waiting for transfers between devices  53 us (27%)
  starting transfers between devices  30.8 us (16%)
  Pallas kernels  16.6 us (9%)
    all_to_all x5, blocking collectives, exchanged(): return lax.all_to_all(pieces, axis, 0, 0, tiled=True)  91.1 us
    ppermute x1, waiting for transfers between devices, shards(): kv_own_before = lax.ppermute(kv_own, 'z', ring)  38.9 us
    pallas_call x9, Pallas kernels, local_call(): pl.pallas_call(body, in_specs=specs, out_specs=out_specs[0] if single els...  16.6 us
    ppermute x3, waiting for transfers between devices, shards(): lax.ppermute(old_slice, 'y', [(i, i ^ d) for i in range(CHIPS_Y)])  14.1 us
    ppermute x3, starting transfers between devices, shards(): lax.ppermute(old_slice, 'y', [(i, i ^ d) for i in range(CHIPS_Y)])  12.2 us
    all_to_all x1, starting transfers between devices, exchanged(): return lax.all_to_all(pieces, axis, 0, 0, tiled=True)  7.06 us
  transfers between devices with their start and end apart: 9, of which 3 were waited for; matrix products, arithmetic and copies ran while one was open for 0% of the time, Pallas kernels for 3%

profile of v4, /device:TPU:56, one launch (start us, length us, event | category | flops | bytes accessed | tf_op | source)
XLA Modules:
  0.0 194.0 jit_solution(12120366719642859993)
XLA Ops:
  0.6 0.0 copy-start
  0.6 1.0 copy-done
  1.6 0.0 copy-start.4
  1.7 12.9 %all_to_all.30.arr_ref = bf16[8,3,16,512]{3,2,1,0:T(8,128)(2,1)S(1)} all-to-all(bf16[8,3,16,512]{3,2,1,0:T(8,128)(2,1)S(1)} %shard_map.59), channel_id=1, replica_groups=mesh['z'=8,'y'=4,'core'=2,'head'=8] {'head'}, dimensions={0} | all-to-all | bytes 786432 | tf_op jit(solution)/shard_map/all_to_all | solution.py:235
  14.6 0.0 copy-done.4
  14.6 0.1 shard_map.60
  14.7 0.0 copy-start.2
  14.7 0.0 copy-start.1
  14.7 31.2 %all_to_all.31.own_ref = bf16[4,264,512]{2,1,0:T(8,128)(2,1)S(1)} all-to-all(bf16[4,264,512]{2,1,0:T(8,128)(2,1)S(1)} %get-tuple-element.7), channel_id=1, replica_groups=mesh['z'=8,'y'=4,'core'=2,'head'=8] {'y'}, dimensions={0} | all-to-all | bytes 2162688 | tf_op jit(solution)/shard_map/all_to_all | solution.py:235
  45.9 0.0 copy-done.2
  45.9 1.9 collective-permute-start
  47.8 0.0 copy-done.1
  47.8 21.2 %all_to_all.32.w_ref.refs_0_ = bf16[8,3,8,512]{3,2,1,0:T(8,128)(2,1)S(1)} all-to-all(bf16[8,3,8,512]{3,2,1,0:T(8,128)(2,1)S(1)} %shard_map.61), channel_id=1, replica_groups=mesh['z'=8,'y'=4,'core'=2,'head'=8] {'z'}, dimensions={0} | all-to-all | bytes 393216 | tf_op jit(solution)/shard_map/all_to_all | solution.py:235
  69.1 0.0 collective-permute-done.other_ref
  69.1 1.7 shard_map.62
  70.8 13.2 %all_to_all.33.arr_ref = bf16[8,3,8,512]{3,2,1,0:T(8,128)(2,1)S(1)} all-to-all(bf16[8,3,8,512]{3,2,1,0:T(8,128)(2,1)S(1)} %shard_map.62), channel_id=1, replica_groups=mesh['z'=8,'y'=4,'core'=2,'head'=8] {'z'}, dimensions={0} | all-to-all | bytes 393216 | tf_op jit(solution)/shard_map/all_to_all | solution.py:235
  84.0 0.9 shard_map.63
  84.9 7.1 %all-to-all-start.4 = ((bf16[32,3,8,512]{3,2,1,0:T(8,128)(2,1)}), bf16[32,3,8,512]{3,2,1,0:T(8,128)(2,1)S(1)}, u32[]{:S(2)}, u32[]{:S(2)}) async-start(bf16[32,3,8,512]{3,2,1,0:T(8,128)(2,1)} %shard_map.63), calls=%async_computation.4 | async-start | bytes 1572864 | tf_op jit(solution)/shard_map/all_to_all | solution.py:235
  92.0 3.4 %collective-permute-start.6 = (bf16[4,264,512]{2,1,0:T(8,128)(2,1)S(1)}, bf16[4,264,512]{2,1,0:T(8,128)(2,1)}, u32[]{:S(2)}, u32[]{:S(2)}) collective-permute-start(bf16[4,264,512]{2,1,0:T(8,128)(2,1)S(1)} %all_to_all.31.own_ref), channel_id=1, source_target_pairs={{0,64},{64,128},{128,192},{192,256},{256,320},{320,384},{384,448},... | collective-permute-start | bytes 3244040 | tf_op jit(solution)/shard_map/ppermute | solution.py:258
  95.4 38.9 %collective-permute-done.6.own_before_ref = bf16[4,264,512]{2,1,0:T(8,128)(2,1)} collective-permute-done((bf16[4,264,512]{2,1,0:T(8,128)(2,1)S(1)}, bf16[4,264,512]{2,1,0:T(8,128)(2,1)}, u32[]{:S(2)}, u32[]{:S(2)}) %collective-permute-start.6) | collective-permute-done | bytes 1081376 | tf_op jit(solution)/shard_map/ppermute | solution.py:258
  134.3 1.9 collective-permute-start.7
  136.2 4.2 %collective-permute-start.2 = (bf16[8,3,8,512]{3,2,1,0:T(8,128)(2,1)S(1)}, bf16[8,3,8,512]{3,2,1,0:T(8,128)(2,1)S(1)}, u32[]{:S(2)}, u32[]{:S(2)}) collective-permute-start(bf16[8,3,8,512]{3,2,1,0:T(8,128)(2,1)S(1)} %all_to_all.32.w_ref.refs_0_), channel_id=1, source_target_pairs={{0,16},{16,0},{32,48},{48,32},{1,17},{17,1},{33,49},{49,33},{2,18}... | collective-permute-start | bytes 589832 | tf_op jit(solution)/shard_map/ppermute | solution.py:267
  140.4 2.8 %collective-permute-start.3 = (bf16[8,3,8,512]{3,2,1,0:T(8,128)(2,1)S(1)}, bf16[8,3,8,512]{3,2,1,0:T(8,128)(2,1)}, u32[]{:S(2)}, u32[]{:S(2)}) collective-permute-start(bf16[8,3,8,512]{3,2,1,0:T(8,128)(2,1)S(1)} %all_to_all.32.w_ref.refs_0_), channel_id=1, source_target_pairs={{0,32},{16,48},{32,0},{48,16},{1,33},{17,49},{33,1},{49,17},{2,34}... | collective-permute-start | bytes 589832 | tf_op jit(solution)/shard_map/ppermute | solution.py:267
  143.2 5.3 %collective-permute-start.4 = (bf16[8,3,8,512]{3,2,1,0:T(8,128)(2,1)S(1)}, bf16[8,3,8,512]{3,2,1,0:T(8,128)(2,1)}, u32[]{:S(2)}, u32[]{:S(2)}) collective-permute-start(bf16[8,3,8,512]{3,2,1,0:T(8,128)(2,1)S(1)} %all_to_all.32.w_ref.refs_0_), channel_id=1, source_target_pairs={{0,48},{16,32},{32,16},{48,0},{1,49},{17,33},{33,17},{49,1},{2,50}... | collective-permute-start | bytes 589832 | tf_op jit(solution)/shard_map/ppermute | solution.py:267
  148.5 0.1 pad_add_fusion.where_ref
  148.6 10.1 %collective-permute-done.2.refs_1_ = bf16[8,3,8,512]{3,2,1,0:T(8,128)(2,1)S(1)} collective-permute-done((bf16[8,3,8,512]{3,2,1,0:T(8,128)(2,1)S(1)}, bf16[8,3,8,512]{3,2,1,0:T(8,128)(2,1)S(1)}, u32[]{:S(2)}, u32[]{:S(2)}) %collective-permute-start.2) | collective-permute-done | bytes 196640 | tf_op jit(solution)/shard_map/ppermute | solution.py:267
  158.7 0.0 collective-permute-done.3.refs_2_
  158.7 3.9 %collective-permute-done.4.refs_3_ = bf16[8,3,8,512]{3,2,1,0:T(8,128)(2,1)} collective-permute-done((bf16[8,3,8,512]{3,2,1,0:T(8,128)(2,1)S(1)}, bf16[8,3,8,512]{3,2,1,0:T(8,128)(2,1)}, u32[]{:S(2)}, u32[]{:S(2)}) %collective-permute-start.4) | collective-permute-done | bytes 196640 | tf_op jit(solution)/shard_map/ppermute | solution.py:267
  162.6 2.0 %shard_map.64.old_own = bf16[32,3,8,512]{3,2,1,0:T(8,128)(2,1)} custom-call(s32[3]{0:T(128)S(1)} %pad_add_fusion.where_ref, bf16[8,3,8,512]{3,2,1,0:T(8,128)(2,1)S(1)} %all_to_all.32.w_ref.refs_0_, bf16[8,3,8,512]{3,2,1,0:T(8,128)(2,1)S(1)} %collective-permute-done.2.refs_1_, bf16[8,3,8,512]{3,2,1,0:T(8,128)(2,1)} %collective-permute-done.3.refs_2_, ...), custom_call_target="tpu_custom_call" | custom-call | tf_op jit(solution)/shard_map/pallas_call | solution.py:46
  164.6 1.9 collective-permute-start.5
  166.5 0.0 all-to-all-done.4.g_own
  166.5 2.4 %collective-permute-start.1 = (bf16[32,3,8,512]{3,2,1,0:T(8,128)(2,1)S(1)}, bf16[32,3,8,512]{3,2,1,0:T(8,128)(2,1)S(1)}, u32[]{:S(2)}, u32[]{:S(2)}) collective-permute-start(bf16[32,3,8,512]{3,2,1,0:T(8,128)(2,1)S(1)} %all-to-all-done.4.g_own), channel_id=1, source_target_pairs={{0,8},{8,0},{1,9},{9,1},{2,10},{10,2},{3,11},{11,3},{4,12},{12,4},... | collective-permute-start | bytes 2359304 | tf_op jit(solution)/shard_map/ppermute | solution.py:272
  169.6 0.0 collective-permute-done.7.other_before_ref
  169.6 0.0 copy-start.3
  169.6 3.2 %shard_map.65.att_ref = f32[128,512]{1,0:T(8,128)S(1)} custom-call(s32[3]{0:T(128)S(1)} %pad_add_fusion.where_ref, bf16[128,512]{1,0:T(8,128)(2,1)S(1)} %get-tuple-element.9.q_ref, bf16[4,264,512]{2,1,0:T(8,128)(2,1)S(1)} %all_to_all.31.own_ref, bf16[4,264,512]{2,1,0:T(8,128)(2,1)S(1)} %collective-permute-done.other_ref, ...), custom_call_target="tpu_custom_call" | custom-call | tf_op jit(solution)/shard_map/pallas_call | solution.py:46
  172.8 0.0 collective-permute-done.5.old_other
  172.8 0.0 collective-permute-done.1.g_other
  172.8 0.0 copy-done.3
  172.8 8.0 %shard_map.66 = (f32[3,8,512]{2,1,0:T(8,128)}, bf16[128,512]{1,0:T(8,128)(2,1)S(1)}) custom-call(s32[3]{0:T(128)S(1)} %pad_add_fusion.where_ref, f32[1]{0:T(128)S(6)} %copy.7.rate_ref, bf16[32,3,8,512]{3,2,1,0:T(8,128)(2,1)S(1)} %all-to-all-done.4.g_own, bf16[32,3,8,512]{3,2,1,0:T(8,128)(2,1)S(1)} %collective-permute-done.1.g_other, ...), custom_call_target="tpu_custom_call" | custom-call | tf_op jit(solution)/shard_map/pallas_call | solution.py:46
  180.8 12.6 %all_to_all.34.arr_ref = bf16[8,16,512]{2,1,0:T(8,128)(2,1)S(1)} all-to-all(bf16[8,16,512]{2,1,0:T(8,128)(2,1)S(1)} %bitcast.11), channel_id=1, replica_groups=mesh['z'=8,'y'=4,'core'=2,'head'=8] {'head'}, dimensions={0} | all-to-all | bytes 262144 | tf_op jit(solution)/shard_map/all_to_all | solution.py:235
  193.4 0.7 shard_map.67
  (2 shorter events, 0.0 us)
Async XLA Ops:
  0.6 1.0 copy-start
  1.6 12.9 %copy-start.4 = (f32[128,1]{0,1:T(1,128)S(1)}, f32[128,1]{0,1:T(1,128)}, u32[]{:S(2)}) copy-start(f32[128,1]{0,1:T(1,128)} %param.5) | copy-start | bytes 1540
  14.7 31.2 %copy-start.2 = (bf16[128,512]{1,0:T(8,128)(2,1)}, bf16[128,512]{1,0:T(8,128)(2,1)S(1)}, u32[]{:S(2)}) copy-start(bf16[128,512]{1,0:T(8,128)(2,1)S(1)} %get-tuple-element.8.qn_ref) | copy-start | bytes 393220
  14.7 33.1 %copy-start.1 = (f32[3,1,8,512]{3,2,1,0:T(8,128)S(1)}, f32[3,1,8,512]{3,2,1,0:T(8,128)}, u32[]{:S(2)}) copy-start(f32[3,1,8,512]{3,2,1,0:T(8,128)} %param.7) | copy-start | bytes 147460
  45.9 23.2 %collective-permute-start = (bf16[4,264,512]{2,1,0:T(8,128)(2,1)S(1)}, bf16[4,264,512]{2,1,0:T(8,128)(2,1)S(1)}, u32[]{:S(2)}, u32[]{:S(2)}) collective-permute-start(bf16[4,264,512]{2,1,0:T(8,128)(2,1)S(1)} %all_to_all.31.own_ref), channel_id=1, source_target_pairs={{0,8},{8,0},{1,9},{9,1},{2,10},{10,2},{3,11},{11,3},{4,12},{12,4},... | collective-permute-start | bytes 3244040 | tf_op jit(solution)/shard_map/ppermute | solution.py:250
  84.9 81.6 %all-to-all-start.4 = ((bf16[32,3,8,512]{3,2,1,0:T(8,128)(2,1)}), bf16[32,3,8,512]{3,2,1,0:T(8,128)(2,1)S(1)}, u32[]{:S(2)}, u32[]{:S(2)}) async-start(bf16[32,3,8,512]{3,2,1,0:T(8,128)(2,1)} %shard_map.63), calls=%async_computation.4 | async-start | bytes 1572864 | tf_op jit(solution)/shard_map/all_to_all | solution.py:235
  92.0 42.3 %collective-permute-start.6 = (bf16[4,264,512]{2,1,0:T(8,128)(2,1)S(1)}, bf16[4,264,512]{2,1,0:T(8,128)(2,1)}, u32[]{:S(2)}, u32[]{:S(2)}) collective-permute-start(bf16[4,264,512]{2,1,0:T(8,128)(2,1)S(1)} %all_to_all.31.own_ref), channel_id=1, source_target_pairs={{0,64},{64,128},{128,192},{192,256},{256,320},{320,384},{384,448},... | collective-permute-start | bytes 3244040 | tf_op jit(solution)/shard_map/ppermute | solution.py:258
  134.3 35.3 %collective-permute-start.7 = (bf16[4,264,512]{2,1,0:T(8,128)(2,1)}, bf16[4,264,512]{2,1,0:T(8,128)(2,1)}, u32[]{:S(2)}, u32[]{:S(2)}) collective-permute-start(bf16[4,264,512]{2,1,0:T(8,128)(2,1)} %collective-permute-done.6.own_before_ref), channel_id=1, source_target_pairs={{0,8},{8,0},{1,9},{9,1},{2,10},{10,2},{3,11},{11,3},{4,12},{12,4},... | collective-permute-start | bytes 3244040 | tf_op jit(solution)/shard_map/ppermute | solution.py:259
  136.2 22.5 %collective-permute-start.2 = (bf16[8,3,8,512]{3,2,1,0:T(8,128)(2,1)S(1)}, bf16[8,3,8,512]{3,2,1,0:T(8,128)(2,1)S(1)}, u32[]{:S(2)}, u32[]{:S(2)}) collective-permute-start(bf16[8,3,8,512]{3,2,1,0:T(8,128)(2,1)S(1)} %all_to_all.32.w_ref.refs_0_), channel_id=1, source_target_pairs={{0,16},{16,0},{32,48},{48,32},{1,17},{17,1},{33,49},{49,33},{2,18}... | collective-permute-start | bytes 589832 | tf_op jit(solution)/shard_map/ppermute | solution.py:267
  140.4 18.3 %collective-permute-start.3 = (bf16[8,3,8,512]{3,2,1,0:T(8,128)(2,1)S(1)}, bf16[8,3,8,512]{3,2,1,0:T(8,128)(2,1)}, u32[]{:S(2)}, u32[]{:S(2)}) collective-permute-start(bf16[8,3,8,512]{3,2,1,0:T(8,128)(2,1)S(1)} %all_to_all.32.w_ref.refs_0_), channel_id=1, source_target_pairs={{0,32},{16,48},{32,0},{48,16},{1,33},{17,49},{33,1},{49,17},{2,34}... | collective-permute-start | bytes 589832 | tf_op jit(solution)/shard_map/ppermute | solution.py:267
  143.2 19.4 %collective-permute-start.4 = (bf16[8,3,8,512]{3,2,1,0:T(8,128)(2,1)S(1)}, bf16[8,3,8,512]{3,2,1,0:T(8,128)(2,1)}, u32[]{:S(2)}, u32[]{:S(2)}) collective-permute-start(bf16[8,3,8,512]{3,2,1,0:T(8,128)(2,1)S(1)} %all_to_all.32.w_ref.refs_0_), channel_id=1, source_target_pairs={{0,48},{16,32},{32,16},{48,0},{1,49},{17,33},{33,17},{49,1},{2,50}... | collective-permute-start | bytes 589832 | tf_op jit(solution)/shard_map/ppermute | solution.py:267
  164.6 8.2 %collective-permute-start.5 = (bf16[32,3,8,512]{3,2,1,0:T(8,128)(2,1)}, bf16[32,3,8,512]{3,2,1,0:T(8,128)(2,1)}, u32[]{:S(2)}, u32[]{:S(2)}) collective-permute-start(bf16[32,3,8,512]{3,2,1,0:T(8,128)(2,1)} %shard_map.64.old_own), channel_id=1, source_target_pairs={{0,8},{8,0},{1,9},{9,1},{2,10},{10,2},{3,11},{11,3},{4,12},{12,4},... | collective-permute-start | bytes 2359304 | tf_op jit(solution)/shard_map/ppermute | solution.py:271
  166.5 6.2 %collective-permute-start.1 = (bf16[32,3,8,512]{3,2,1,0:T(8,128)(2,1)S(1)}, bf16[32,3,8,512]{3,2,1,0:T(8,128)(2,1)S(1)}, u32[]{:S(2)}, u32[]{:S(2)}) collective-permute-start(bf16[32,3,8,512]{3,2,1,0:T(8,128)(2,1)S(1)} %all-to-all-done.4.g_own), channel_id=1, source_target_pairs={{0,8},{8,0},{1,9},{9,1},{2,10},{10,2},{3,11},{11,3},{4,12},{12,4},... | collective-permute-start | bytes 2359304 | tf_op jit(solution)/shard_map/ppermute | solution.py:272
  169.6 3.2 %copy-start.3 = (bf16[128,512]{1,0:T(8,128)(2,1)S(1)}, bf16[128,512]{1,0:T(8,128)(2,1)}, u32[]{:S(2)}) copy-start(bf16[128,512]{1,0:T(8,128)(2,1)} %copy-done.2) | copy-start | bytes 393220

commit v5 on v4

--- a/solution.py
+++ b/solution.py
@@ -36,7 +36,8 @@
     single = not isinstance(outs, (list, tuple))
     out_list = [outs] if single else list(outs)
     out_list = [
-        o if i in hbm_out else pltpu.VMEM(o.shape, o.dtype) for i, o in enumerate(out_list)
+        (pltpu.HBM if i in hbm_out else pltpu.VMEM)(o.shape, o.dtype)
+        for i, o in enumerate(out_list)
     ]
     args = [
         a if i in smem or i in hbm_in else pltpu.with_memory_space_constraint(a, pltpu.VMEM)
@@ -66,7 +67,7 @@
 
 def prepare(arr_ref, rate_ref, q_ref, qn_ref, sent_ref):
     n, _, t, _ = arr_ref.shape
-    copies, lines, w = sent_ref.shape
+    lines, w = sent_ref.shape
     tok = n * t
     rate = rate_ref[...]
     high = rate.astype(BF16).astype(F32)
@@ -81,17 +82,23 @@
         q = arr_ref[j, 0]
         q_ref[rows] = q
         qn_ref[rows] = rms_scaled(q.astype(F32)).astype(BF16)
-    for d in range(copies):
-        for j in range(n):
-            sent_ref[d, j * t : (j + 1) * t] = arr_ref[j, 1]
-            sent_ref[d, tok + j * t : tok + (j + 1) * t] = arr_ref[j, 2]
-        sent_ref[d, 2 * tok :] = rate_rows
-
-
-def copies_of(rows_ref, out_ref):
-    rows = rows_ref[...].astype(BF16)
-    for d in range(out_ref.shape[0]):
-        out_ref[d] = rows
+    for j in range(n):
+        sent_ref[j * t : (j + 1) * t] = arr_ref[j, 1]
+        sent_ref[tok + j * t : tok + (j + 1) * t] = arr_ref[j, 2]
+    sent_ref[2 * tok :] = rate_rows
+
+
+def old_copies(where_ref, near_ref, far_ref, out_ref):
+    for z in range(out_ref.shape[0]):
+        for ref, odd in ((near_ref, 0), (far_ref, 1)):
+            for i in range(2):
+                out_ref[z, where_ref[1] ^ (2 * i + odd)] = ref[i]
+
+
+def in_order(where_ref, *refs):
+    pieces, out_ref = refs[:-1], refs[-1]
+    for d, piece in enumerate(pieces):
+        out_ref[(where_ref[1] + CHIPS_Y - d) % CHIPS_Y] = piece[...]
 
 
 def merged_rows(ref, m):
@@ -99,9 +106,12 @@
     return ref[:, m].astype(F32).reshape(n * r, w)
 
 
-def gradient(own_ref, other_ref, w_ref, out_ref):
-    n, _, r, w = w_ref.shape
-    weights = [merged_rows(w_ref, m).astype(BF16) for m in range(3)]
+def gradient(where_ref, own_ref, other_ref, w_ref, out_ref):
+    n, _, r, w = out_ref.shape
+    weights = []
+    for m in range(3):
+        rows = [w_ref[z * CHIPS_Y + where_ref[1], m].astype(F32) for z in range(n)]
+        weights.append(jnp.concatenate(rows, axis=0).astype(BF16))
     chips, lines, _ = own_ref.shape
     tok = (lines - RATE_ROWS) // 2
     sums = [None, None, None]
@@ -140,14 +150,6 @@
         out_ref[d] = total
 
 
-def arrange(where_ref, *refs):
-    pieces, out_ref = refs[:-1], refs[-1]
-    planes = pieces[0].shape[0]
-    for d, piece in enumerate(pieces):
-        for z in range(planes):
-            out_ref[z * len(pieces) + (where_ref[1] ^ d)] = piece[z]
-
-
 def attend(where_ref, q_ref, own_ref, other_ref, own_before_ref, other_before_ref, out_ref):
     q = q_ref[...]
     t, w = q.shape
@@ -238,36 +240,67 @@
         split_heads, shape((heads, 3, tok_part, hd)), (qkv,), hbm_in=(0,), hbm_out=(0,)
     )
     arrived = exchanged(split, "head")
-    old_copies = local_call(copies_of, shape((CHIPS_Z, 3, rows, hd)), (state,), hbm_out=(0,))
-    old_slice = exchanged(old_copies, "z")
+
+    def across(distance):
+        return [(i, i ^ distance) for i in range(CHIPS_Y)]
+
+    old_one = state.astype(BF16)[None]
+    old_two = jnp.concatenate([old_one, lax.ppermute(old_one, "y", across(2))])
+    old_far = lax.ppermute(old_two, "y", across(1))
+    copies = local_call(
+        old_copies,
+        shape((CHIPS_Z, CHIPS_Y, 3, rows, hd)),
+        (where, old_two, old_far),
+        smem=(0,),
+        hbm_out=(0,),
+    )
+    old_own = exchanged(copies, "z").reshape(chips, 3, rows, hd)
     q, q_norm, sent = local_call(
         prepare,
-        [shape((tok, hd)), shape((tok, hd)), shape((CHIPS_Y, 2 * tok + RATE_ROWS, hd))],
+        [shape((tok, hd)), shape((tok, hd)), shape((2 * tok + RATE_ROWS, hd))],
         (arrived, token_rate.reshape(1, tok)),
-        hbm_out=(2,),
-    )
-    kv_own = exchanged(sent, "y")
+        hbm_out=(0, 1),
+    )
+
+    def behind(distance):
+        return [(i, (i + distance) % CHIPS_Y) for i in range(CHIPS_Y)]
+
+    relay = [(2 * i, 2 * j) for i, j in behind(1)] + [(2 * i + 1, 2 * j + 1) for i, j in behind(3)]
+
+    def of_plane(block):
+        one = lax.ppermute(block, "y", behind(1))
+        three = lax.ppermute(block, "y", behind(3))
+        relayed = jnp.where(lax.axis_index("core") == 0, one, three)
+        two = lax.ppermute(relayed, ("y", "core"), relay)
+        return local_call(
+            in_order,
+            shape((CHIPS_Y, *block.shape)),
+            (where, block, one, two, three),
+            smem=(0,),
+        )
+
+    kv_own = of_plane(sent)
     kv_other = lax.ppermute(kv_own, "core", swap)
     partial = local_call(
-        gradient, shape((CHIPS_Z, 3, rows, hd)), (kv_own, kv_other, old_slice), hbm_out=(0,)
+        gradient,
+        shape((CHIPS_Z, 3, rows, hd)),
+        (where, kv_own, kv_other, old_own),
+        smem=(0,),
+        hbm_out=(0,),
     )
     parts = exchanged(partial, "z")
     g_copies = local_call(sum_and_copy, shape((chips, 3, rows, hd)), (parts,), hbm_out=(0,))
     g_own = exchanged(g_copies, CHIPS)
     ring = [(i, (i + 1) % CHIPS_Z) for i in range(CHIPS_Z)]
-    kv_own_before = lax.ppermute(kv_own, "z", ring)
+    kv_own_before = of_plane(lax.ppermute(sent, "z", ring))
     kv_other_before = lax.ppermute(kv_own_before, "core", swap)
     attention = local_call(
         attend,
         shape((tok, hd), F32),
         (where, q, kv_own, kv_other, kv_own_before, kv_other_before),
         smem=(0,),
-    )
-    olds = [old_slice] + [
-        lax.ppermute(old_slice, "y", [(i, i ^ d) for i in range(CHIPS_Y)])
-        for d in range(1, CHIPS_Y)
-    ]
-    old_own = local_call(arrange, shape((chips, 3, rows, hd)), (where, *olds), smem=(0,))
+        hbm_in=(1,),
+    )
     old_other = lax.ppermute(old_own, "core", swap)
     g_other = lax.ppermute(g_own, "core", swap)
     new_rows, combined = local_call(
@@ -275,6 +308,7 @@
         [shape((3, rows, hd), F32), shape((tok, hd))],
         (where, head_rate, g_own, g_other, old_own, old_other, state, q_norm, attention),
         smem=(0, 1),
+        hbm_in=(6, 7),
         hbm_out=(0, 1),
         scratch=[
             pltpu.VMEM((3, chips * rows, hd), F32),

time: 195 us -> 192 us (0.985)
  the two profiles are of different devices: /device:TPU:56 before, /device:TPU:40 now
where the time goes in v5:
time: 192 us; the launch traced here: 191 us
  waiting for transfers between devices  69.6 us (36%)
  starting transfers between devices  54.7 us (28%)
  blocking collectives  42.7 us (22%)
  Pallas kernels  19.9 us (10%)
  local copies, waits for them, and re-layouts  2.24 us (1%)
    all_to_all x3, blocking collectives, exchanged(): return lax.all_to_all(pieces, axis, 0, 0, tiled=True)  42.7 us
    ppermute x1, waiting for transfers between devices, shards(): kv_own_before = of_plane(lax.ppermute(sent, 'z', ring))  22.2 us
    pallas_call x10, Pallas kernels, local_call(): pl.pallas_call(body, in_specs=specs, out_specs=out_specs[0] if single els...  19.9 us
    ppermute x2, waiting for transfers between devices, of_plane(): two = lax.ppermute(relayed, ('y', 'core'), relay)  17.2 us
    all_to_all x2, starting transfers between devices, exchanged(): return lax.all_to_all(pieces, axis, 0, 0, tiled=True)  15.7 us
    ppermute x2, waiting for transfers between devices, of_plane(): three = lax.ppermute(block, 'y', behind(3))  9.77 us
    ppermute x1, waiting for transfers between devices, shards(): old_two = jnp.concatenate([old_one, lax.ppermute(old_one, 'y', across(2))])  9.64 us
    ppermute x2, starting transfers between devices, of_plane(): three = lax.ppermute(block, 'y', behind(3))  8.05 us
  transfers between devices with their start and end apart: 15, of which 9 were waited for; matrix products, arithmetic and copies ran while one was open for 0% of the time, Pallas kernels for 3%

profile of v5, /device:TPU:40, one launch (start us, length us, event | category | flops | bytes accessed | tf_op | source)
XLA Modules:
  0.0 190.8 jit_solution(14349279722107451476)
XLA Ops:
  0.6 1.0 copy-done.2
  1.6 0.8 shard_map.59
  2.4 13.1 %all_to_all.25.arr_ref = bf16[8,3,16,512]{3,2,1,0:T(8,128)(2,1)S(1)} all-to-all(bf16[8,3,16,512]{3,2,1,0:T(8,128)(2,1)} %shard_map.59), channel_id=1, replica_groups=mesh['z'=8,'y'=4,'core'=2,'head'=8] {'head'}, dimensions={0} | all-to-all | bytes 786432 | tf_op jit(solution)/shard_map/all_to_all | solution.py:237
  15.5 0.0 copy-done.6
  15.5 0.8 shard_map.60
  16.3 2.7 %collective-permute-start = (bf16[264,512]{1,0:T(8,128)(2,1)S(1)}, bf16[264,512]{1,0:T(8,128)(2,1)S(1)}, u32[]{:S(2)}, u32[]{:S(2)}) collective-permute-start(bf16[264,512]{1,0:T(8,128)(2,1)S(1)} %get-tuple-element.7.refs_0_), channel_id=1, source_target_pairs={{0,16},{16,32},{32,48},{48,0},{1,17},{17,33},{33,49},{49,1},{2,18}... | collective-permute-start | bytes 811016 | tf_op jit(solution)/shard_map/ppermute | solution.py:271
  19.0 5.3 %collective-permute-start.1 = (bf16[264,512]{1,0:T(8,128)(2,1)S(1)}, bf16[264,512]{1,0:T(8,128)(2,1)S(1)}, u32[]{:S(2)}, u32[]{:S(2)}) collective-permute-start(bf16[264,512]{1,0:T(8,128)(2,1)S(1)} %get-tuple-element.7.refs_0_), channel_id=1, source_target_pairs={{0,48},{16,0},{32,16},{48,32},{1,49},{17,1},{33,17},{49,33},{2,50}... | collective-permute-start | bytes 811016 | tf_op jit(solution)/shard_map/ppermute | solution.py:272
  24.2 5.6 %collective-permute-start.4 = (bf16[1,3,8,512]{3,2,1,0:T(8,128)(2,1)S(1)}, bf16[1,3,8,512]{3,2,1,0:T(8,128)(2,1)S(1)}, u32[]{:S(2)}, u32[]{:S(2)}) collective-permute-start(bf16[1,3,8,512]{3,2,1,0:T(8,128)(2,1)S(1)} %fusion), channel_id=1, source_target_pairs={{0,32},{16,48},{32,0},{48,16},{1,33},{17,49},{33,1},{49,17},{2,34}... | collective-permute-start | bytes 73736 | tf_op jit(solution)/shard_map/ppermute | solution.py:248
  29.9 9.6 %collective-permute-done.4 = bf16[1,3,8,512]{3,2,1,0:T(8,128)(2,1)S(1)} collective-permute-done((bf16[1,3,8,512]{3,2,1,0:T(8,128)(2,1)S(1)}, bf16[1,3,8,512]{3,2,1,0:T(8,128)(2,1)S(1)}, u32[]{:S(2)}, u32[]{:S(2)}) %collective-permute-start.4) | collective-permute-done | bytes 24608 | tf_op jit(solution)/shard_map/ppermute | solution.py:248
  39.5 1.9 %collective-permute-start.5 = (bf16[2,3,8,512]{3,2,1,0:T(8,128)(2,1)S(1)}, bf16[2,3,8,512]{3,2,1,0:T(8,128)(2,1)S(1)}, u32[]{:S(2)}, u32[]{:S(2)}) collective-permute-start(bf16[2,3,8,512]{3,2,1,0:T(8,128)(2,1)S(1)} %pad_maximum_fusion.near_ref), channel_id=1, source_target_pairs={{0,16},{16,0},{32,48},{48,32},{1,17},{17,1},{33,49},{49,33},{2,18}... | collective-permute-start | bytes 147464 | tf_op jit(solution)/shard_map/ppermute | solution.py:249
  41.4 0.1 pad_add_fusion.where_ref
  41.5 4.9 %collective-permute-done.5.far_ref = bf16[2,3,8,512]{3,2,1,0:T(8,128)(2,1)S(1)} collective-permute-done((bf16[2,3,8,512]{3,2,1,0:T(8,128)(2,1)S(1)}, bf16[2,3,8,512]{3,2,1,0:T(8,128)(2,1)S(1)}, u32[]{:S(2)}, u32[]{:S(2)}) %collective-permute-start.5) | collective-permute-done | bytes 49184 | tf_op jit(solution)/shard_map/ppermute | solution.py:249
  46.4 1.5 shard_map.62
  47.9 8.2 %all-to-all-start.1 = ((bf16[8,4,3,8,512]{4,3,2,1,0:T(8,128)(2,1)}), bf16[8,4,3,8,512]{4,3,2,1,0:T(8,128)(2,1)S(1)}, u32[]{:S(2)}, u32[]{:S(2)}) async-start(bf16[8,4,3,8,512]{4,3,2,1,0:T(8,128)(2,1)} %shard_map.62), calls=%async_computation.1 | async-start | bytes 1572864 | tf_op jit(solution)/shard_map/all_to_all | solution.py:237
  56.1 0.0 collective-permute-done.refs_1_
  56.1 0.0 collective-permute-done.1.refs_3_
  56.2 1.9 %collective-permute-start.2 = (bf16[264,512]{1,0:T(8,128)(2,1)S(1)}, bf16[264,512]{1,0:T(8,128)(2,1)S(1)}, u32[]{:S(2)}, u32[]{:S(2)}) collective-permute-start(bf16[264,512]{1,0:T(8,128)(2,1)S(1)} %broadcast_select_fusion.1), channel_id=1, source_target_pairs={{0,16},{16,32},{32,48},{48,0},{8,56},{24,8},{40,24},{56,40},{1,17}... | collective-permute-start | bytes 811016 | tf_op jit(solution)/shard_map/ppermute | solution.py:274
  58.1 9.1 %collective-permute-done.2.refs_2_ = bf16[264,512]{1,0:T(8,128)(2,1)S(1)} collective-permute-done((bf16[264,512]{1,0:T(8,128)(2,1)S(1)}, bf16[264,512]{1,0:T(8,128)(2,1)S(1)}, u32[]{:S(2)}, u32[]{:S(2)}) %collective-permute-start.2) | collective-permute-done | bytes 270368 | tf_op jit(solution)/shard_map/ppermute | solution.py:274
  67.2 0.6 shard_map.61.own_ref
  67.8 1.9 %collective-permute-start.3 = (bf16[4,264,512]{2,1,0:T(8,128)(2,1)S(1)}, bf16[4,264,512]{2,1,0:T(8,128)(2,1)S(1)}, u32[]{:S(2)}, u32[]{:S(2)}) collective-permute-start(bf16[4,264,512]{2,1,0:T(8,128)(2,1)S(1)} %shard_map.61.own_ref), channel_id=1, source_target_pairs={{0,8},{8,0},{1,9},{9,1},{2,10},{10,2},{3,11},{11,3},{4,12},{12,4},... | collective-permute-start | bytes 3244040 | tf_op jit(solution)/shard_map/ppermute | solution.py:283
  69.8 2.5 %all-to-all-done.1 = bf16[8,4,3,8,512]{4,3,2,1,0:T(8,128)(2,1)S(1)} async-done(((bf16[8,4,3,8,512]{4,3,2,1,0:T(8,128)(2,1)}), bf16[8,4,3,8,512]{4,3,2,1,0:T(8,128)(2,1)S(1)}, u32[]{:S(2)}, u32[]{:S(2)}) %all-to-all-start.1) | async-done | bytes 786464 | tf_op jit(solution)/shard_map/all_to_all | solution.py:237
  72.2 0.2 collective-permute-done.3.other_ref
  72.4 2.9 %shard_map.63 = bf16[8,3,8,512]{3,2,1,0:T(8,128)(2,1)} custom-call(s32[3]{0:T(128)S(1)} %pad_add_fusion.where_ref, bf16[4,264,512]{2,1,0:T(8,128)(2,1)S(1)} %shard_map.61.own_ref, bf16[4,264,512]{2,1,0:T(8,128)(2,1)S(1)} %collective-permute-done.3.other_ref, bf16[32,3,8,512]{3,2,1,0:T(8,128)(2,1)S(1)} %bitcast.16), custom_call_target="tpu_custom_call" | custom-call | tf_op jit(solution)/shard_map/pallas_call | solution.py:47
  75.4 18.0 %all_to_all.26.arr_ref = bf16[8,3,8,512]{3,2,1,0:T(8,128)(2,1)S(1)} all-to-all(bf16[8,3,8,512]{3,2,1,0:T(8,128)(2,1)} %shard_map.63), channel_id=1, replica_groups=mesh['z'=8,'y'=4,'core'=2,'head'=8] {'z'}, dimensions={0} | all-to-all | bytes 393216 | tf_op jit(solution)/shard_map/all_to_all | solution.py:237
  93.4 0.9 shard_map.64
  94.3 7.4 %all-to-all-start.3 = ((bf16[32,3,8,512]{3,2,1,0:T(8,128)(2,1)}), bf16[32,3,8,512]{3,2,1,0:T(8,128)(2,1)}, u32[]{:S(2)}, u32[]{:S(2)}) async-start(bf16[32,3,8,512]{3,2,1,0:T(8,128)(2,1)} %shard_map.64), calls=%async_computation.3 | async-start | bytes 1572864 | tf_op jit(solution)/shard_map/all_to_all | solution.py:237
  101.7 3.4 %collective-permute-start.8 = (bf16[264,512]{1,0:T(8,128)(2,1)S(1)}, bf16[264,512]{1,0:T(8,128)(2,1)S(1)}, u32[]{:S(2)}, u32[]{:S(2)}) collective-permute-start(bf16[264,512]{1,0:T(8,128)(2,1)S(1)} %get-tuple-element.7.refs_0_), channel_id=1, source_target_pairs={{0,64},{64,128},{128,192},{192,256},{256,320},{320,384},{384,448},... | collective-permute-start | bytes 811016 | tf_op jit(solution)/shard_map/ppermute | solution.py:295
  105.1 22.2 %collective-permute-done.8.refs_0_ = bf16[264,512]{1,0:T(8,128)(2,1)S(1)} collective-permute-done((bf16[264,512]{1,0:T(8,128)(2,1)S(1)}, bf16[264,512]{1,0:T(8,128)(2,1)S(1)}, u32[]{:S(2)}, u32[]{:S(2)}) %collective-permute-start.8) | collective-permute-done | bytes 270368 | tf_op jit(solution)/shard_map/ppermute | solution.py:295
  127.3 2.8 %collective-permute-start.10 = (bf16[264,512]{1,0:T(8,128)(2,1)S(1)}, bf16[264,512]{1,0:T(8,128)(2,1)S(1)}, u32[]{:S(2)}, u32[]{:S(2)}) collective-permute-start(bf16[264,512]{1,0:T(8,128)(2,1)S(1)} %collective-permute-done.8.refs_0_), channel_id=1, source_target_pairs={{0,48},{16,0},{32,16},{48,32},{1,49},{17,1},{33,17},{49,33},{2,50}... | collective-permute-start | bytes 811016 | tf_op jit(solution)/shard_map/ppermute | solution.py:272
  130.1 3.9 %collective-permute-start.9 = (bf16[264,512]{1,0:T(8,128)(2,1)S(1)}, bf16[264,512]{1,0:T(8,128)(2,1)S(1)}, u32[]{:S(2)}, u32[]{:S(2)}) collective-permute-start(bf16[264,512]{1,0:T(8,128)(2,1)S(1)} %collective-permute-done.8.refs_0_), channel_id=1, source_target_pairs={{0,16},{16,32},{32,48},{48,0},{1,17},{17,33},{33,49},{49,1},{2,18}... | collective-permute-start | bytes 811016 | tf_op jit(solution)/shard_map/ppermute | solution.py:271
  134.1 9.8 %collective-permute-done.10.refs_3_ = bf16[264,512]{1,0:T(8,128)(2,1)S(1)} collective-permute-done((bf16[264,512]{1,0:T(8,128)(2,1)S(1)}, bf16[264,512]{1,0:T(8,128)(2,1)S(1)}, u32[]{:S(2)}, u32[]{:S(2)}) %collective-permute-start.10) | collective-permute-done | bytes 270368 | tf_op jit(solution)/shard_map/ppermute | solution.py:272
  143.8 3.2 %collective-permute-done.9.refs_1_ = bf16[264,512]{1,0:T(8,128)(2,1)S(1)} collective-permute-done((bf16[264,512]{1,0:T(8,128)(2,1)S(1)}, bf16[264,512]{1,0:T(8,128)(2,1)S(1)}, u32[]{:S(2)}, u32[]{:S(2)}) %collective-permute-start.9) | collective-permute-done | bytes 270368 | tf_op jit(solution)/shard_map/ppermute | solution.py:271
  147.1 0.0 copy-start.4
  147.1 3.4 %collective-permute-start.11 = (bf16[264,512]{1,0:T(8,128)(2,1)S(1)}, bf16[264,512]{1,0:T(8,128)(2,1)S(1)}, u32[]{:S(2)}, u32[]{:S(2)}) collective-permute-start(bf16[264,512]{1,0:T(8,128)(2,1)S(1)} %broadcast_select_fusion), channel_id=1, source_target_pairs={{0,16},{16,32},{32,48},{48,0},{8,56},{24,8},{40,24},{56,40},{1,17}... | collective-permute-start | bytes 811016 | tf_op jit(solution)/shard_map/ppermute | solution.py:274
  150.4 8.1 %collective-permute-done.11.refs_2_ = bf16[264,512]{1,0:T(8,128)(2,1)S(1)} collective-permute-done((bf16[264,512]{1,0:T(8,128)(2,1)S(1)}, bf16[264,512]{1,0:T(8,128)(2,1)S(1)}, u32[]{:S(2)}, u32[]{:S(2)}) %collective-permute-start.11) | collective-permute-done | bytes 270368 | tf_op jit(solution)/shard_map/ppermute | solution.py:274
  158.5 0.6 shard_map.65.own_before_ref
  159.1 1.9 %collective-permute-start.12 = (bf16[4,264,512]{2,1,0:T(8,128)(2,1)S(1)}, bf16[4,264,512]{2,1,0:T(8,128)(2,1)}, u32[]{:S(2)}, u32[]{:S(2)}) collective-permute-start(bf16[4,264,512]{2,1,0:T(8,128)(2,1)S(1)} %shard_map.65.own_before_ref), channel_id=1, source_target_pairs={{0,8},{8,0},{1,9},{9,1},{2,10},{10,2},{3,11},{11,3},{4,12},{12,4},... | collective-permute-start | bytes 3244040 | tf_op jit(solution)/shard_map/ppermute | solution.py:296
  161.1 2.4 %collective-permute-start.7 = (bf16[32,3,8,512]{3,2,1,0:T(8,128)(2,1)S(1)}, bf16[32,3,8,512]{3,2,1,0:T(8,128)(2,1)}, u32[]{:S(2)}, u32[]{:S(2)}) collective-permute-start(bf16[32,3,8,512]{3,2,1,0:T(8,128)(2,1)S(1)} %bitcast.17), channel_id=1, source_target_pairs={{0,8},{8,0},{1,9},{9,1},{2,10},{10,2},{3,11},{11,3},{4,12},{12,4},... | collective-permute-start | bytes 2359304 | tf_op jit(solution)/shard_map/ppermute | solution.py:304
  163.5 0.0 all-to-all-done.3.g_own
  163.5 1.9 %collective-permute-start.6 = (bf16[32,3,8,512]{3,2,1,0:T(8,128)(2,1)}, bf16[32,3,8,512]{3,2,1,0:T(8,128)(2,1)S(1)}, u32[]{:S(2)}, u32[]{:S(2)}) collective-permute-start(bf16[32,3,8,512]{3,2,1,0:T(8,128)(2,1)} %all-to-all-done.3.g_own), channel_id=1, source_target_pairs={{0,8},{8,0},{1,9},{9,1},{2,10},{10,2},{3,11},{11,3},{4,12},{12,4},... | collective-permute-start | bytes 2359304 | tf_op jit(solution)/shard_map/ppermute | solution.py:305
  166.1 0.0 collective-permute-done.12.other_before_ref
  166.1 1.2 copy-done.1
  167.3 2.9 %shard_map.66.att_ref = f32[128,512]{1,0:T(8,128)S(1)} custom-call(s32[3]{0:T(128)S(1)} %pad_add_fusion.where_ref, bf16[128,512]{1,0:T(8,128)(2,1)S(1)} %copy-done.4, bf16[4,264,512]{2,1,0:T(8,128)(2,1)S(1)} %shard_map.61.own_ref, bf16[4,264,512]{2,1,0:T(8,128)(2,1)S(1)} %copy-done.1, bf16[4,264,512]{2,1,0:T(8,128)(2,1)S(1)} %shard_map.65.own_before_ref, ...), custom_call_target="tpu_custom_call" | custom-call | tf_op jit(solution)/shard_map/pallas_call | solution.py:47
  170.2 0.0 collective-permute-done.7.old_other
  170.2 0.0 collective-permute-done.6.g_other
  170.2 8.3 %shard_map.67 = (f32[3,8,512]{2,1,0:T(8,128)}, bf16[128,512]{1,0:T(8,128)(2,1)}) custom-call(s32[3]{0:T(128)S(1)} %pad_add_fusion.where_ref, f32[1]{0:T(128)S(6)} %copy.8.rate_ref, bf16[32,3,8,512]{3,2,1,0:T(8,128)(2,1)} %all-to-all-done.3.g_own, bf16[32,3,8,512]{3,2,1,0:T(8,128)(2,1)S(1)} %collective-permute-done.6.g_other, ...), custom_call_target="tpu_custom_call" | custom-call | tf_op jit(solution)/shard_map/pallas_call | solution.py:47
  178.5 11.6 %all_to_all.27.arr_ref = bf16[8,16,512]{2,1,0:T(8,128)(2,1)S(1)} all-to-all(bf16[8,16,512]{2,1,0:T(8,128)(2,1)} %bitcast.21), channel_id=1, replica_groups=mesh['z'=8,'y'=4,'core'=2,'head'=8] {'head'}, dimensions={0} | all-to-all | bytes 262144 | tf_op jit(solution)/shard_map/all_to_all | solution.py:237
  190.1 0.7 shard_map.68
  (14 shorter events, 0.1 us)
Async XLA Ops:
  0.6 1.0 copy-start.2
  1.6 13.9 %copy-start.6 = (f32[128,1]{0,1:T(1,128)S(1)}, f32[128,1]{0,1:T(1,128)}, u32[]{:S(2)}) copy-start(f32[128,1]{0,1:T(1,128)} %param.5) | copy-start | bytes 1540
  1.6 22.6 %copy-start.3 = (f32[3,1,8,512]{3,2,1,0:T(8,128)S(1)}, f32[3,1,8,512]{3,2,1,0:T(8,128)}, u32[]{:S(2)}) copy-start(f32[3,1,8,512]{3,2,1,0:T(8,128)} %param.7) | copy-start | bytes 147460
  16.3 39.8 %collective-permute-start = (bf16[264,512]{1,0:T(8,128)(2,1)S(1)}, bf16[264,512]{1,0:T(8,128)(2,1)S(1)}, u32[]{:S(2)}, u32[]{:S(2)}) collective-permute-start(bf16[264,512]{1,0:T(8,128)(2,1)S(1)} %get-tuple-element.7.refs_0_), channel_id=1, source_target_pairs={{0,16},{16,32},{32,48},{48,0},{1,17},{17,33},{33,49},{49,1},{2,18}... | collective-permute-start | bytes 811016 | tf_op jit(solution)/shard_map/ppermute | solution.py:271
  19.0 37.2 %collective-permute-start.1 = (bf16[264,512]{1,0:T(8,128)(2,1)S(1)}, bf16[264,512]{1,0:T(8,128)(2,1)S(1)}, u32[]{:S(2)}, u32[]{:S(2)}) collective-permute-start(bf16[264,512]{1,0:T(8,128)(2,1)S(1)} %get-tuple-element.7.refs_0_), channel_id=1, source_target_pairs={{0,48},{16,0},{32,16},{48,32},{1,49},{17,1},{33,17},{49,33},{2,50}... | collective-permute-start | bytes 811016 | tf_op jit(solution)/shard_map/ppermute | solution.py:272
  24.2 15.3 %collective-permute-start.4 = (bf16[1,3,8,512]{3,2,1,0:T(8,128)(2,1)S(1)}, bf16[1,3,8,512]{3,2,1,0:T(8,128)(2,1)S(1)}, u32[]{:S(2)}, u32[]{:S(2)}) collective-permute-start(bf16[1,3,8,512]{3,2,1,0:T(8,128)(2,1)S(1)} %fusion), channel_id=1, source_target_pairs={{0,32},{16,48},{32,0},{48,16},{1,33},{17,49},{33,1},{49,17},{2,34}... | collective-permute-start | bytes 73736 | tf_op jit(solution)/shard_map/ppermute | solution.py:248
  39.5 6.9 %collective-permute-start.5 = (bf16[2,3,8,512]{3,2,1,0:T(8,128)(2,1)S(1)}, bf16[2,3,8,512]{3,2,1,0:T(8,128)(2,1)S(1)}, u32[]{:S(2)}, u32[]{:S(2)}) collective-permute-start(bf16[2,3,8,512]{3,2,1,0:T(8,128)(2,1)S(1)} %pad_maximum_fusion.near_ref), channel_id=1, source_target_pairs={{0,16},{16,0},{32,48},{48,32},{1,17},{17,1},{33,49},{49,33},{2,18}... | collective-permute-start | bytes 147464 | tf_op jit(solution)/shard_map/ppermute | solution.py:249
  47.9 24.4 %all-to-all-start.1 = ((bf16[8,4,3,8,512]{4,3,2,1,0:T(8,128)(2,1)}), bf16[8,4,3,8,512]{4,3,2,1,0:T(8,128)(2,1)S(1)}, u32[]{:S(2)}, u32[]{:S(2)}) async-start(bf16[8,4,3,8,512]{4,3,2,1,0:T(8,128)(2,1)} %shard_map.62), calls=%async_computation.1 | async-start | bytes 1572864 | tf_op jit(solution)/shard_map/all_to_all | solution.py:237
  56.2 11.1 %collective-permute-start.2 = (bf16[264,512]{1,0:T(8,128)(2,1)S(1)}, bf16[264,512]{1,0:T(8,128)(2,1)S(1)}, u32[]{:S(2)}, u32[]{:S(2)}) collective-permute-start(bf16[264,512]{1,0:T(8,128)(2,1)S(1)} %broadcast_select_fusion.1), channel_id=1, source_target_pairs={{0,16},{16,32},{32,48},{48,0},{8,56},{24,8},{40,24},{56,40},{1,17}... | collective-permute-start | bytes 811016 | tf_op jit(solution)/shard_map/ppermute | solution.py:274
  67.8 4.6 %collective-permute-start.3 = (bf16[4,264,512]{2,1,0:T(8,128)(2,1)S(1)}, bf16[4,264,512]{2,1,0:T(8,128)(2,1)S(1)}, u32[]{:S(2)}, u32[]{:S(2)}) collective-permute-start(bf16[4,264,512]{2,1,0:T(8,128)(2,1)S(1)} %shard_map.61.own_ref), channel_id=1, source_target_pairs={{0,8},{8,0},{1,9},{9,1},{2,10},{10,2},{3,11},{11,3},{4,12},{12,4},... | collective-permute-start | bytes 3244040 | tf_op jit(solution)/shard_map/ppermute | solution.py:283
  72.4 2.9 %copy-start = (bf16[4,264,512]{2,1,0:T(8,128)(2,1)}, bf16[4,264,512]{2,1,0:T(8,128)(2,1)S(1)}, u32[]{:S(2)}) copy-start(bf16[4,264,512]{2,1,0:T(8,128)(2,1)S(1)} %collective-permute-done.3.other_ref) | copy-start | bytes 3244036
  94.3 69.2 %all-to-all-start.3 = ((bf16[32,3,8,512]{3,2,1,0:T(8,128)(2,1)}), bf16[32,3,8,512]{3,2,1,0:T(8,128)(2,1)}, u32[]{:S(2)}, u32[]{:S(2)}) async-start(bf16[32,3,8,512]{3,2,1,0:T(8,128)(2,1)} %shard_map.64), calls=%async_computation.3 | async-start | bytes 1572864 | tf_op jit(solution)/shard_map/all_to_all | solution.py:237
  101.7 25.6 %collective-permute-start.8 = (bf16[264,512]{1,0:T(8,128)(2,1)S(1)}, bf16[264,512]{1,0:T(8,128)(2,1)S(1)}, u32[]{:S(2)}, u32[]{:S(2)}) collective-permute-start(bf16[264,512]{1,0:T(8,128)(2,1)S(1)} %get-tuple-element.7.refs_0_), channel_id=1, source_target_pairs={{0,64},{64,128},{128,192},{192,256},{256,320},{320,384},{384,448},... | collective-permute-start | bytes 811016 | tf_op jit(solution)/shard_map/ppermute | solution.py:295
  127.3 16.5 %collective-permute-start.10 = (bf16[264,512]{1,0:T(8,128)(2,1)S(1)}, bf16[264,512]{1,0:T(8,128)(2,1)S(1)}, u32[]{:S(2)}, u32[]{:S(2)}) collective-permute-start(bf16[264,512]{1,0:T(8,128)(2,1)S(1)} %collective-permute-done.8.refs_0_), channel_id=1, source_target_pairs={{0,48},{16,0},{32,16},{48,32},{1,49},{17,1},{33,17},{49,33},{2,50}... | collective-permute-start | bytes 811016 | tf_op jit(solution)/shard_map/ppermute | solution.py:272
  130.1 16.9 %collective-permute-start.9 = (bf16[264,512]{1,0:T(8,128)(2,1)S(1)}, bf16[264,512]{1,0:T(8,128)(2,1)S(1)}, u32[]{:S(2)}, u32[]{:S(2)}) collective-permute-start(bf16[264,512]{1,0:T(8,128)(2,1)S(1)} %collective-permute-done.8.refs_0_), channel_id=1, source_target_pairs={{0,16},{16,32},{32,48},{48,0},{1,17},{17,33},{33,49},{49,1},{2,18}... | collective-permute-start | bytes 811016 | tf_op jit(solution)/shard_map/ppermute | solution.py:271
  147.1 19.0 %copy-start.4 = (bf16[128,512]{1,0:T(8,128)(2,1)S(1)}, bf16[128,512]{1,0:T(8,128)(2,1)}, u32[]{:S(2)}) copy-start(bf16[128,512]{1,0:T(8,128)(2,1)} %get-tuple-element.9.q_ref) | copy-start | bytes 393220
  147.1 11.4 %collective-permute-start.11 = (bf16[264,512]{1,0:T(8,128)(2,1)S(1)}, bf16[264,512]{1,0:T(8,128)(2,1)S(1)}, u32[]{:S(2)}, u32[]{:S(2)}) collective-permute-start(bf16[264,512]{1,0:T(8,128)(2,1)S(1)} %broadcast_select_fusion), channel_id=1, source_target_pairs={{0,16},{16,32},{32,48},{48,0},{8,56},{24,8},{40,24},{56,40},{1,17}... | collective-permute-start | bytes 811016 | tf_op jit(solution)/shard_map/ppermute | solution.py:274
  159.1 6.9 %collective-permute-start.12 = (bf16[4,264,512]{2,1,0:T(8,128)(2,1)S(1)}, bf16[4,264,512]{2,1,0:T(8,128)(2,1)}, u32[]{:S(2)}, u32[]{:S(2)}) collective-permute-start(bf16[4,264,512]{2,1,0:T(8,128)(2,1)S(1)} %shard_map.65.own_before_ref), channel_id=1, source_target_pairs={{0,8},{8,0},{1,9},{9,1},{2,10},{10,2},{3,11},{11,3},{4,12},{12,4},... | collective-permute-start | bytes 3244040 | tf_op jit(solution)/shard_map/ppermute | solution.py:296
  161.1 9.1 %collective-permute-start.7 = (bf16[32,3,8,512]{3,2,1,0:T(8,128)(2,1)S(1)}, bf16[32,3,8,512]{3,2,1,0:T(8,128)(2,1)}, u32[]{:S(2)}, u32[]{:S(2)}) collective-permute-start(bf16[32,3,8,512]{3,2,1,0:T(8,128)(2,1)S(1)} %bitcast.17), channel_id=1, source_target_pairs={{0,8},{8,0},{1,9},{9,1},{2,10},{10,2},{3,11},{11,3},{4,12},{12,4},... | collective-permute-start | bytes 2359304 | tf_op jit(solution)/shard_map/ppermute | solution.py:304
  163.5 6.7 %collective-permute-start.6 = (bf16[32,3,8,512]{3,2,1,0:T(8,128)(2,1)}, bf16[32,3,8,512]{3,2,1,0:T(8,128)(2,1)S(1)}, u32[]{:S(2)}, u32[]{:S(2)}) collective-permute-start(bf16[32,3,8,512]{3,2,1,0:T(8,128)(2,1)} %all-to-all-done.3.g_own), channel_id=1, source_target_pairs={{0,8},{8,0},{1,9},{9,1},{2,10},{10,2},{3,11},{11,3},{4,12},{12,4},... | collective-permute-start | bytes 2359304 | tf_op jit(solution)/shard_map/ppermute | solution.py:305
  166.1 1.2 copy-start.1
  167.3 2.9 %copy-start.5 = (bf16[128,512]{1,0:T(8,128)(2,1)S(1)}, bf16[128,512]{1,0:T(8,128)(2,1)}, u32[]{:S(2)}) copy-start(bf16[128,512]{1,0:T(8,128)(2,1)} %get-tuple-element.8.qn_ref) | copy-start | bytes 393220

commit v6 on v4

--- a/solution.py
+++ b/solution.py
@@ -36,7 +36,8 @@
     single = not isinstance(outs, (list, tuple))
     out_list = [outs] if single else list(outs)
     out_list = [
-        o if i in hbm_out else pltpu.VMEM(o.shape, o.dtype) for i, o in enumerate(out_list)
+        (pltpu.HBM if i in hbm_out else pltpu.VMEM)(o.shape, o.dtype)
+        for i, o in enumerate(out_list)
     ]
     args = [
         a if i in smem or i in hbm_in else pltpu.with_memory_space_constraint(a, pltpu.VMEM)
@@ -86,12 +87,6 @@
             sent_ref[d, j * t : (j + 1) * t] = arr_ref[j, 1]
             sent_ref[d, tok + j * t : tok + (j + 1) * t] = arr_ref[j, 2]
         sent_ref[d, 2 * tok :] = rate_rows
-
-
-def copies_of(rows_ref, out_ref):
-    rows = rows_ref[...].astype(BF16)
-    for d in range(out_ref.shape[0]):
-        out_ref[d] = rows
 
 
 def merged_rows(ref, m):
@@ -140,6 +135,12 @@
         out_ref[d] = total
 
 
+def slice_of(where_ref, near_ref, far_ref, out_ref):
+    for ref, odd in ((near_ref, 0), (far_ref, 1)):
+        for i, d in enumerate((0, 4, 2, 6)):
+            out_ref[where_ref[0] ^ (d + odd)] = ref[i]
+
+
 def arrange(where_ref, *refs):
     pieces, out_ref = refs[:-1], refs[-1]
     planes = pieces[0].shape[0]
@@ -238,15 +239,24 @@
         split_heads, shape((heads, 3, tok_part, hd)), (qkv,), hbm_in=(0,), hbm_out=(0,)
     )
     arrived = exchanged(split, "head")
-    old_copies = local_call(copies_of, shape((CHIPS_Z, 3, rows, hd)), (state,), hbm_out=(0,))
-    old_slice = exchanged(old_copies, "z")
     q, q_norm, sent = local_call(
         prepare,
         [shape((tok, hd)), shape((tok, hd)), shape((CHIPS_Y, 2 * tok + RATE_ROWS, hd))],
         (arrived, token_rate.reshape(1, tok)),
-        hbm_out=(2,),
+        hbm_out=(0, 1, 2),
     )
     kv_own = exchanged(sent, "y")
+
+    def across(distance):
+        return [(i, i ^ distance) for i in range(CHIPS_Z)]
+
+    old_two = state.astype(BF16)[None]
+    old_two = jnp.concatenate([old_two, lax.ppermute(old_two, "z", across(4))])
+    old_four = jnp.concatenate([old_two, lax.ppermute(old_two, "z", across(2))])
+    old_far = lax.ppermute(old_four, "z", across(1))
+    old_slice = local_call(
+        slice_of, shape((CHIPS_Z, 3, rows, hd)), (where, old_four, old_far), smem=(0,)
+    )
     kv_other = lax.ppermute(kv_own, "core", swap)
     partial = local_call(
         gradient, shape((CHIPS_Z, 3, rows, hd)), (kv_own, kv_other, old_slice), hbm_out=(0,)

time: 195 us -> 205 us (1.051)
  the two profiles are of different devices: /device:TPU:56 before, /device:TPU:1 now
where the time goes in v6:
time: 205 us; the launch traced here: 204 us
  blocking collectives  70.2 us (34%)
  waiting for transfers between devices  62.6 us (31%)
  starting transfers between devices  49.4 us (24%)
  Pallas kernels  19.5 us (10%)
    all_to_all x4, blocking collectives, exchanged(): return lax.all_to_all(pieces, axis, 0, 0, tiled=True)  70.2 us
    ppermute x1, waiting for transfers between devices, shards(): kv_own_before = lax.ppermute(kv_own, 'z', ring)  39.4 us
    pallas_call x9, Pallas kernels, local_call(): pl.pallas_call(body, in_specs=specs, out_specs=out_specs[0] if single els...  19.5 us
    ppermute x3, waiting for transfers between devices, shards(): lax.ppermute(old_slice, 'y', [(i, i ^ d) for i in range(CHIPS_Y)])  17.7 us
    ppermute x3, starting transfers between devices, shards(): lax.ppermute(old_slice, 'y', [(i, i ^ d) for i in range(CHIPS_Y)])  11.4 us
    ppermute x1, starting transfers between devices, shards(): old_two = jnp.concatenate([old_two, lax.ppermute(old_two, 'z', across(4))])  10.6 us
    ppermute x1, starting transfers between devices, shards(): old_four = jnp.concatenate([old_two, lax.ppermute(old_two, 'z', across(2))])  4.69 us
    ppermute x1, starting transfers between devices, shards(): kv_other = lax.ppermute(kv_own, 'core', swap)  4.48 us
  transfers between devices with their start and end apart: 12, of which 6 were waited for; matrix products, arithmetic and copies ran while one was open for 0% of the time, Pallas kernels for 3%

profile of v6, /device:TPU:1, one launch (start us, length us, event | category | flops | bytes accessed | tf_op | source)
XLA Modules:
  0.0 204.3 jit_solution(3483622704951097703)
XLA Ops:
  0.6 0.0 copy-start
  0.6 1.0 copy-done
  1.6 0.0 copy-start.4
  1.6 0.8 shard_map.59
  2.4 12.7 %all_to_all.25.arr_ref = bf16[8,3,16,512]{3,2,1,0:T(8,128)(2,1)S(1)} all-to-all(bf16[8,3,16,512]{3,2,1,0:T(8,128)(2,1)} %shard_map.59), channel_id=1, replica_groups=mesh['z'=8,'y'=4,'core'=2,'head'=8] {'head'}, dimensions={0} | all-to-all | bytes 786432 | tf_op jit(solution)/shard_map/all_to_all | solution.py:236
  15.1 0.0 copy-done.4
  15.1 1.2 shard_map.60
  16.2 0.0 copy-start.1
  16.2 33.5 %all_to_all.26.own_ref = bf16[4,264,512]{2,1,0:T(8,128)(2,1)S(1)} all-to-all(bf16[4,264,512]{2,1,0:T(8,128)(2,1)} %get-tuple-element.7), channel_id=1, replica_groups=mesh['z'=8,'y'=4,'core'=2,'head'=8] {'y'}, dimensions={0} | all-to-all | bytes 2162688 | tf_op jit(solution)/shard_map/all_to_all | solution.py:236
  49.7 4.5 %collective-permute-start = (bf16[4,264,512]{2,1,0:T(8,128)(2,1)S(1)}, bf16[4,264,512]{2,1,0:T(8,128)(2,1)S(1)}, u32[]{:S(2)}, u32[]{:S(2)}) collective-permute-start(bf16[4,264,512]{2,1,0:T(8,128)(2,1)S(1)} %all_to_all.26.own_ref), channel_id=1, source_target_pairs={{0,8},{8,0},{1,9},{9,1},{2,10},{10,2},{3,11},{11,3},{4,12},{12,4},... | collective-permute-start | bytes 3244040 | tf_op jit(solution)/shard_map/ppermute | solution.py:260
  54.2 0.0 copy-done.1
  54.2 10.6 %collective-permute-start.1 = (bf16[1,3,8,512]{3,2,1,0:T(8,128)(2,1)S(1)}, bf16[1,3,8,512]{3,2,1,0:T(8,128)(2,1)S(1)}, u32[]{:S(2)}, u32[]{:S(2)}) collective-permute-start(bf16[1,3,8,512]{3,2,1,0:T(8,128)(2,1)S(1)} %fusion), channel_id=1, source_target_pairs={{0,256},{64,320},{128,384},{192,448},{256,0},{320,64},{384,128},{4... | collective-permute-start | bytes 73736 | tf_op jit(solution)/shard_map/ppermute | solution.py:254
  64.9 1.6 collective-permute-done.1
  66.5 4.7 %collective-permute-start.2 = (bf16[2,3,8,512]{3,2,1,0:T(8,128)(2,1)S(1)}, bf16[2,3,8,512]{3,2,1,0:T(8,128)(2,1)S(1)}, u32[]{:S(2)}, u32[]{:S(2)}) collective-permute-start(bf16[2,3,8,512]{3,2,1,0:T(8,128)(2,1)S(1)} %pad_maximum_fusion.1), channel_id=1, source_target_pairs={{0,128},{64,192},{128,0},{192,64},{256,384},{320,448},{384,256},{4... | collective-permute-start | bytes 147464 | tf_op jit(solution)/shard_map/ppermute | solution.py:255
  71.2 1.5 collective-permute-done.2
  72.6 2.7 %collective-permute-start.3 = (bf16[4,3,8,512]{3,2,1,0:T(8,128)(2,1)S(1)}, bf16[4,3,8,512]{3,2,1,0:T(8,128)(2,1)S(1)}, u32[]{:S(2)}, u32[]{:S(2)}) collective-permute-start(bf16[4,3,8,512]{3,2,1,0:T(8,128)(2,1)S(1)} %pad_maximum_fusion.near_ref), channel_id=1, source_target_pairs={{0,64},{64,0},{128,192},{192,128},{256,320},{320,256},{384,448},{4... | collective-permute-start | bytes 294920 | tf_op jit(solution)/shard_map/ppermute | solution.py:256
  75.4 0.1 pad_add_fusion.where_ref
  75.5 2.5 %collective-permute-done.3.far_ref = bf16[4,3,8,512]{3,2,1,0:T(8,128)(2,1)S(1)} collective-permute-done((bf16[4,3,8,512]{3,2,1,0:T(8,128)(2,1)S(1)}, bf16[4,3,8,512]{3,2,1,0:T(8,128)(2,1)S(1)}, u32[]{:S(2)}, u32[]{:S(2)}) %collective-permute-start.3) | collective-permute-done | bytes 98336 | tf_op jit(solution)/shard_map/ppermute | solution.py:256
  78.0 0.6 shard_map.61.w_ref.refs_0_
  78.6 0.0 collective-permute-done.other_ref
  78.6 2.4 %shard_map.62 = bf16[8,3,8,512]{3,2,1,0:T(8,128)(2,1)} custom-call(bf16[4,264,512]{2,1,0:T(8,128)(2,1)S(1)} %all_to_all.26.own_ref, bf16[4,264,512]{2,1,0:T(8,128)(2,1)S(1)} %collective-permute-done.other_ref, bf16[8,3,8,512]{3,2,1,0:T(8,128)(2,1)S(1)} %shard_map.61.w_ref.refs_0_), custom_call_target="tpu_custom_call" | custom-call | tf_op jit(solution)/shard_map/pallas_call | solution.py:47
  81.0 15.1 %all_to_all.27.arr_ref = bf16[8,3,8,512]{3,2,1,0:T(8,128)(2,1)S(1)} all-to-all(bf16[8,3,8,512]{3,2,1,0:T(8,128)(2,1)} %shard_map.62), channel_id=1, replica_groups=mesh['z'=8,'y'=4,'core'=2,'head'=8] {'z'}, dimensions={0} | all-to-all | bytes 393216 | tf_op jit(solution)/shard_map/all_to_all | solution.py:236
  96.1 1.0 shard_map.63
  97.1 3.9 %all-to-all-start.3 = ((bf16[32,3,8,512]{3,2,1,0:T(8,128)(2,1)}), bf16[32,3,8,512]{3,2,1,0:T(8,128)(2,1)S(1)}, u32[]{:S(2)}, u32[]{:S(2)}) async-start(bf16[32,3,8,512]{3,2,1,0:T(8,128)(2,1)} %shard_map.63), calls=%async_computation.3 | async-start | bytes 1572864 | tf_op jit(solution)/shard_map/all_to_all | solution.py:236
  101.0 0.0 copy-start.2
  101.0 3.2 %collective-permute-start.9 = (bf16[4,264,512]{2,1,0:T(8,128)(2,1)S(1)}, bf16[4,264,512]{2,1,0:T(8,128)(2,1)}, u32[]{:S(2)}, u32[]{:S(2)}) collective-permute-start(bf16[4,264,512]{2,1,0:T(8,128)(2,1)S(1)} %all_to_all.26.own_ref), channel_id=1, source_target_pairs={{0,64},{64,128},{128,192},{192,256},{256,320},{320,384},{384,448},... | collective-permute-start | bytes 3244040 | tf_op jit(solution)/shard_map/ppermute | solution.py:268
  104.2 39.4 %collective-permute-done.9.own_before_ref = bf16[4,264,512]{2,1,0:T(8,128)(2,1)} collective-permute-done((bf16[4,264,512]{2,1,0:T(8,128)(2,1)S(1)}, bf16[4,264,512]{2,1,0:T(8,128)(2,1)}, u32[]{:S(2)}, u32[]{:S(2)}) %collective-permute-start.9) | collective-permute-done | bytes 1081376 | tf_op jit(solution)/shard_map/ppermute | solution.py:268
  143.6 4.0 %collective-permute-start.10 = (bf16[4,264,512]{2,1,0:T(8,128)(2,1)}, bf16[4,264,512]{2,1,0:T(8,128)(2,1)}, u32[]{:S(2)}, u32[]{:S(2)}) collective-permute-start(bf16[4,264,512]{2,1,0:T(8,128)(2,1)} %collective-permute-done.9.own_before_ref), channel_id=1, source_target_pairs={{0,8},{8,0},{1,9},{9,1},{2,10},{10,2},{3,11},{11,3},{4,12},{12,4},... | collective-permute-start | bytes 3244040 | tf_op jit(solution)/shard_map/ppermute | solution.py:269
  147.6 5.1 %collective-permute-start.7 = (bf16[8,3,8,512]{3,2,1,0:T(8,128)(2,1)S(1)}, bf16[8,3,8,512]{3,2,1,0:T(8,128)(2,1)S(1)}, u32[]{:S(2)}, u32[]{:S(2)}) collective-permute-start(bf16[8,3,8,512]{3,2,1,0:T(8,128)(2,1)S(1)} %shard_map.61.w_ref.refs_0_), channel_id=1, source_target_pairs={{0,48},{16,32},{32,16},{48,0},{1,49},{17,33},{33,17},{49,1},{2,50}... | collective-permute-start | bytes 589832 | tf_op jit(solution)/shard_map/ppermute | solution.py:277
  152.7 4.1 %collective-permute-start.6 = (bf16[8,3,8,512]{3,2,1,0:T(8,128)(2,1)S(1)}, bf16[8,3,8,512]{3,2,1,0:T(8,128)(2,1)S(1)}, u32[]{:S(2)}, u32[]{:S(2)}) collective-permute-start(bf16[8,3,8,512]{3,2,1,0:T(8,128)(2,1)S(1)} %shard_map.61.w_ref.refs_0_), channel_id=1, source_target_pairs={{0,32},{16,48},{32,0},{48,16},{1,33},{17,49},{33,1},{49,17},{2,34}... | collective-permute-start | bytes 589832 | tf_op jit(solution)/shard_map/ppermute | solution.py:277
  156.9 2.2 %collective-permute-start.5 = (bf16[8,3,8,512]{3,2,1,0:T(8,128)(2,1)S(1)}, bf16[8,3,8,512]{3,2,1,0:T(8,128)(2,1)S(1)}, u32[]{:S(2)}, u32[]{:S(2)}) collective-permute-start(bf16[8,3,8,512]{3,2,1,0:T(8,128)(2,1)S(1)} %shard_map.61.w_ref.refs_0_), channel_id=1, source_target_pairs={{0,16},{16,0},{32,48},{48,32},{1,17},{17,1},{33,49},{49,33},{2,18}... | collective-permute-start | bytes 589832 | tf_op jit(solution)/shard_map/ppermute | solution.py:277
  159.0 10.7 %collective-permute-done.7.refs_3_ = bf16[8,3,8,512]{3,2,1,0:T(8,128)(2,1)S(1)} collective-permute-done((bf16[8,3,8,512]{3,2,1,0:T(8,128)(2,1)S(1)}, bf16[8,3,8,512]{3,2,1,0:T(8,128)(2,1)S(1)}, u32[]{:S(2)}, u32[]{:S(2)}) %collective-permute-start.7) | collective-permute-done | bytes 196640 | tf_op jit(solution)/shard_map/ppermute | solution.py:277
  169.7 0.0 collective-permute-done.6.refs_2_
  169.7 7.0 %collective-permute-done.5.refs_1_ = bf16[8,3,8,512]{3,2,1,0:T(8,128)(2,1)S(1)} collective-permute-done((bf16[8,3,8,512]{3,2,1,0:T(8,128)(2,1)S(1)}, bf16[8,3,8,512]{3,2,1,0:T(8,128)(2,1)S(1)}, u32[]{:S(2)}, u32[]{:S(2)}) %collective-permute-start.5) | collective-permute-done | bytes 196640 | tf_op jit(solution)/shard_map/ppermute | solution.py:277
  176.7 1.5 shard_map.64.old_own
  178.2 2.4 %collective-permute-start.8 = (bf16[32,3,8,512]{3,2,1,0:T(8,128)(2,1)}, bf16[32,3,8,512]{3,2,1,0:T(8,128)(2,1)}, u32[]{:S(2)}, u32[]{:S(2)}) collective-permute-start(bf16[32,3,8,512]{3,2,1,0:T(8,128)(2,1)} %shard_map.64.old_own), channel_id=1, source_target_pairs={{0,8},{8,0},{1,9},{9,1},{2,10},{10,2},{3,11},{11,3},{4,12},{12,4},... | collective-permute-start | bytes 2359304 | tf_op jit(solution)/shard_map/ppermute | solution.py:281
  180.6 0.0 all-to-all-done.3.g_own
  180.6 1.9 collective-permute-start.4
  183.2 0.0 collective-permute-done.10.other_before_ref
  183.2 0.0 copy-done.2
  183.2 0.0 copy-start.3
  183.2 3.2 %shard_map.65.att_ref = f32[128,512]{1,0:T(8,128)S(1)} custom-call(s32[3]{0:T(128)S(1)} %pad_add_fusion.where_ref, bf16[128,512]{1,0:T(8,128)(2,1)S(1)} %copy-done.2, bf16[4,264,512]{2,1,0:T(8,128)(2,1)S(1)} %all_to_all.26.own_ref, bf16[4,264,512]{2,1,0:T(8,128)(2,1)S(1)} %collective-permute-done.other_ref, ...), custom_call_target="tpu_custom_call" | custom-call | tf_op jit(solution)/shard_map/pallas_call | solution.py:47
  186.4 0.0 collective-permute-done.8.old_other
  186.4 0.0 collective-permute-done.4.g_other
  186.4 0.0 copy-done.3
  186.4 8.3 %shard_map.66 = (f32[3,8,512]{2,1,0:T(8,128)}, bf16[128,512]{1,0:T(8,128)(2,1)}) custom-call(s32[3]{0:T(128)S(1)} %pad_add_fusion.where_ref, f32[1]{0:T(128)S(6)} %copy.8.rate_ref, bf16[32,3,8,512]{3,2,1,0:T(8,128)(2,1)S(1)} %all-to-all-done.3.g_own, bf16[32,3,8,512]{3,2,1,0:T(8,128)(2,1)S(1)} %collective-permute-done.4.g_other, ...), custom_call_target="tpu_custom_call" | custom-call | tf_op jit(solution)/shard_map/pallas_call | solution.py:47
  194.7 8.9 %all_to_all.28.arr_ref = bf16[8,16,512]{2,1,0:T(8,128)(2,1)S(1)} all-to-all(bf16[8,16,512]{2,1,0:T(8,128)(2,1)} %bitcast.17), channel_id=1, replica_groups=mesh['z'=8,'y'=4,'core'=2,'head'=8] {'head'}, dimensions={0} | all-to-all | bytes 262144 | tf_op jit(solution)/shard_map/all_to_all | solution.py:236
  203.6 0.7 shard_map.67
  (3 shorter events, 0.0 us)
Async XLA Ops:
  0.6 1.0 copy-start
  1.6 13.5 %copy-start.4 = (f32[128,1]{0,1:T(1,128)S(1)}, f32[128,1]{0,1:T(1,128)}, u32[]{:S(2)}) copy-start(f32[128,1]{0,1:T(1,128)} %param.5) | copy-start | bytes 1540
  16.2 38.0 %copy-start.1 = (f32[3,1,8,512]{3,2,1,0:T(8,128)S(1)}, f32[3,1,8,512]{3,2,1,0:T(8,128)}, u32[]{:S(2)}) copy-start(f32[3,1,8,512]{3,2,1,0:T(8,128)} %param.7) | copy-start | bytes 147460
  49.7 28.8 %collective-permute-start = (bf16[4,264,512]{2,1,0:T(8,128)(2,1)S(1)}, bf16[4,264,512]{2,1,0:T(8,128)(2,1)S(1)}, u32[]{:S(2)}, u32[]{:S(2)}) collective-permute-start(bf16[4,264,512]{2,1,0:T(8,128)(2,1)S(1)} %all_to_all.26.own_ref), channel_id=1, source_target_pairs={{0,8},{8,0},{1,9},{9,1},{2,10},{10,2},{3,11},{11,3},{4,12},{12,4},... | collective-permute-start | bytes 3244040 | tf_op jit(solution)/shard_map/ppermute | solution.py:260
  54.2 12.2 %collective-permute-start.1 = (bf16[1,3,8,512]{3,2,1,0:T(8,128)(2,1)S(1)}, bf16[1,3,8,512]{3,2,1,0:T(8,128)(2,1)S(1)}, u32[]{:S(2)}, u32[]{:S(2)}) collective-permute-start(bf16[1,3,8,512]{3,2,1,0:T(8,128)(2,1)S(1)} %fusion), channel_id=1, source_target_pairs={{0,256},{64,320},{128,384},{192,448},{256,0},{320,64},{384,128},{4... | collective-permute-start | bytes 73736 | tf_op jit(solution)/shard_map/ppermute | solution.py:254
  66.5 6.2 %collective-permute-start.2 = (bf16[2,3,8,512]{3,2,1,0:T(8,128)(2,1)S(1)}, bf16[2,3,8,512]{3,2,1,0:T(8,128)(2,1)S(1)}, u32[]{:S(2)}, u32[]{:S(2)}) collective-permute-start(bf16[2,3,8,512]{3,2,1,0:T(8,128)(2,1)S(1)} %pad_maximum_fusion.1), channel_id=1, source_target_pairs={{0,128},{64,192},{128,0},{192,64},{256,384},{320,448},{384,256},{4... | collective-permute-start | bytes 147464 | tf_op jit(solution)/shard_map/ppermute | solution.py:255
  72.6 5.4 %collective-permute-start.3 = (bf16[4,3,8,512]{3,2,1,0:T(8,128)(2,1)S(1)}, bf16[4,3,8,512]{3,2,1,0:T(8,128)(2,1)S(1)}, u32[]{:S(2)}, u32[]{:S(2)}) collective-permute-start(bf16[4,3,8,512]{3,2,1,0:T(8,128)(2,1)S(1)} %pad_maximum_fusion.near_ref), channel_id=1, source_target_pairs={{0,64},{64,0},{128,192},{192,128},{256,320},{320,256},{384,448},{4... | collective-permute-start | bytes 294920 | tf_op jit(solution)/shard_map/ppermute | solution.py:256
  97.1 83.5 %all-to-all-start.3 = ((bf16[32,3,8,512]{3,2,1,0:T(8,128)(2,1)}), bf16[32,3,8,512]{3,2,1,0:T(8,128)(2,1)S(1)}, u32[]{:S(2)}, u32[]{:S(2)}) async-start(bf16[32,3,8,512]{3,2,1,0:T(8,128)(2,1)} %shard_map.63), calls=%async_computation.3 | async-start | bytes 1572864 | tf_op jit(solution)/shard_map/all_to_all | solution.py:236
  101.0 82.2 %copy-start.2 = (bf16[128,512]{1,0:T(8,128)(2,1)S(1)}, bf16[128,512]{1,0:T(8,128)(2,1)}, u32[]{:S(2)}) copy-start(bf16[128,512]{1,0:T(8,128)(2,1)} %get-tuple-element.9.q_ref) | copy-start | bytes 393220
  101.0 42.6 %collective-permute-start.9 = (bf16[4,264,512]{2,1,0:T(8,128)(2,1)S(1)}, bf16[4,264,512]{2,1,0:T(8,128)(2,1)}, u32[]{:S(2)}, u32[]{:S(2)}) collective-permute-start(bf16[4,264,512]{2,1,0:T(8,128)(2,1)S(1)} %all_to_all.26.own_ref), channel_id=1, source_target_pairs={{0,64},{64,128},{128,192},{192,256},{256,320},{320,384},{384,448},... | collective-permute-start | bytes 3244040 | tf_op jit(solution)/shard_map/ppermute | solution.py:268
  143.6 39.6 %collective-permute-start.10 = (bf16[4,264,512]{2,1,0:T(8,128)(2,1)}, bf16[4,264,512]{2,1,0:T(8,128)(2,1)}, u32[]{:S(2)}, u32[]{:S(2)}) collective-permute-start(bf16[4,264,512]{2,1,0:T(8,128)(2,1)} %collective-permute-done.9.own_before_ref), channel_id=1, source_target_pairs={{0,8},{8,0},{1,9},{9,1},{2,10},{10,2},{3,11},{11,3},{4,12},{12,4},... | collective-permute-start | bytes 3244040 | tf_op jit(solution)/shard_map/ppermute | solution.py:269
  147.6 22.1 %collective-permute-start.7 = (bf16[8,3,8,512]{3,2,1,0:T(8,128)(2,1)S(1)}, bf16[8,3,8,512]{3,2,1,0:T(8,128)(2,1)S(1)}, u32[]{:S(2)}, u32[]{:S(2)}) collective-permute-start(bf16[8,3,8,512]{3,2,1,0:T(8,128)(2,1)S(1)} %shard_map.61.w_ref.refs_0_), channel_id=1, source_target_pairs={{0,48},{16,32},{32,16},{48,0},{1,49},{17,33},{33,17},{49,1},{2,50}... | collective-permute-start | bytes 589832 | tf_op jit(solution)/shard_map/ppermute | solution.py:277
  152.7 17.0 %collective-permute-start.6 = (bf16[8,3,8,512]{3,2,1,0:T(8,128)(2,1)S(1)}, bf16[8,3,8,512]{3,2,1,0:T(8,128)(2,1)S(1)}, u32[]{:S(2)}, u32[]{:S(2)}) collective-permute-start(bf16[8,3,8,512]{3,2,1,0:T(8,128)(2,1)S(1)} %shard_map.61.w_ref.refs_0_), channel_id=1, source_target_pairs={{0,32},{16,48},{32,0},{48,16},{1,33},{17,49},{33,1},{49,17},{2,34}... | collective-permute-start | bytes 589832 | tf_op jit(solution)/shard_map/ppermute | solution.py:277
  156.9 19.9 %collective-permute-start.5 = (bf16[8,3,8,512]{3,2,1,0:T(8,128)(2,1)S(1)}, bf16[8,3,8,512]{3,2,1,0:T(8,128)(2,1)S(1)}, u32[]{:S(2)}, u32[]{:S(2)}) collective-permute-start(bf16[8,3,8,512]{3,2,1,0:T(8,128)(2,1)S(1)} %shard_map.61.w_ref.refs_0_), channel_id=1, source_target_pairs={{0,16},{16,0},{32,48},{48,32},{1,17},{17,1},{33,49},{49,33},{2,18}... | collective-permute-start | bytes 589832 | tf_op jit(solution)/shard_map/ppermute | solution.py:277
  178.2 8.2 %collective-permute-start.8 = (bf16[32,3,8,512]{3,2,1,0:T(8,128)(2,1)}, bf16[32,3,8,512]{3,2,1,0:T(8,128)(2,1)}, u32[]{:S(2)}, u32[]{:S(2)}) collective-permute-start(bf16[32,3,8,512]{3,2,1,0:T(8,128)(2,1)} %shard_map.64.old_own), channel_id=1, source_target_pairs={{0,8},{8,0},{1,9},{9,1},{2,10},{10,2},{3,11},{11,3},{4,12},{12,4},... | collective-permute-start | bytes 2359304 | tf_op jit(solution)/shard_map/ppermute | solution.py:281
  180.6 5.8 %collective-permute-start.4 = (bf16[32,3,8,512]{3,2,1,0:T(8,128)(2,1)S(1)}, bf16[32,3,8,512]{3,2,1,0:T(8,128)(2,1)S(1)}, u32[]{:S(2)}, u32[]{:S(2)}) collective-permute-start(bf16[32,3,8,512]{3,2,1,0:T(8,128)(2,1)S(1)} %all-to-all-done.3.g_own), channel_id=1, source_target_pairs={{0,8},{8,0},{1,9},{9,1},{2,10},{10,2},{3,11},{11,3},{4,12},{12,4},... | collective-permute-start | bytes 2359304 | tf_op jit(solution)/shard_map/ppermute | solution.py:282
  183.2 3.2 %copy-start.3 = (bf16[128,512]{1,0:T(8,128)(2,1)S(1)}, bf16[128,512]{1,0:T(8,128)(2,1)}, u32[]{:S(2)}) copy-start(bf16[128,512]{1,0:T(8,128)(2,1)} %get-tuple-element.8.qn_ref) | copy-start | bytes 393220

commit v7 on v6

--- a/solution.py
+++ b/solution.py
@@ -11,6 +11,7 @@
 NS_1, NS_2, NS_3 = 3.4445, -4.775, 2.0315
 RMS_EPS = 1e-06
 NORM_EPS = 1e-07
+HIDDEN = -1e30
 
 SEQ = ("z", "y", "core")
 SEQ_HEAD = ("z", "y", "core", "head")
@@ -18,7 +19,7 @@
 F32, BF16 = jnp.float32, jnp.bfloat16
 CHIPS_Z, CHIPS_Y = 8, 4
 RATE_ROWS = 8
-KERNEL_VMEM = 20 * 1024 * 1024
+KERNEL_VMEM = 18 * 1024 * 1024
 
 
 def dot_nt(a, b):
@@ -70,9 +71,7 @@
     copies, lines, w = sent_ref.shape
     tok = n * t
     rate = rate_ref[...]
-    high = rate.astype(BF16).astype(F32)
-    middle = (rate - high).astype(BF16).astype(F32)
-    low = rate - high - middle
+    high, middle, low = in_parts(rate)
     spare = jnp.zeros((1, w - 3 * tok), F32)
     rate_rows = jnp.broadcast_to(
         jnp.concatenate([high, middle, low, spare], axis=1), (lines - 2 * tok, w)
@@ -149,46 +148,66 @@
             out_ref[z * len(pieces) + (where_ref[1] ^ d)] = piece[z]
 
 
-def attend(where_ref, q_ref, own_ref, other_ref, own_before_ref, other_before_ref, out_ref):
-    q = q_ref[...]
+def in_parts(x):
+    high = x.astype(BF16).astype(F32)
+    middle = (x - high).astype(BF16).astype(F32)
+    return high, middle, x - high - middle
+
+
+def attended(where_ref, q, own_ref, other_ref, q_plane, k_plane):
     t, w = q.shape
     chips = own_ref.shape[0]
-    z, y, core = where_ref[0], where_ref[1], where_ref[2]
+    y, core = where_ref[1], where_ref[2]
     plane = 2 * chips * t
-    q_pos = z * plane + (2 * y + core) * t + lax.broadcasted_iota(jnp.int32, (t, chips * t), 0)
+    q_pos = q_plane * plane + (2 * y + core) * t
+    q_pos = q_pos + lax.broadcasted_iota(jnp.int32, (t, chips * t), 0)
     lane = lax.broadcasted_iota(jnp.int32, (t, chips * t), 1)
     lane = lane + lane // t * t
-    sides = (
-        (own_ref, z, core),
-        (other_ref, z, 1 - core),
-        (own_before_ref, z - 1, core),
-        (other_before_ref, z - 1, 1 - core),
-    )
     parts = []
-    for ref, k_plane, k_core in sides:
+    for ref, k_core in ((own_ref, core), (other_ref, 1 - core)):
         k_pos = k_plane * plane + k_core * t + lane
         seen = (k_pos <= q_pos) & (k_pos > q_pos - WINDOW) & (k_pos >= 0)
         scores = dot_nt(q, ref[:, :t].reshape(chips * t, w)) * (w ** (-0.5))
-        parts.append(jnp.where(seen, scores, -jnp.inf))
-    top = jnp.maximum(jnp.maximum(parts[0], parts[1]), jnp.maximum(parts[2], parts[3]))
-    top = jnp.max(top, axis=1, keepdims=True)
+        parts.append(jnp.where(seen, scores, HIDDEN))
+    top = jnp.max(jnp.maximum(parts[0], parts[1]), axis=1, keepdims=True)
     parts = [jnp.exp(p - top) for p in parts]
-    inverse = 1.0 / jnp.sum(parts[0] + parts[1] + parts[2] + parts[3], axis=1, keepdims=True)
+    total = jnp.sum(parts[0] + parts[1], axis=1, keepdims=True)
     out = jnp.zeros((t, w), F32)
-    for p, (ref, _, _) in zip(parts, sides):
-        out = out + dot_nn((p * inverse).astype(BF16), ref[:, t : 2 * t].reshape(chips * t, w))
-    out_ref[...] = out
-
-
-def finish(
-    where_ref, rate_ref, g_own, g_other, old_own, old_other, state_ref, qn_ref, att_ref,
-    rows_ref, out_ref, x_ref, fresh_ref,
-):
-    n, _, r, _ = g_own.shape
-    half = n * r
+    for p, ref in zip(parts, (own_ref, other_ref)):
+        out = out + dot_nn(p.astype(BF16), ref[:, t : 2 * t].reshape(chips * t, w))
+    return out, top, total
+
+
+def attend_before(where_ref, q_ref, own_ref, other_ref, out_ref):
+    q_plane = (where_ref[0] + 1) % CHIPS_Z
+    out, top, total = attended(where_ref, q_ref[...], own_ref, other_ref, q_plane, q_plane - 1)
+    t, w = out.shape
+    out_ref[:, :w] = (out / total).astype(BF16)
+    lane = lax.broadcasted_iota(jnp.int32, (t, out_ref.shape[1] - w), 1)
+    extra = jnp.zeros(lane.shape, F32)
+    for i, part in enumerate((*in_parts(top), *in_parts(total))):
+        extra = jnp.where(lane == i, part, extra)
+    out_ref[:, w:] = extra.astype(BF16)
+
+
+def attend(where_ref, q_ref, own_ref, other_ref, before_ref, out_ref):
+    z = where_ref[0]
+    out, top, total = attended(where_ref, q_ref[...], own_ref, other_ref, z, z)
+    w = out.shape[1]
+    extra = before_ref[:, w:].astype(F32)
+    top_before = extra[:, 0:1] + extra[:, 1:2] + extra[:, 2:3]
+    total_before = extra[:, 3:4] + extra[:, 4:5] + extra[:, 5:6]
+    highest = jnp.maximum(top, top_before)
+    share = jnp.exp(top - highest)
+    share_before = total_before * jnp.exp(top_before - highest)
+    inverse = 1.0 / (total * share + share_before)
+    out_ref[...] = out * (share * inverse) + before_ref[:, :w].astype(F32) * (share_before * inverse)
+
+
+def newton(where_ref, rate_ref, g_own, g_other, state_ref, rows_ref, x_ref):
+    _, _, r, _ = g_own.shape
     rate = rate_ref[0]
     chip = where_ref[0] * CHIPS_Y + where_ref[1]
-
     xs = []
     for m in range(3):
         g = jnp.concatenate([merged_rows(g_own, m), merged_rows(g_other, m)], axis=0)
@@ -202,10 +221,17 @@
         moved = [dot_nn(poly, low) for poly, low in zip(polys, lows)]
         xs = [NS_1 * x + move for x, move in zip(xs, moved)]
     for m, x in enumerate(xs):
-        fresh_ref[m, :half] = (merged_rows(old_own, m) - rate * x[:half]).astype(BF16)
-        fresh_ref[m, half:] = (merged_rows(old_other, m) - rate * x[half:]).astype(BF16)
-        x_ref[m] = x[:half]
+        x_ref[m] = x
         rows_ref[m] = state_ref[m] - rate * x_ref[m, pl.ds(pl.multiple_of(chip * r, r), r)]
+
+
+def finish(rate_ref, x_ref, old_own, old_other, qn_ref, att_ref, out_ref, fresh_ref):
+    n, _, r, _ = old_own.shape
+    half = n * r
+    rate = rate_ref[0]
+    for m in range(3):
+        fresh_ref[m, :half] = (merged_rows(old_own, m) - rate * x_ref[m, :half]).astype(BF16)
+        fresh_ref[m, half:] = (merged_rows(old_other, m) - rate * x_ref[m, half:]).astype(BF16)
     gate = dot_nt(qn_ref[...], fresh_ref[0])
     up = dot_nt(qn_ref[...], fresh_ref[1])
     active = (jax.nn.silu(gate) * up).astype(BF16)
@@ -247,6 +273,8 @@
     )
     kv_own = exchanged(sent, "y")
 
+    q_above = lax.ppermute(q, "z", [((i + 1) % CHIPS_Z, i) for i in range(CHIPS_Z)])
+
     def across(distance):
         return [(i, i ^ distance) for i in range(CHIPS_Z)]
 
@@ -264,14 +292,20 @@
     parts = exchanged(partial, "z")
     g_copies = local_call(sum_and_copy, shape((chips, 3, rows, hd)), (parts,), hbm_out=(0,))
     g_own = exchanged(g_copies, CHIPS)
-    ring = [(i, (i + 1) % CHIPS_Z) for i in range(CHIPS_Z)]
-    kv_own_before = lax.ppermute(kv_own, "z", ring)
-    kv_other_before = lax.ppermute(kv_own_before, "core", swap)
+    share = local_call(
+        attend_before,
+        shape((tok, hd + 128)),
+        (where, q_above, kv_own, kv_other),
+        smem=(0,),
+    )
+    up = [(i, (i + 1) % CHIPS_Z) for i in range(CHIPS_Z)]
+    before = lax.ppermute(share, "z", up)
     attention = local_call(
         attend,
         shape((tok, hd), F32),
-        (where, q, kv_own, kv_other, kv_own_before, kv_other_before),
+        (where, q, kv_own, kv_other, before),
         smem=(0,),
+        hbm_in=(1,),
     )
     olds = [old_slice] + [
         lax.ppermute(old_slice, "y", [(i, i ^ d) for i in range(CHIPS_Y)])
@@ -280,16 +314,22 @@
     old_own = local_call(arrange, shape((chips, 3, rows, hd)), (where, *olds), smem=(0,))
     old_other = lax.ppermute(old_own, "core", swap)
     g_other = lax.ppermute(g_own, "core", swap)
-    new_rows, combined = local_call(
+    new_rows, x = local_call(
+        newton,
+        [shape((3, rows, hd), F32), shape((3, 2 * chips * rows, hd), F32)],
+        (where, head_rate, g_own, g_other, state),
+        smem=(0, 1),
+        hbm_in=(4,),
+        hbm_out=(0,),
+    )
+    combined = local_call(
         finish,
-        [shape((3, rows, hd), F32), shape((tok, hd))],
-        (where, head_rate, g_own, g_other, old_own, old_other, state, q_norm, attention),
-        smem=(0, 1),
-        hbm_out=(0, 1),
-        scratch=[
-            pltpu.VMEM((3, chips * rows, hd), F32),
-            pltpu.VMEM((3, 2 * chips * rows, hd), BF16),
-        ],
+        shape((tok, hd)),
+        (head_rate, x, old_own, old_other, q_norm, attention),
+        smem=(0,),
+        hbm_in=(4,),
+        hbm_out=(0,),
+        scratch=[pltpu.VMEM((3, 2 * chips * rows, hd), BF16)],
     )
     back = exchanged(combined.reshape(heads, tok_part, hd), "head")
     return (

time: 205 us -> 182 us (0.89)
  the two profiles are of different devices: /device:TPU:1 before, /device:TPU:8 now
where the time goes in v7:
time: 182 us; the launch traced here: 181 us
  blocking collectives  72.8 us (40%)
  starting transfers between devices  46.1 us (25%)
  waiting for transfers between devices  40.7 us (22%)
  Pallas kernels  18.8 us (10%)
    all_to_all x4, blocking collectives, exchanged(): return lax.all_to_all(pieces, axis, 0, 0, tiled=True)  72.8 us
    all_to_all x1, waiting for transfers between devices, exchanged(): return lax.all_to_all(pieces, axis, 0, 0, tiled=True)  22.2 us
    pallas_call x11, Pallas kernels, local_call(): pl.pallas_call(body, in_specs=specs, out_specs=out_specs[0] if single els...  18.8 us
    ppermute x3, starting transfers between devices, shards(): lax.ppermute(old_slice, 'y', [(i, i ^ d) for i in range(CHIPS_Y)])  12.4 us
    ppermute x1, starting transfers between devices, shards(): old_two = jnp.concatenate([old_two, lax.ppermute(old_two, 'z', across(4))])  10.9 us
    ppermute x1, waiting for transfers between devices, shards(): lax.ppermute(q, 'z', [((i + 1) % CHIPS_Z, i) for i in range(CHIPS_Z)])  4.85 us
    ppermute x1, starting transfers between devices, shards(): old_four = jnp.concatenate([old_two, lax.ppermute(old_two, 'z', across(2))])  4.76 us
    ppermute x1, waiting for transfers between devices, shards(): before = lax.ppermute(share, 'z', up)  4.7 us
  transfers between devices with their start and end apart: 12, of which 6 were waited for; matrix products, arithmetic and copies ran while one was open for 0% of the time, Pallas kernels for 6%

profile of v7, /device:TPU:8, one launch (start us, length us, event | category | flops | bytes accessed | tf_op | source)
XLA Modules:
  0.0 181.0 jit_solution(14891521165366667132)
XLA Ops:
  0.6 0.0 copy-start
  0.6 1.0 copy-done
  1.6 0.0 copy-start.4
  1.6 0.8 shard_map.59
  2.4 15.8 %all_to_all.25.arr_ref = bf16[8,3,16,512]{3,2,1,0:T(8,128)(2,1)S(1)} all-to-all(bf16[8,3,16,512]{3,2,1,0:T(8,128)(2,1)} %shard_map.59), channel_id=1, replica_groups=mesh['z'=8,'y'=4,'core'=2,'head'=8] {'head'}, dimensions={0} | all-to-all | bytes 786432 | tf_op jit(solution)/shard_map/all_to_all | solution.py:262
  18.2 0.0 copy-done.4
  18.2 1.2 shard_map.60
  19.4 31.4 %all_to_all.26.own_ref = bf16[4,264,512]{2,1,0:T(8,128)(2,1)S(1)} all-to-all(bf16[4,264,512]{2,1,0:T(8,128)(2,1)} %get-tuple-element.7), channel_id=1, replica_groups=mesh['z'=8,'y'=4,'core'=2,'head'=8] {'y'}, dimensions={0} | all-to-all | bytes 2162688 | tf_op jit(solution)/shard_map/all_to_all | solution.py:262
  50.7 1.9 %collective-permute-start = (bf16[4,264,512]{2,1,0:T(8,128)(2,1)S(1)}, bf16[4,264,512]{2,1,0:T(8,128)(2,1)S(1)}, u32[]{:S(2)}, u32[]{:S(2)}) collective-permute-start(bf16[4,264,512]{2,1,0:T(8,128)(2,1)S(1)} %all_to_all.26.own_ref), channel_id=1, source_target_pairs={{0,8},{8,0},{1,9},{9,1},{2,10},{10,2},{3,11},{11,3},{4,12},{12,4},... | collective-permute-start | bytes 3244040 | tf_op jit(solution)/shard_map/ppermute | solution.py:288
  52.6 0.0 copy-done.1
  52.7 10.9 %collective-permute-start.1 = (bf16[1,3,8,512]{3,2,1,0:T(8,128)(2,1)S(1)}, bf16[1,3,8,512]{3,2,1,0:T(8,128)(2,1)S(1)}, u32[]{:S(2)}, u32[]{:S(2)}) collective-permute-start(bf16[1,3,8,512]{3,2,1,0:T(8,128)(2,1)S(1)} %fusion), channel_id=1, source_target_pairs={{0,256},{64,320},{128,384},{192,448},{256,0},{320,64},{384,128},{4... | collective-permute-start | bytes 73736 | tf_op jit(solution)/shard_map/ppermute | solution.py:282
  63.6 1.9 %collective-permute-done.1 = bf16[1,3,8,512]{3,2,1,0:T(8,128)(2,1)S(1)} collective-permute-done((bf16[1,3,8,512]{3,2,1,0:T(8,128)(2,1)S(1)}, bf16[1,3,8,512]{3,2,1,0:T(8,128)(2,1)S(1)}, u32[]{:S(2)}, u32[]{:S(2)}) %collective-permute-start.1) | collective-permute-done | bytes 24608 | tf_op jit(solution)/shard_map/ppermute | solution.py:282
  65.5 4.8 %collective-permute-start.2 = (bf16[2,3,8,512]{3,2,1,0:T(8,128)(2,1)S(1)}, bf16[2,3,8,512]{3,2,1,0:T(8,128)(2,1)S(1)}, u32[]{:S(2)}, u32[]{:S(2)}) collective-permute-start(bf16[2,3,8,512]{3,2,1,0:T(8,128)(2,1)S(1)} %pad_maximum_fusion.1), channel_id=1, source_target_pairs={{0,128},{64,192},{128,0},{192,64},{256,384},{320,448},{384,256},{4... | collective-permute-start | bytes 147464 | tf_op jit(solution)/shard_map/ppermute | solution.py:283
  70.3 3.0 %collective-permute-done.2 = bf16[2,3,8,512]{3,2,1,0:T(8,128)(2,1)S(1)} collective-permute-done((bf16[2,3,8,512]{3,2,1,0:T(8,128)(2,1)S(1)}, bf16[2,3,8,512]{3,2,1,0:T(8,128)(2,1)S(1)}, u32[]{:S(2)}, u32[]{:S(2)}) %collective-permute-start.2) | collective-permute-done | bytes 49184 | tf_op jit(solution)/shard_map/ppermute | solution.py:283
  73.3 2.4 %collective-permute-start.3 = (bf16[4,3,8,512]{3,2,1,0:T(8,128)(2,1)S(1)}, bf16[4,3,8,512]{3,2,1,0:T(8,128)(2,1)S(1)}, u32[]{:S(2)}, u32[]{:S(2)}) collective-permute-start(bf16[4,3,8,512]{3,2,1,0:T(8,128)(2,1)S(1)} %pad_maximum_fusion.near_ref), channel_id=1, source_target_pairs={{0,64},{64,0},{128,192},{192,128},{256,320},{320,256},{384,448},{4... | collective-permute-start | bytes 294920 | tf_op jit(solution)/shard_map/ppermute | solution.py:284
  75.7 0.1 pad_add_fusion.where_ref
  75.8 4.0 %collective-permute-done.3.far_ref = bf16[4,3,8,512]{3,2,1,0:T(8,128)(2,1)S(1)} collective-permute-done((bf16[4,3,8,512]{3,2,1,0:T(8,128)(2,1)S(1)}, bf16[4,3,8,512]{3,2,1,0:T(8,128)(2,1)S(1)}, u32[]{:S(2)}, u32[]{:S(2)}) %collective-permute-start.3) | collective-permute-done | bytes 98336 | tf_op jit(solution)/shard_map/ppermute | solution.py:284
  79.8 0.6 shard_map.61.w_ref.refs_0_
  80.4 0.0 collective-permute-done.other_ref
  80.4 2.4 %shard_map.62 = bf16[8,3,8,512]{3,2,1,0:T(8,128)(2,1)} custom-call(bf16[4,264,512]{2,1,0:T(8,128)(2,1)S(1)} %all_to_all.26.own_ref, bf16[4,264,512]{2,1,0:T(8,128)(2,1)S(1)} %collective-permute-done.other_ref, bf16[8,3,8,512]{3,2,1,0:T(8,128)(2,1)S(1)} %shard_map.61.w_ref.refs_0_), custom_call_target="tpu_custom_call" | custom-call | tf_op jit(solution)/shard_map/pallas_call | solution.py:48
  82.8 16.5 %all_to_all.27.arr_ref = bf16[8,3,8,512]{3,2,1,0:T(8,128)(2,1)S(1)} all-to-all(bf16[8,3,8,512]{3,2,1,0:T(8,128)(2,1)} %shard_map.62), channel_id=1, replica_groups=mesh['z'=8,'y'=4,'core'=2,'head'=8] {'z'}, dimensions={0} | all-to-all | bytes 393216 | tf_op jit(solution)/shard_map/all_to_all | solution.py:262
  99.3 0.9 shard_map.63
  100.2 3.9 %all-to-all-start.3 = ((bf16[32,3,8,512]{3,2,1,0:T(8,128)(2,1)}), bf16[32,3,8,512]{3,2,1,0:T(8,128)(2,1)S(1)}, u32[]{:S(2)}, u32[]{:S(2)}) async-start(bf16[32,3,8,512]{3,2,1,0:T(8,128)(2,1)} %shard_map.63), calls=%async_computation.3 | async-start | bytes 1572864 | tf_op jit(solution)/shard_map/all_to_all | solution.py:262
  104.2 0.0 copy-start.3
  104.2 5.8 %collective-permute-start.7 = (bf16[8,3,8,512]{3,2,1,0:T(8,128)(2,1)S(1)}, bf16[8,3,8,512]{3,2,1,0:T(8,128)(2,1)S(1)}, u32[]{:S(2)}, u32[]{:S(2)}) collective-permute-start(bf16[8,3,8,512]{3,2,1,0:T(8,128)(2,1)S(1)} %shard_map.61.w_ref.refs_0_), channel_id=1, source_target_pairs={{0,48},{16,32},{32,16},{48,0},{1,49},{17,33},{33,17},{49,1},{2,50}... | collective-permute-start | bytes 589832 | tf_op jit(solution)/shard_map/ppermute | solution.py:311
  110.0 4.3 %collective-permute-start.6 = (bf16[8,3,8,512]{3,2,1,0:T(8,128)(2,1)S(1)}, bf16[8,3,8,512]{3,2,1,0:T(8,128)(2,1)}, u32[]{:S(2)}, u32[]{:S(2)}) collective-permute-start(bf16[8,3,8,512]{3,2,1,0:T(8,128)(2,1)S(1)} %shard_map.61.w_ref.refs_0_), channel_id=1, source_target_pairs={{0,32},{16,48},{32,0},{48,16},{1,33},{17,49},{33,1},{49,17},{2,34}... | collective-permute-start | bytes 589832 | tf_op jit(solution)/shard_map/ppermute | solution.py:311
  114.3 2.3 %collective-permute-start.5 = (bf16[8,3,8,512]{3,2,1,0:T(8,128)(2,1)S(1)}, bf16[8,3,8,512]{3,2,1,0:T(8,128)(2,1)}, u32[]{:S(2)}, u32[]{:S(2)}) collective-permute-start(bf16[8,3,8,512]{3,2,1,0:T(8,128)(2,1)S(1)} %shard_map.61.w_ref.refs_0_), channel_id=1, source_target_pairs={{0,16},{16,0},{32,48},{48,32},{1,17},{17,1},{33,49},{49,33},{2,18}... | collective-permute-start | bytes 589832 | tf_op jit(solution)/shard_map/ppermute | solution.py:311
  116.5 22.2 %all-to-all-done.3.g_own = bf16[32,3,8,512]{3,2,1,0:T(8,128)(2,1)S(1)} async-done(((bf16[32,3,8,512]{3,2,1,0:T(8,128)(2,1)}), bf16[32,3,8,512]{3,2,1,0:T(8,128)(2,1)S(1)}, u32[]{:S(2)}, u32[]{:S(2)}) %all-to-all-start.3) | async-done | bytes 786464 | tf_op jit(solution)/shard_map/all_to_all | solution.py:262
  138.8 1.9 %collective-permute-start.4 = (bf16[32,3,8,512]{3,2,1,0:T(8,128)(2,1)S(1)}, bf16[32,3,8,512]{3,2,1,0:T(8,128)(2,1)S(1)}, u32[]{:S(2)}, u32[]{:S(2)}) collective-permute-start(bf16[32,3,8,512]{3,2,1,0:T(8,128)(2,1)S(1)} %all-to-all-done.3.g_own), channel_id=1, source_target_pairs={{0,8},{8,0},{1,9},{9,1},{2,10},{10,2},{3,11},{11,3},{4,12},{12,4},... | collective-permute-start | bytes 2359304 | tf_op jit(solution)/shard_map/ppermute | solution.py:316
  140.7 0.0 collective-permute-done.7.refs_3_
  140.7 0.0 collective-permute-done.6.refs_2_
  140.7 0.0 collective-permute-done.5.refs_1_
  140.7 1.1 shard_map.65.old_own
  141.8 2.4 %collective-permute-start.8 = (bf16[32,3,8,512]{3,2,1,0:T(8,128)(2,1)S(1)}, bf16[32,3,8,512]{3,2,1,0:T(8,128)(2,1)S(1)}, u32[]{:S(2)}, u32[]{:S(2)}) collective-permute-start(bf16[32,3,8,512]{3,2,1,0:T(8,128)(2,1)S(1)} %shard_map.65.old_own), channel_id=1, source_target_pairs={{0,8},{8,0},{1,9},{9,1},{2,10},{10,2},{3,11},{11,3},{4,12},{12,4},... | collective-permute-start | bytes 2359304 | tf_op jit(solution)/shard_map/ppermute | solution.py:315
  144.2 0.0 copy-done.3
  144.2 2.5 %collective-permute-start.9 = (bf16[128,512]{1,0:T(8,128)(2,1)S(1)}, bf16[128,512]{1,0:T(8,128)(2,1)S(1)}, u32[]{:S(2)}, u32[]{:S(2)}) collective-permute-start(bf16[128,512]{1,0:T(8,128)(2,1)S(1)} %copy-done.3), channel_id=1, source_target_pairs={{64,0},{128,64},{192,128},{256,192},{320,256},{384,320},{448,384},... | collective-permute-start | bytes 393224 | tf_op jit(solution)/shard_map/ppermute | solution.py:276
  146.7 4.8 %collective-permute-done.9.q_ref = bf16[128,512]{1,0:T(8,128)(2,1)S(1)} collective-permute-done((bf16[128,512]{1,0:T(8,128)(2,1)S(1)}, bf16[128,512]{1,0:T(8,128)(2,1)S(1)}, u32[]{:S(2)}, u32[]{:S(2)}) %collective-permute-start.9) | collective-permute-done | bytes 131104 | tf_op jit(solution)/shard_map/ppermute | solution.py:276
  151.5 1.4 shard_map.66
  152.9 3.1 %collective-permute-start.10 = (bf16[128,640]{1,0:T(8,128)(2,1)S(1)}, bf16[128,640]{1,0:T(8,128)(2,1)S(1)}, u32[]{:S(2)}, u32[]{:S(2)}) collective-permute-start(bf16[128,640]{1,0:T(8,128)(2,1)S(1)} %shard_map.66), channel_id=1, source_target_pairs={{0,64},{64,128},{128,192},{192,256},{256,320},{320,384},{384,448},... | collective-permute-start | bytes 491528 | tf_op jit(solution)/shard_map/ppermute | solution.py:302
  156.7 4.7 %collective-permute-done.10.before_ref = bf16[128,640]{1,0:T(8,128)(2,1)S(1)} collective-permute-done((bf16[128,640]{1,0:T(8,128)(2,1)S(1)}, bf16[128,640]{1,0:T(8,128)(2,1)S(1)}, u32[]{:S(2)}, u32[]{:S(2)}) %collective-permute-start.10) | collective-permute-done | bytes 163872 | tf_op jit(solution)/shard_map/ppermute | solution.py:302
  161.4 1.6 shard_map.67.att_ref
  163.0 0.0 collective-permute-done.4.g_other
  163.0 6.9 %shard_map.64 = (f32[3,8,512]{2,1,0:T(8,128)}, f32[3,512,512]{2,1,0:T(8,128)S(1)}) custom-call(s32[3]{0:T(128)S(1)} %pad_add_fusion.where_ref, f32[1]{0:T(128)S(6)} %copy.8.rate_ref, bf16[32,3,8,512]{3,2,1,0:T(8,128)(2,1)S(1)} %all-to-all-done.3.g_own, bf16[32,3,8,512]{3,2,1,0:T(8,128)(2,1)S(1)} %collective-permute-done.4.g_other, f32[3,8,512]{2,1,0:T(8,128)S(1)} %bitcast.15), custom_call_target="tpu_custom_call" | custom-call | tf_op jit(solution)/shard_map/pallas_call | solution.py:48
  169.9 0.0 collective-permute-done.8.old_other
  169.9 0.0 copy-done.2
  169.9 1.3 shard_map.68
  171.2 9.1 %all_to_all.28.arr_ref = bf16[8,16,512]{2,1,0:T(8,128)(2,1)S(1)} all-to-all(bf16[8,16,512]{2,1,0:T(8,128)(2,1)} %bitcast.17), channel_id=1, replica_groups=mesh['z'=8,'y'=4,'core'=2,'head'=8] {'head'}, dimensions={0} | all-to-all | bytes 262144 | tf_op jit(solution)/shard_map/all_to_all | solution.py:262
  180.3 0.7 shard_map.69
  (5 shorter events, 0.0 us)
Async XLA Ops:
  0.6 1.0 copy-start
  1.6 16.6 %copy-start.4 = (f32[128,1]{0,1:T(1,128)S(1)}, f32[128,1]{0,1:T(1,128)}, u32[]{:S(2)}) copy-start(f32[128,1]{0,1:T(1,128)} %param.5) | copy-start | bytes 1540
  19.4 33.3 %copy-start.1 = (f32[3,1,8,512]{3,2,1,0:T(8,128)S(1)}, f32[3,1,8,512]{3,2,1,0:T(8,128)}, u32[]{:S(2)}) copy-start(f32[3,1,8,512]{3,2,1,0:T(8,128)} %param.7) | copy-start | bytes 147460
  50.7 29.7 %collective-permute-start = (bf16[4,264,512]{2,1,0:T(8,128)(2,1)S(1)}, bf16[4,264,512]{2,1,0:T(8,128)(2,1)S(1)}, u32[]{:S(2)}, u32[]{:S(2)}) collective-permute-start(bf16[4,264,512]{2,1,0:T(8,128)(2,1)S(1)} %all_to_all.26.own_ref), channel_id=1, source_target_pairs={{0,8},{8,0},{1,9},{9,1},{2,10},{10,2},{3,11},{11,3},{4,12},{12,4},... | collective-permute-start | bytes 3244040 | tf_op jit(solution)/shard_map/ppermute | solution.py:288
  52.7 12.8 %collective-permute-start.1 = (bf16[1,3,8,512]{3,2,1,0:T(8,128)(2,1)S(1)}, bf16[1,3,8,512]{3,2,1,0:T(8,128)(2,1)S(1)}, u32[]{:S(2)}, u32[]{:S(2)}) collective-permute-start(bf16[1,3,8,512]{3,2,1,0:T(8,128)(2,1)S(1)} %fusion), channel_id=1, source_target_pairs={{0,256},{64,320},{128,384},{192,448},{256,0},{320,64},{384,128},{4... | collective-permute-start | bytes 73736 | tf_op jit(solution)/shard_map/ppermute | solution.py:282
  65.5 7.8 %collective-permute-start.2 = (bf16[2,3,8,512]{3,2,1,0:T(8,128)(2,1)S(1)}, bf16[2,3,8,512]{3,2,1,0:T(8,128)(2,1)S(1)}, u32[]{:S(2)}, u32[]{:S(2)}) collective-permute-start(bf16[2,3,8,512]{3,2,1,0:T(8,128)(2,1)S(1)} %pad_maximum_fusion.1), channel_id=1, source_target_pairs={{0,128},{64,192},{128,0},{192,64},{256,384},{320,448},{384,256},{4... | collective-permute-start | bytes 147464 | tf_op jit(solution)/shard_map/ppermute | solution.py:283
  73.3 6.5 %collective-permute-start.3 = (bf16[4,3,8,512]{3,2,1,0:T(8,128)(2,1)S(1)}, bf16[4,3,8,512]{3,2,1,0:T(8,128)(2,1)S(1)}, u32[]{:S(2)}, u32[]{:S(2)}) collective-permute-start(bf16[4,3,8,512]{3,2,1,0:T(8,128)(2,1)S(1)} %pad_maximum_fusion.near_ref), channel_id=1, source_target_pairs={{0,64},{64,0},{128,192},{192,128},{256,320},{320,256},{384,448},{4... | collective-permute-start | bytes 294920 | tf_op jit(solution)/shard_map/ppermute | solution.py:284
  100.2 38.5 %all-to-all-start.3 = ((bf16[32,3,8,512]{3,2,1,0:T(8,128)(2,1)}), bf16[32,3,8,512]{3,2,1,0:T(8,128)(2,1)S(1)}, u32[]{:S(2)}, u32[]{:S(2)}) async-start(bf16[32,3,8,512]{3,2,1,0:T(8,128)(2,1)} %shard_map.63), calls=%async_computation.3 | async-start | bytes 1572864 | tf_op jit(solution)/shard_map/all_to_all | solution.py:262
  104.2 40.1 %copy-start.3 = (bf16[128,512]{1,0:T(8,128)(2,1)S(1)}, bf16[128,512]{1,0:T(8,128)(2,1)}, u32[]{:S(2)}) copy-start(bf16[128,512]{1,0:T(8,128)(2,1)} %get-tuple-element.10.q_ref) | copy-start | bytes 393220
  104.2 36.5 %collective-permute-start.7 = (bf16[8,3,8,512]{3,2,1,0:T(8,128)(2,1)S(1)}, bf16[8,3,8,512]{3,2,1,0:T(8,128)(2,1)S(1)}, u32[]{:S(2)}, u32[]{:S(2)}) collective-permute-start(bf16[8,3,8,512]{3,2,1,0:T(8,128)(2,1)S(1)} %shard_map.61.w_ref.refs_0_), channel_id=1, source_target_pairs={{0,48},{16,32},{32,16},{48,0},{1,49},{17,33},{33,17},{49,1},{2,50}... | collective-permute-start | bytes 589832 | tf_op jit(solution)/shard_map/ppermute | solution.py:311
  110.0 30.7 %collective-permute-start.6 = (bf16[8,3,8,512]{3,2,1,0:T(8,128)(2,1)S(1)}, bf16[8,3,8,512]{3,2,1,0:T(8,128)(2,1)}, u32[]{:S(2)}, u32[]{:S(2)}) collective-permute-start(bf16[8,3,8,512]{3,2,1,0:T(8,128)(2,1)S(1)} %shard_map.61.w_ref.refs_0_), channel_id=1, source_target_pairs={{0,32},{16,48},{32,0},{48,16},{1,33},{17,49},{33,1},{49,17},{2,34}... | collective-permute-start | bytes 589832 | tf_op jit(solution)/shard_map/ppermute | solution.py:311
  114.3 26.4 %collective-permute-start.5 = (bf16[8,3,8,512]{3,2,1,0:T(8,128)(2,1)S(1)}, bf16[8,3,8,512]{3,2,1,0:T(8,128)(2,1)}, u32[]{:S(2)}, u32[]{:S(2)}) collective-permute-start(bf16[8,3,8,512]{3,2,1,0:T(8,128)(2,1)S(1)} %shard_map.61.w_ref.refs_0_), channel_id=1, source_target_pairs={{0,16},{16,0},{32,48},{48,32},{1,17},{17,1},{33,49},{49,33},{2,18}... | collective-permute-start | bytes 589832 | tf_op jit(solution)/shard_map/ppermute | solution.py:311
  138.8 24.2 %collective-permute-start.4 = (bf16[32,3,8,512]{3,2,1,0:T(8,128)(2,1)S(1)}, bf16[32,3,8,512]{3,2,1,0:T(8,128)(2,1)S(1)}, u32[]{:S(2)}, u32[]{:S(2)}) collective-permute-start(bf16[32,3,8,512]{3,2,1,0:T(8,128)(2,1)S(1)} %all-to-all-done.3.g_own), channel_id=1, source_target_pairs={{0,8},{8,0},{1,9},{9,1},{2,10},{10,2},{3,11},{11,3},{4,12},{12,4},... | collective-permute-start | bytes 2359304 | tf_op jit(solution)/shard_map/ppermute | solution.py:316
  141.8 28.1 %collective-permute-start.8 = (bf16[32,3,8,512]{3,2,1,0:T(8,128)(2,1)S(1)}, bf16[32,3,8,512]{3,2,1,0:T(8,128)(2,1)S(1)}, u32[]{:S(2)}, u32[]{:S(2)}) collective-permute-start(bf16[32,3,8,512]{3,2,1,0:T(8,128)(2,1)S(1)} %shard_map.65.old_own), channel_id=1, source_target_pairs={{0,8},{8,0},{1,9},{9,1},{2,10},{10,2},{3,11},{11,3},{4,12},{12,4},... | collective-permute-start | bytes 2359304 | tf_op jit(solution)/shard_map/ppermute | solution.py:315
  144.2 7.3 %collective-permute-start.9 = (bf16[128,512]{1,0:T(8,128)(2,1)S(1)}, bf16[128,512]{1,0:T(8,128)(2,1)S(1)}, u32[]{:S(2)}, u32[]{:S(2)}) collective-permute-start(bf16[128,512]{1,0:T(8,128)(2,1)S(1)} %copy-done.3), channel_id=1, source_target_pairs={{64,0},{128,64},{192,128},{256,192},{320,256},{384,320},{448,384},... | collective-permute-start | bytes 393224 | tf_op jit(solution)/shard_map/ppermute | solution.py:276
  152.9 8.4 %collective-permute-start.10 = (bf16[128,640]{1,0:T(8,128)(2,1)S(1)}, bf16[128,640]{1,0:T(8,128)(2,1)S(1)}, u32[]{:S(2)}, u32[]{:S(2)}) collective-permute-start(bf16[128,640]{1,0:T(8,128)(2,1)S(1)} %shard_map.66), channel_id=1, source_target_pairs={{0,64},{64,128},{128,192},{192,256},{256,320},{320,384},{384,448},... | collective-permute-start | bytes 491528 | tf_op jit(solution)/shard_map/ppermute | solution.py:302
  163.0 6.9 %copy-start.2 = (bf16[128,512]{1,0:T(8,128)(2,1)S(1)}, bf16[128,512]{1,0:T(8,128)(2,1)}, u32[]{:S(2)}) copy-start(bf16[128,512]{1,0:T(8,128)(2,1)} %get-tuple-element.9.qn_ref) | copy-start | bytes 393220

commit v8 on v7

--- a/solution.py
+++ b/solution.py
@@ -135,9 +135,11 @@
 
 
 def slice_of(where_ref, near_ref, far_ref, out_ref):
-    for ref, odd in ((near_ref, 0), (far_ref, 1)):
-        for i, d in enumerate((0, 4, 2, 6)):
-            out_ref[where_ref[0] ^ (d + odd)] = ref[i]
+    _, mats, r, w = near_ref.shape
+    for i, d in enumerate((0, 4, 2, 6)):
+        out_ref[(where_ref[0] + d) % CHIPS_Z] = near_ref[i]
+        rows = far_ref[i * mats * r : (i + 1) * mats * r].astype(F32).reshape(mats, r, w)
+        out_ref[(where_ref[0] + d + 1) % CHIPS_Z] = rows.astype(BF16)
 
 
 def arrange(where_ref, *refs):
@@ -180,7 +182,8 @@
 
 def attend_before(where_ref, q_ref, own_ref, other_ref, out_ref):
     q_plane = (where_ref[0] + 1) % CHIPS_Z
-    out, top, total = attended(where_ref, q_ref[...], own_ref, other_ref, q_plane, q_plane - 1)
+    q = q_ref[q_ref.shape[0] - out_ref.shape[0] :]
+    out, top, total = attended(where_ref, q, own_ref, other_ref, q_plane, q_plane - 1)
     t, w = out.shape
     out_ref[:, :w] = (out / total).astype(BF16)
     lane = lax.broadcasted_iota(jnp.int32, (t, out_ref.shape[1] - w), 1)
@@ -273,15 +276,14 @@
     )
     kv_own = exchanged(sent, "y")
 
-    q_above = lax.ppermute(q, "z", [((i + 1) % CHIPS_Z, i) for i in range(CHIPS_Z)])
-
-    def across(distance):
-        return [(i, i ^ distance) for i in range(CHIPS_Z)]
+    def above(distance):
+        return [((i + distance) % CHIPS_Z, i) for i in range(CHIPS_Z)]
 
     old_two = state.astype(BF16)[None]
-    old_two = jnp.concatenate([old_two, lax.ppermute(old_two, "z", across(4))])
-    old_four = jnp.concatenate([old_two, lax.ppermute(old_two, "z", across(2))])
-    old_far = lax.ppermute(old_four, "z", across(1))
+    old_two = jnp.concatenate([old_two, lax.ppermute(old_two, "z", above(4))])
+    old_four = jnp.concatenate([old_two, lax.ppermute(old_two, "z", above(2))])
+    sent_down = jnp.concatenate([old_four.reshape(-1, hd), q])
+    old_far = lax.ppermute(sent_down, "z", above(1))
     old_slice = local_call(
         slice_of, shape((CHIPS_Z, 3, rows, hd)), (where, old_four, old_far), smem=(0,)
     )
@@ -295,7 +297,7 @@
     share = local_call(
         attend_before,
         shape((tok, hd + 128)),
-        (where, q_above, kv_own, kv_other),
+        (where, old_far, kv_own, kv_other),
         smem=(0,),
     )
     up = [(i, (i + 1) % CHIPS_Z) for i in range(CHIPS_Z)]

time: 182 us -> 180 us (0.989)
  the two profiles are of different devices: /device:TPU:8 before, /device:TPU:16 now
where the time goes in v8:
time: 180 us; the launch traced here: 179 us
  blocking collectives  70.6 us (39%)
  starting transfers between devices  50.5 us (28%)
  waiting for transfers between devices  35.7 us (20%)
  Pallas kernels  19 us (11%)
    all_to_all x4, blocking collectives, exchanged(): return lax.all_to_all(pieces, axis, 0, 0, tiled=True)  70.6 us
    all_to_all x1, waiting for transfers between devices, exchanged(): return lax.all_to_all(pieces, axis, 0, 0, tiled=True)  21.9 us
    pallas_call x11, Pallas kernels, local_call(): pl.pallas_call(body, in_specs=specs, out_specs=out_specs[0] if single els...  19 us
    ppermute x3, starting transfers between devices, shards(): lax.ppermute(old_slice, 'y', [(i, i ^ d) for i in range(CHIPS_Y)])  12.2 us
    ppermute x1, starting transfers between devices, shards(): old_two = jnp.concatenate([old_two, lax.ppermute(old_two, 'z', above(4))])  10.9 us
    ppermute x1, starting transfers between devices, shards(): old_four = jnp.concatenate([old_two, lax.ppermute(old_two, 'z', above(2))])  8.01 us
    ppermute x1, waiting for transfers between devices, shards(): before = lax.ppermute(share, 'z', up)  6.65 us
    ppermute x1, starting transfers between devices, shards(): old_far = lax.ppermute(sent_down, 'z', above(1))  6.07 us
  transfers between devices with their start and end apart: 11, of which 5 were waited for; matrix products, arithmetic and copies ran while one was open for 0% of the time, Pallas kernels for 6%

profile of v8, /device:TPU:16, one launch (start us, length us, event | category | flops | bytes accessed | tf_op | source)
XLA Modules:
  0.0 179.1 jit_solution(14646967925984269253)
XLA Ops:
  0.6 0.0 copy-start.1
  0.6 1.0 copy-done.1
  1.6 0.0 copy-start.6
  1.6 0.8 shard_map.59
  2.4 14.0 %all_to_all.25.arr_ref = bf16[8,3,16,512]{3,2,1,0:T(8,128)(2,1)S(1)} all-to-all(bf16[8,3,16,512]{3,2,1,0:T(8,128)(2,1)} %shard_map.59), channel_id=1, replica_groups=mesh['z'=8,'y'=4,'core'=2,'head'=8] {'head'}, dimensions={0} | all-to-all | bytes 786432 | tf_op jit(solution)/shard_map/all_to_all | solution.py:265
  16.4 0.0 copy-done.6
  16.4 1.2 shard_map.60
  17.6 32.0 %all_to_all.26.own_ref = bf16[4,264,512]{2,1,0:T(8,128)(2,1)S(1)} all-to-all(bf16[4,264,512]{2,1,0:T(8,128)(2,1)} %get-tuple-element.7), channel_id=1, replica_groups=mesh['z'=8,'y'=4,'core'=2,'head'=8] {'y'}, dimensions={0} | all-to-all | bytes 2162688 | tf_op jit(solution)/shard_map/all_to_all | solution.py:265
  49.6 1.9 %collective-permute-start = (bf16[4,264,512]{2,1,0:T(8,128)(2,1)S(1)}, bf16[4,264,512]{2,1,0:T(8,128)(2,1)S(1)}, u32[]{:S(2)}, u32[]{:S(2)}) collective-permute-start(bf16[4,264,512]{2,1,0:T(8,128)(2,1)S(1)} %all_to_all.26.own_ref), channel_id=1, source_target_pairs={{0,8},{8,0},{1,9},{9,1},{2,10},{10,2},{3,11},{11,3},{4,12},{12,4},... | collective-permute-start | bytes 3244040 | tf_op jit(solution)/shard_map/ppermute | solution.py:290
  51.5 0.0 copy-done.2
  51.5 10.9 %collective-permute-start.1 = (bf16[1,3,8,512]{3,2,1,0:T(8,128)(2,1)S(1)}, bf16[1,3,8,512]{3,2,1,0:T(8,128)(2,1)S(1)}, u32[]{:S(2)}, u32[]{:S(2)}) collective-permute-start(bf16[1,3,8,512]{3,2,1,0:T(8,128)(2,1)S(1)} %fusion), channel_id=1, source_target_pairs={{256,0},{320,64},{384,128},{448,192},{0,256},{64,320},{128,384},{1... | collective-permute-start | bytes 73736 | tf_op jit(solution)/shard_map/ppermute | solution.py:283
  62.4 1.9 %collective-permute-done.1 = bf16[1,3,8,512]{3,2,1,0:T(8,128)(2,1)S(1)} collective-permute-done((bf16[1,3,8,512]{3,2,1,0:T(8,128)(2,1)S(1)}, bf16[1,3,8,512]{3,2,1,0:T(8,128)(2,1)S(1)}, u32[]{:S(2)}, u32[]{:S(2)}) %collective-permute-start.1) | collective-permute-done | bytes 24608 | tf_op jit(solution)/shard_map/ppermute | solution.py:283
  64.4 8.0 %collective-permute-start.2 = (bf16[2,3,8,512]{3,2,1,0:T(8,128)(2,1)S(1)}, bf16[2,3,8,512]{3,2,1,0:T(8,128)(2,1)S(1)}, u32[]{:S(2)}, u32[]{:S(2)}) collective-permute-start(bf16[2,3,8,512]{3,2,1,0:T(8,128)(2,1)S(1)} %pad_maximum_fusion.2), channel_id=1, source_target_pairs={{128,0},{192,64},{256,128},{320,192},{384,256},{448,320},{0,384},{... | collective-permute-start | bytes 147464 | tf_op jit(solution)/shard_map/ppermute | solution.py:284
  72.4 1.7 collective-permute-done.2
  74.1 0.0 copy-done
  74.2 6.1 %collective-permute-start.3 = (bf16[224,512]{1,0:T(8,128)(2,1)S(1)}, bf16[224,512]{1,0:T(8,128)(2,1)S(1)}, u32[]{:S(2)}, u32[]{:S(2)}) collective-permute-start(bf16[224,512]{1,0:T(8,128)(2,1)S(1)} %pad_maximum_fusion), channel_id=1, source_target_pairs={{64,0},{128,64},{192,128},{256,192},{320,256},{384,320},{448,384},... | collective-permute-start | bytes 688136 | tf_op jit(solution)/shard_map/ppermute | solution.py:286
  80.2 0.1 pad_add_fusion.where_ref
  80.3 3.4 %collective-permute-done.3.far_ref.q_ref = bf16[224,512]{1,0:T(8,128)(2,1)S(1)} collective-permute-done((bf16[224,512]{1,0:T(8,128)(2,1)S(1)}, bf16[224,512]{1,0:T(8,128)(2,1)S(1)}, u32[]{:S(2)}, u32[]{:S(2)}) %collective-permute-start.3) | collective-permute-done | bytes 229408 | tf_op jit(solution)/shard_map/ppermute | solution.py:286
  83.8 0.6 shard_map.61.w_ref.refs_0_
  84.3 0.0 collective-permute-done.other_ref
  84.4 0.0 copy-done.4
  84.4 2.4 %shard_map.62 = bf16[8,3,8,512]{3,2,1,0:T(8,128)(2,1)} custom-call(bf16[4,264,512]{2,1,0:T(8,128)(2,1)S(1)} %all_to_all.26.own_ref, bf16[4,264,512]{2,1,0:T(8,128)(2,1)S(1)} %collective-permute-done.other_ref, bf16[8,3,8,512]{3,2,1,0:T(8,128)(2,1)S(1)} %shard_map.61.w_ref.refs_0_), custom_call_target="tpu_custom_call" | custom-call | tf_op jit(solution)/shard_map/pallas_call | solution.py:48
  86.8 14.7 %all_to_all.27.arr_ref = bf16[8,3,8,512]{3,2,1,0:T(8,128)(2,1)S(1)} all-to-all(bf16[8,3,8,512]{3,2,1,0:T(8,128)(2,1)} %shard_map.62), channel_id=1, replica_groups=mesh['z'=8,'y'=4,'core'=2,'head'=8] {'z'}, dimensions={0} | all-to-all | bytes 393216 | tf_op jit(solution)/shard_map/all_to_all | solution.py:265
  101.5 0.9 shard_map.63
  102.4 5.2 %all-to-all-start.3 = ((bf16[32,3,8,512]{3,2,1,0:T(8,128)(2,1)}), bf16[32,3,8,512]{3,2,1,0:T(8,128)(2,1)S(1)}, u32[]{:S(2)}, u32[]{:S(2)}) async-start(bf16[32,3,8,512]{3,2,1,0:T(8,128)(2,1)} %shard_map.63), calls=%async_computation.3 | async-start | bytes 1572864 | tf_op jit(solution)/shard_map/all_to_all | solution.py:265
  107.6 5.5 %collective-permute-start.7 = (bf16[8,3,8,512]{3,2,1,0:T(8,128)(2,1)S(1)}, bf16[8,3,8,512]{3,2,1,0:T(8,128)(2,1)}, u32[]{:S(2)}, u32[]{:S(2)}) collective-permute-start(bf16[8,3,8,512]{3,2,1,0:T(8,128)(2,1)S(1)} %shard_map.61.w_ref.refs_0_), channel_id=1, source_target_pairs={{0,48},{16,32},{32,16},{48,0},{1,49},{17,33},{33,17},{49,1},{2,50}... | collective-permute-start | bytes 589832 | tf_op jit(solution)/shard_map/ppermute | solution.py:313
  113.1 2.3 %collective-permute-start.6 = (bf16[8,3,8,512]{3,2,1,0:T(8,128)(2,1)S(1)}, bf16[8,3,8,512]{3,2,1,0:T(8,128)(2,1)}, u32[]{:S(2)}, u32[]{:S(2)}) collective-permute-start(bf16[8,3,8,512]{3,2,1,0:T(8,128)(2,1)S(1)} %shard_map.61.w_ref.refs_0_), channel_id=1, source_target_pairs={{0,32},{16,48},{32,0},{48,16},{1,33},{17,49},{33,1},{49,17},{2,34}... | collective-permute-start | bytes 589832 | tf_op jit(solution)/shard_map/ppermute | solution.py:313
  115.4 4.5 %collective-permute-start.5 = (bf16[8,3,8,512]{3,2,1,0:T(8,128)(2,1)S(1)}, bf16[8,3,8,512]{3,2,1,0:T(8,128)(2,1)}, u32[]{:S(2)}, u32[]{:S(2)}) collective-permute-start(bf16[8,3,8,512]{3,2,1,0:T(8,128)(2,1)S(1)} %shard_map.61.w_ref.refs_0_), channel_id=1, source_target_pairs={{0,16},{16,0},{32,48},{48,32},{1,17},{17,1},{33,49},{49,33},{2,18}... | collective-permute-start | bytes 589832 | tf_op jit(solution)/shard_map/ppermute | solution.py:313
  119.9 21.9 %all-to-all-done.3.g_own = bf16[32,3,8,512]{3,2,1,0:T(8,128)(2,1)S(1)} async-done(((bf16[32,3,8,512]{3,2,1,0:T(8,128)(2,1)}), bf16[32,3,8,512]{3,2,1,0:T(8,128)(2,1)S(1)}, u32[]{:S(2)}, u32[]{:S(2)}) %all-to-all-start.3) | async-done | bytes 786464 | tf_op jit(solution)/shard_map/all_to_all | solution.py:265
  141.8 1.9 %collective-permute-start.4 = (bf16[32,3,8,512]{3,2,1,0:T(8,128)(2,1)S(1)}, bf16[32,3,8,512]{3,2,1,0:T(8,128)(2,1)S(1)}, u32[]{:S(2)}, u32[]{:S(2)}) collective-permute-start(bf16[32,3,8,512]{3,2,1,0:T(8,128)(2,1)S(1)} %all-to-all-done.3.g_own), channel_id=1, source_target_pairs={{0,8},{8,0},{1,9},{9,1},{2,10},{10,2},{3,11},{11,3},{4,12},{12,4},... | collective-permute-start | bytes 2359304 | tf_op jit(solution)/shard_map/ppermute | solution.py:318
  143.7 0.0 collective-permute-done.7.refs_3_
  143.7 0.0 collective-permute-done.6.refs_2_
  143.7 0.0 collective-permute-done.5.refs_1_
  143.7 0.0 copy-start.5
  143.8 0.6 copy-done.5
  144.4 1.2 shard_map.65.old_own
  145.6 2.4 %collective-permute-start.8 = (bf16[32,3,8,512]{3,2,1,0:T(8,128)(2,1)S(1)}, bf16[32,3,8,512]{3,2,1,0:T(8,128)(2,1)S(1)}, u32[]{:S(2)}, u32[]{:S(2)}) collective-permute-start(bf16[32,3,8,512]{3,2,1,0:T(8,128)(2,1)S(1)} %shard_map.65.old_own), channel_id=1, source_target_pairs={{0,8},{8,0},{1,9},{9,1},{2,10},{10,2},{3,11},{11,3},{4,12},{12,4},... | collective-permute-start | bytes 2359304 | tf_op jit(solution)/shard_map/ppermute | solution.py:317
  148.0 1.4 shard_map.66
  149.4 1.9 %collective-permute-start.9 = (bf16[128,640]{1,0:T(8,128)(2,1)S(1)}, bf16[128,640]{1,0:T(8,128)(2,1)S(1)}, u32[]{:S(2)}, u32[]{:S(2)}) collective-permute-start(bf16[128,640]{1,0:T(8,128)(2,1)S(1)} %shard_map.66), channel_id=1, source_target_pairs={{0,64},{64,128},{128,192},{192,256},{256,320},{320,384},{384,448},... | collective-permute-start | bytes 491528 | tf_op jit(solution)/shard_map/ppermute | solution.py:304
  152.0 6.6 %collective-permute-done.9.before_ref = bf16[128,640]{1,0:T(8,128)(2,1)S(1)} collective-permute-done((bf16[128,640]{1,0:T(8,128)(2,1)S(1)}, bf16[128,640]{1,0:T(8,128)(2,1)S(1)}, u32[]{:S(2)}, u32[]{:S(2)}) %collective-permute-start.9) | collective-permute-done | bytes 163872 | tf_op jit(solution)/shard_map/ppermute | solution.py:304
  158.6 1.6 shard_map.67.att_ref
  160.2 0.0 collective-permute-done.4.g_other
  160.2 6.9 %shard_map.64 = (f32[3,8,512]{2,1,0:T(8,128)}, f32[3,512,512]{2,1,0:T(8,128)S(1)}) custom-call(s32[3]{0:T(128)S(1)} %copy-done.5, f32[1]{0:T(128)S(6)} %copy.8.rate_ref, bf16[32,3,8,512]{3,2,1,0:T(8,128)(2,1)S(1)} %all-to-all-done.3.g_own, bf16[32,3,8,512]{3,2,1,0:T(8,128)(2,1)S(1)} %collective-permute-done.4.g_other, f32[3,8,512]{2,1,0:T(8,128)S(1)} %bitcast.17), custom_call_target="tpu_custom_call" | custom-call | tf_op jit(solution)/shard_map/pallas_call | solution.py:48
  167.1 0.0 collective-permute-done.8.old_other
  167.1 0.0 copy-done.3
  167.1 1.4 shard_map.68
  168.5 9.9 %all_to_all.28.arr_ref = bf16[8,16,512]{2,1,0:T(8,128)(2,1)S(1)} all-to-all(bf16[8,16,512]{2,1,0:T(8,128)(2,1)} %bitcast.19), channel_id=1, replica_groups=mesh['z'=8,'y'=4,'core'=2,'head'=8] {'head'}, dimensions={0} | all-to-all | bytes 262144 | tf_op jit(solution)/shard_map/all_to_all | solution.py:265
  178.4 0.7 shard_map.69
  (8 shorter events, 0.0 us)
Async XLA Ops:
  0.6 1.0 copy-start.1
  1.6 14.8 %copy-start.6 = (f32[128,1]{0,1:T(1,128)S(1)}, f32[128,1]{0,1:T(1,128)}, u32[]{:S(2)}) copy-start(f32[128,1]{0,1:T(1,128)} %param.5) | copy-start | bytes 1540
  17.6 33.9 %copy-start.2 = (f32[3,1,8,512]{3,2,1,0:T(8,128)S(1)}, f32[3,1,8,512]{3,2,1,0:T(8,128)}, u32[]{:S(2)}) copy-start(f32[3,1,8,512]{3,2,1,0:T(8,128)} %param.7) | copy-start | bytes 147460
  17.6 56.6 %copy-start = (bf16[128,512]{1,0:T(8,128)(2,1)S(1)}, bf16[128,512]{1,0:T(8,128)(2,1)}, u32[]{:S(2)}) copy-start(bf16[128,512]{1,0:T(8,128)(2,1)} %get-tuple-element.8.q_ref) | copy-start | bytes 393220
  49.6 34.8 %collective-permute-start = (bf16[4,264,512]{2,1,0:T(8,128)(2,1)S(1)}, bf16[4,264,512]{2,1,0:T(8,128)(2,1)S(1)}, u32[]{:S(2)}, u32[]{:S(2)}) collective-permute-start(bf16[4,264,512]{2,1,0:T(8,128)(2,1)S(1)} %all_to_all.26.own_ref), channel_id=1, source_target_pairs={{0,8},{8,0},{1,9},{9,1},{2,10},{10,2},{3,11},{11,3},{4,12},{12,4},... | collective-permute-start | bytes 3244040 | tf_op jit(solution)/shard_map/ppermute | solution.py:290
  51.5 12.8 %collective-permute-start.1 = (bf16[1,3,8,512]{3,2,1,0:T(8,128)(2,1)S(1)}, bf16[1,3,8,512]{3,2,1,0:T(8,128)(2,1)S(1)}, u32[]{:S(2)}, u32[]{:S(2)}) collective-permute-start(bf16[1,3,8,512]{3,2,1,0:T(8,128)(2,1)S(1)} %fusion), channel_id=1, source_target_pairs={{256,0},{320,64},{384,128},{448,192},{0,256},{64,320},{128,384},{1... | collective-permute-start | bytes 73736 | tf_op jit(solution)/shard_map/ppermute | solution.py:283
  64.4 9.7 %collective-permute-start.2 = (bf16[2,3,8,512]{3,2,1,0:T(8,128)(2,1)S(1)}, bf16[2,3,8,512]{3,2,1,0:T(8,128)(2,1)S(1)}, u32[]{:S(2)}, u32[]{:S(2)}) collective-permute-start(bf16[2,3,8,512]{3,2,1,0:T(8,128)(2,1)S(1)} %pad_maximum_fusion.2), channel_id=1, source_target_pairs={{128,0},{192,64},{256,128},{320,192},{384,256},{448,320},{0,384},{... | collective-permute-start | bytes 147464 | tf_op jit(solution)/shard_map/ppermute | solution.py:284
  74.2 9.6 %collective-permute-start.3 = (bf16[224,512]{1,0:T(8,128)(2,1)S(1)}, bf16[224,512]{1,0:T(8,128)(2,1)S(1)}, u32[]{:S(2)}, u32[]{:S(2)}) collective-permute-start(bf16[224,512]{1,0:T(8,128)(2,1)S(1)} %pad_maximum_fusion), channel_id=1, source_target_pairs={{64,0},{128,64},{192,128},{256,192},{320,256},{384,320},{448,384},... | collective-permute-start | bytes 688136 | tf_op jit(solution)/shard_map/ppermute | solution.py:286
  80.3 4.0 %copy-start.4 = (s32[3]{0:T(128)}, s32[3]{0:T(128)S(1)}, u32[]{:S(2)}) copy-start(s32[3]{0:T(128)S(1)} %pad_add_fusion.where_ref) | copy-start | bytes 40
  102.4 39.4 %all-to-all-start.3 = ((bf16[32,3,8,512]{3,2,1,0:T(8,128)(2,1)}), bf16[32,3,8,512]{3,2,1,0:T(8,128)(2,1)S(1)}, u32[]{:S(2)}, u32[]{:S(2)}) async-start(bf16[32,3,8,512]{3,2,1,0:T(8,128)(2,1)} %shard_map.63), calls=%async_computation.3 | async-start | bytes 1572864 | tf_op jit(solution)/shard_map/all_to_all | solution.py:265
  107.6 36.1 %collective-permute-start.7 = (bf16[8,3,8,512]{3,2,1,0:T(8,128)(2,1)S(1)}, bf16[8,3,8,512]{3,2,1,0:T(8,128)(2,1)}, u32[]{:S(2)}, u32[]{:S(2)}) collective-permute-start(bf16[8,3,8,512]{3,2,1,0:T(8,128)(2,1)S(1)} %shard_map.61.w_ref.refs_0_), channel_id=1, source_target_pairs={{0,48},{16,32},{32,16},{48,0},{1,49},{17,33},{33,17},{49,1},{2,50}... | collective-permute-start | bytes 589832 | tf_op jit(solution)/shard_map/ppermute | solution.py:313
  113.1 30.6 %collective-permute-start.6 = (bf16[8,3,8,512]{3,2,1,0:T(8,128)(2,1)S(1)}, bf16[8,3,8,512]{3,2,1,0:T(8,128)(2,1)}, u32[]{:S(2)}, u32[]{:S(2)}) collective-permute-start(bf16[8,3,8,512]{3,2,1,0:T(8,128)(2,1)S(1)} %shard_map.61.w_ref.refs_0_), channel_id=1, source_target_pairs={{0,32},{16,48},{32,0},{48,16},{1,33},{17,49},{33,1},{49,17},{2,34}... | collective-permute-start | bytes 589832 | tf_op jit(solution)/shard_map/ppermute | solution.py:313
  115.4 28.4 %collective-permute-start.5 = (bf16[8,3,8,512]{3,2,1,0:T(8,128)(2,1)S(1)}, bf16[8,3,8,512]{3,2,1,0:T(8,128)(2,1)}, u32[]{:S(2)}, u32[]{:S(2)}) collective-permute-start(bf16[8,3,8,512]{3,2,1,0:T(8,128)(2,1)S(1)} %shard_map.61.w_ref.refs_0_), channel_id=1, source_target_pairs={{0,16},{16,0},{32,48},{48,32},{1,17},{17,1},{33,49},{49,33},{2,18}... | collective-permute-start | bytes 589832 | tf_op jit(solution)/shard_map/ppermute | solution.py:313
  141.8 18.4 %collective-permute-start.4 = (bf16[32,3,8,512]{3,2,1,0:T(8,128)(2,1)S(1)}, bf16[32,3,8,512]{3,2,1,0:T(8,128)(2,1)S(1)}, u32[]{:S(2)}, u32[]{:S(2)}) collective-permute-start(bf16[32,3,8,512]{3,2,1,0:T(8,128)(2,1)S(1)} %all-to-all-done.3.g_own), channel_id=1, source_target_pairs={{0,8},{8,0},{1,9},{9,1},{2,10},{10,2},{3,11},{11,3},{4,12},{12,4},... | collective-permute-start | bytes 2359304 | tf_op jit(solution)/shard_map/ppermute | solution.py:318
  143.7 0.7 copy-start.5
  145.6 21.5 %collective-permute-start.8 = (bf16[32,3,8,512]{3,2,1,0:T(8,128)(2,1)S(1)}, bf16[32,3,8,512]{3,2,1,0:T(8,128)(2,1)S(1)}, u32[]{:S(2)}, u32[]{:S(2)}) collective-permute-start(bf16[32,3,8,512]{3,2,1,0:T(8,128)(2,1)S(1)} %shard_map.65.old_own), channel_id=1, source_target_pairs={{0,8},{8,0},{1,9},{9,1},{2,10},{10,2},{3,11},{11,3},{4,12},{12,4},... | collective-permute-start | bytes 2359304 | tf_op jit(solution)/shard_map/ppermute | solution.py:317
  149.4 9.2 %collective-permute-start.9 = (bf16[128,640]{1,0:T(8,128)(2,1)S(1)}, bf16[128,640]{1,0:T(8,128)(2,1)S(1)}, u32[]{:S(2)}, u32[]{:S(2)}) collective-permute-start(bf16[128,640]{1,0:T(8,128)(2,1)S(1)} %shard_map.66), channel_id=1, source_target_pairs={{0,64},{64,128},{128,192},{192,256},{256,320},{320,384},{384,448},... | collective-permute-start | bytes 491528 | tf_op jit(solution)/shard_map/ppermute | solution.py:304
  160.2 6.9 %copy-start.3 = (bf16[128,512]{1,0:T(8,128)(2,1)S(1)}, bf16[128,512]{1,0:T(8,128)(2,1)}, u32[]{:S(2)}) copy-start(bf16[128,512]{1,0:T(8,128)(2,1)} %get-tuple-element.10.qn_ref) | copy-start | bytes 393220

commit v9 on v8

--- a/solution.py
+++ b/solution.py
@@ -19,7 +19,8 @@
 F32, BF16 = jnp.float32, jnp.bfloat16
 CHIPS_Z, CHIPS_Y = 8, 4
 RATE_ROWS = 8
-KERNEL_VMEM = 18 * 1024 * 1024
+KERNEL_VMEM = 9 * 1024 * 1024
+NEWTON_VMEM = 18 * 1024 * 1024
 
 
 def dot_nt(a, b):
@@ -30,7 +31,7 @@
     return lax.dot_general(a, b, (((1,), (0,)), ((), ())), preferred_element_type=F32)
 
 
-def local_call(body, outs, args, smem=(), scratch=(), hbm_in=(), hbm_out=()):
+def local_call(body, outs, args, smem=(), scratch=(), hbm_in=(), hbm_out=(), vmem=KERNEL_VMEM):
     specs = [
         pl.BlockSpec(memory_space=pltpu.SMEM if i in smem else pltpu.VMEM) for i in range(len(args))
     ]
@@ -51,7 +52,7 @@
         out_specs=out_specs[0] if single else out_specs,
         out_shape=out_list[0] if single else out_list,
         scratch_shapes=list(scratch),
-        compiler_params=pltpu.CompilerParams(vmem_limit_bytes=KERNEL_VMEM),
+        compiler_params=pltpu.CompilerParams(vmem_limit_bytes=vmem),
     )(*args)
 
 
@@ -323,6 +324,7 @@
         smem=(0, 1),
         hbm_in=(4,),
         hbm_out=(0,),
+        vmem=NEWTON_VMEM,
     )
     combined = local_call(
         finish,

time: 180 us -> 180 us (level)
  no operation moved by 1% of the time
where the time goes in v9:
time: 180 us; the launch traced here: 179 us
  blocking collectives  70.6 us (39%)
  starting transfers between devices  50.5 us (28%)
  waiting for transfers between devices  35.7 us (20%)
  Pallas kernels  19 us (11%)
    all_to_all x4, blocking collectives, exchanged(): return lax.all_to_all(pieces, axis, 0, 0, tiled=True)  70.6 us
    all_to_all x1, waiting for transfers between devices, exchanged(): return lax.all_to_all(pieces, axis, 0, 0, tiled=True)  21.9 us
    pallas_call x11, Pallas kernels, local_call(): pl.pallas_call(body, in_specs=specs, out_specs=out_specs[0] if single els...  19 us
    ppermute x3, starting transfers between devices, shards(): lax.ppermute(old_slice, 'y', [(i, i ^ d) for i in range(CHIPS_Y)])  12.2 us
    ppermute x1, starting transfers between devices, shards(): old_two = jnp.concatenate([old_two, lax.ppermute(old_two, 'z', above(4))])  10.9 us
    ppermute x1, starting transfers between devices, shards(): old_four = jnp.concatenate([old_two, lax.ppermute(old_two, 'z', above(2))])  8.01 us
    ppermute x1, waiting for transfers between devices, shards(): before = lax.ppermute(share, 'z', up)  6.65 us
    ppermute x1, starting transfers between devices, shards(): old_far = lax.ppermute(sent_down, 'z', above(1))  6.07 us
  transfers between devices with their start and end apart: 11, of which 5 were waited for; matrix products, arithmetic and copies ran while one was open for 0% of the time, Pallas kernels for 6%

profile of v9, /device:TPU:16, one launch (start us, length us, event | category | flops | bytes accessed | tf_op | source)
XLA Modules:
  0.0 179.1 jit_solution(1292194690082767970)
XLA Ops:
  0.6 0.0 copy-start.1
  0.6 1.0 copy-done.1
  1.6 0.8 shard_map.59
  2.4 14.0 %all_to_all.25.arr_ref = bf16[8,3,16,512]{3,2,1,0:T(8,128)(2,1)S(1)} all-to-all(bf16[8,3,16,512]{3,2,1,0:T(8,128)(2,1)} %shard_map.59), channel_id=1, replica_groups=mesh['z'=8,'y'=4,'core'=2,'head'=8] {'head'}, dimensions={0} | all-to-all | bytes 786432 | tf_op jit(solution)/shard_map/all_to_all | solution.py:266
  16.4 0.0 copy-done.7
  16.4 1.2 shard_map.60
  17.6 32.0 %all_to_all.26.own_ref = bf16[4,264,512]{2,1,0:T(8,128)(2,1)S(1)} all-to-all(bf16[4,264,512]{2,1,0:T(8,128)(2,1)} %get-tuple-element.7), channel_id=1, replica_groups=mesh['z'=8,'y'=4,'core'=2,'head'=8] {'y'}, dimensions={0} | all-to-all | bytes 2162688 | tf_op jit(solution)/shard_map/all_to_all | solution.py:266
  49.6 1.9 %collective-permute-start = (bf16[4,264,512]{2,1,0:T(8,128)(2,1)S(1)}, bf16[4,264,512]{2,1,0:T(8,128)(2,1)S(1)}, u32[]{:S(2)}, u32[]{:S(2)}) collective-permute-start(bf16[4,264,512]{2,1,0:T(8,128)(2,1)S(1)} %all_to_all.26.own_ref), channel_id=1, source_target_pairs={{0,8},{8,0},{1,9},{9,1},{2,10},{10,2},{3,11},{11,3},{4,12},{12,4},... | collective-permute-start | bytes 3244040 | tf_op jit(solution)/shard_map/ppermute | solution.py:291
  51.5 0.0 copy-done.2
  51.5 10.9 %collective-permute-start.1 = (bf16[1,3,8,512]{3,2,1,0:T(8,128)(2,1)S(1)}, bf16[1,3,8,512]{3,2,1,0:T(8,128)(2,1)S(1)}, u32[]{:S(2)}, u32[]{:S(2)}) collective-permute-start(bf16[1,3,8,512]{3,2,1,0:T(8,128)(2,1)S(1)} %fusion), channel_id=1, source_target_pairs={{256,0},{320,64},{384,128},{448,192},{0,256},{64,320},{128,384},{1... | collective-permute-start | bytes 73736 | tf_op jit(solution)/shard_map/ppermute | solution.py:284
  62.4 1.9 %collective-permute-done.1 = bf16[1,3,8,512]{3,2,1,0:T(8,128)(2,1)S(1)} collective-permute-done((bf16[1,3,8,512]{3,2,1,0:T(8,128)(2,1)S(1)}, bf16[1,3,8,512]{3,2,1,0:T(8,128)(2,1)S(1)}, u32[]{:S(2)}, u32[]{:S(2)}) %collective-permute-start.1) | collective-permute-done | bytes 24608 | tf_op jit(solution)/shard_map/ppermute | solution.py:284
  64.4 8.0 %collective-permute-start.2 = (bf16[2,3,8,512]{3,2,1,0:T(8,128)(2,1)S(1)}, bf16[2,3,8,512]{3,2,1,0:T(8,128)(2,1)S(1)}, u32[]{:S(2)}, u32[]{:S(2)}) collective-permute-start(bf16[2,3,8,512]{3,2,1,0:T(8,128)(2,1)S(1)} %pad_maximum_fusion.2), channel_id=1, source_target_pairs={{128,0},{192,64},{256,128},{320,192},{384,256},{448,320},{0,384},{... | collective-permute-start | bytes 147464 | tf_op jit(solution)/shard_map/ppermute | solution.py:285
  72.4 1.7 collective-permute-done.2
  74.1 0.0 copy-done
  74.2 6.1 %collective-permute-start.3 = (bf16[224,512]{1,0:T(8,128)(2,1)S(1)}, bf16[224,512]{1,0:T(8,128)(2,1)S(1)}, u32[]{:S(2)}, u32[]{:S(2)}) collective-permute-start(bf16[224,512]{1,0:T(8,128)(2,1)S(1)} %pad_maximum_fusion), channel_id=1, source_target_pairs={{64,0},{128,64},{192,128},{256,192},{320,256},{384,320},{448,384},... | collective-permute-start | bytes 688136 | tf_op jit(solution)/shard_map/ppermute | solution.py:287
  80.2 0.1 pad_add_fusion.where_ref
  80.3 3.4 %collective-permute-done.3.far_ref.q_ref = bf16[224,512]{1,0:T(8,128)(2,1)S(1)} collective-permute-done((bf16[224,512]{1,0:T(8,128)(2,1)S(1)}, bf16[224,512]{1,0:T(8,128)(2,1)S(1)}, u32[]{:S(2)}, u32[]{:S(2)}) %collective-permute-start.3) | collective-permute-done | bytes 229408 | tf_op jit(solution)/shard_map/ppermute | solution.py:287
  83.8 0.6 shard_map.61.w_ref.refs_0_
  84.3 0.0 collective-permute-done.other_ref
  84.3 0.0 copy-done.4
  84.4 2.4 %shard_map.62 = bf16[8,3,8,512]{3,2,1,0:T(8,128)(2,1)} custom-call(bf16[4,264,512]{2,1,0:T(8,128)(2,1)S(1)} %all_to_all.26.own_ref, bf16[4,264,512]{2,1,0:T(8,128)(2,1)S(1)} %collective-permute-done.other_ref, bf16[8,3,8,512]{3,2,1,0:T(8,128)(2,1)S(1)} %shard_map.61.w_ref.refs_0_), custom_call_target="tpu_custom_call" | custom-call | tf_op jit(solution)/shard_map/pallas_call | solution.py:49
  86.7 14.7 %all_to_all.27.arr_ref = bf16[8,3,8,512]{3,2,1,0:T(8,128)(2,1)S(1)} all-to-all(bf16[8,3,8,512]{3,2,1,0:T(8,128)(2,1)} %shard_map.62), channel_id=1, replica_groups=mesh['z'=8,'y'=4,'core'=2,'head'=8] {'z'}, dimensions={0} | all-to-all | bytes 393216 | tf_op jit(solution)/shard_map/all_to_all | solution.py:266
  101.5 0.9 shard_map.63
  102.4 5.2 %all-to-all-start.3 = ((bf16[32,3,8,512]{3,2,1,0:T(8,128)(2,1)}), bf16[32,3,8,512]{3,2,1,0:T(8,128)(2,1)S(1)}, u32[]{:S(2)}, u32[]{:S(2)}) async-start(bf16[32,3,8,512]{3,2,1,0:T(8,128)(2,1)} %shard_map.63), calls=%async_computation.3 | async-start | bytes 1572864 | tf_op jit(solution)/shard_map/all_to_all | solution.py:266
  107.6 5.5 %collective-permute-start.7 = (bf16[8,3,8,512]{3,2,1,0:T(8,128)(2,1)S(1)}, bf16[8,3,8,512]{3,2,1,0:T(8,128)(2,1)}, u32[]{:S(2)}, u32[]{:S(2)}) collective-permute-start(bf16[8,3,8,512]{3,2,1,0:T(8,128)(2,1)S(1)} %shard_map.61.w_ref.refs_0_), channel_id=1, source_target_pairs={{0,48},{16,32},{32,16},{48,0},{1,49},{17,33},{33,17},{49,1},{2,50}... | collective-permute-start | bytes 589832 | tf_op jit(solution)/shard_map/ppermute | solution.py:314
  113.1 2.3 %collective-permute-start.6 = (bf16[8,3,8,512]{3,2,1,0:T(8,128)(2,1)S(1)}, bf16[8,3,8,512]{3,2,1,0:T(8,128)(2,1)}, u32[]{:S(2)}, u32[]{:S(2)}) collective-permute-start(bf16[8,3,8,512]{3,2,1,0:T(8,128)(2,1)S(1)} %shard_map.61.w_ref.refs_0_), channel_id=1, source_target_pairs={{0,32},{16,48},{32,0},{48,16},{1,33},{17,49},{33,1},{49,17},{2,34}... | collective-permute-start | bytes 589832 | tf_op jit(solution)/shard_map/ppermute | solution.py:314
  115.4 4.5 %collective-permute-start.5 = (bf16[8,3,8,512]{3,2,1,0:T(8,128)(2,1)S(1)}, bf16[8,3,8,512]{3,2,1,0:T(8,128)(2,1)}, u32[]{:S(2)}, u32[]{:S(2)}) collective-permute-start(bf16[8,3,8,512]{3,2,1,0:T(8,128)(2,1)S(1)} %shard_map.61.w_ref.refs_0_), channel_id=1, source_target_pairs={{0,16},{16,0},{32,48},{48,32},{1,17},{17,1},{33,49},{49,33},{2,18}... | collective-permute-start | bytes 589832 | tf_op jit(solution)/shard_map/ppermute | solution.py:314
  119.8 21.9 %all-to-all-done.3.g_own = bf16[32,3,8,512]{3,2,1,0:T(8,128)(2,1)S(1)} async-done(((bf16[32,3,8,512]{3,2,1,0:T(8,128)(2,1)}), bf16[32,3,8,512]{3,2,1,0:T(8,128)(2,1)S(1)}, u32[]{:S(2)}, u32[]{:S(2)}) %all-to-all-start.3) | async-done | bytes 786464 | tf_op jit(solution)/shard_map/all_to_all | solution.py:266
  141.8 1.9 %collective-permute-start.4 = (bf16[32,3,8,512]{3,2,1,0:T(8,128)(2,1)S(1)}, bf16[32,3,8,512]{3,2,1,0:T(8,128)(2,1)S(1)}, u32[]{:S(2)}, u32[]{:S(2)}) collective-permute-start(bf16[32,3,8,512]{3,2,1,0:T(8,128)(2,1)S(1)} %all-to-all-done.3.g_own), channel_id=1, source_target_pairs={{0,8},{8,0},{1,9},{9,1},{2,10},{10,2},{3,11},{11,3},{4,12},{12,4},... | collective-permute-start | bytes 2359304 | tf_op jit(solution)/shard_map/ppermute | solution.py:319
  143.7 0.0 collective-permute-done.7.refs_3_
  143.7 0.0 collective-permute-done.6.refs_2_
  143.7 0.0 collective-permute-done.5.refs_1_
  143.7 0.0 copy-start.5
  143.7 0.6 copy-done.5
  144.4 1.2 shard_map.65.old_own
  145.6 0.0 copy-start.6
  145.6 2.4 %collective-permute-start.8 = (bf16[32,3,8,512]{3,2,1,0:T(8,128)(2,1)S(1)}, bf16[32,3,8,512]{3,2,1,0:T(8,128)(2,1)S(1)}, u32[]{:S(2)}, u32[]{:S(2)}) collective-permute-start(bf16[32,3,8,512]{3,2,1,0:T(8,128)(2,1)S(1)} %shard_map.65.old_own), channel_id=1, source_target_pairs={{0,8},{8,0},{1,9},{9,1},{2,10},{10,2},{3,11},{11,3},{4,12},{12,4},... | collective-permute-start | bytes 2359304 | tf_op jit(solution)/shard_map/ppermute | solution.py:318
  148.0 1.4 shard_map.66
  149.4 1.9 %collective-permute-start.9 = (bf16[128,640]{1,0:T(8,128)(2,1)S(1)}, bf16[128,640]{1,0:T(8,128)(2,1)S(1)}, u32[]{:S(2)}, u32[]{:S(2)}) collective-permute-start(bf16[128,640]{1,0:T(8,128)(2,1)S(1)} %shard_map.66), channel_id=1, source_target_pairs={{0,64},{64,128},{128,192},{192,256},{256,320},{320,384},{384,448},... | collective-permute-start | bytes 491528 | tf_op jit(solution)/shard_map/ppermute | solution.py:305
  152.0 6.7 %collective-permute-done.9.before_ref = bf16[128,640]{1,0:T(8,128)(2,1)S(1)} collective-permute-done((bf16[128,640]{1,0:T(8,128)(2,1)S(1)}, bf16[128,640]{1,0:T(8,128)(2,1)S(1)}, u32[]{:S(2)}, u32[]{:S(2)}) %collective-permute-start.9) | collective-permute-done | bytes 163872 | tf_op jit(solution)/shard_map/ppermute | solution.py:305
  158.6 0.0 copy-done.6
  158.6 1.6 shard_map.67.att_ref
  160.2 0.0 collective-permute-done.4.g_other
  160.3 6.9 %shard_map.64 = (f32[3,8,512]{2,1,0:T(8,128)}, f32[3,512,512]{2,1,0:T(8,128)S(1)}) custom-call(s32[3]{0:T(128)S(1)} %copy-done.6, f32[1]{0:T(128)S(6)} %copy.8.rate_ref, bf16[32,3,8,512]{3,2,1,0:T(8,128)(2,1)S(1)} %all-to-all-done.3.g_own, bf16[32,3,8,512]{3,2,1,0:T(8,128)(2,1)S(1)} %collective-permute-done.4.g_other, f32[3,8,512]{2,1,0:T(8,128)S(1)} %bitcast.17), custom_call_target="tpu_custom_call" | custom-call | tf_op jit(solution)/shard_map/pallas_call | solution.py:49
  167.1 0.0 collective-permute-done.8.old_other
  167.1 1.4 shard_map.68
  168.5 9.9 %all_to_all.28.arr_ref = bf16[8,16,512]{2,1,0:T(8,128)(2,1)S(1)} all-to-all(bf16[8,16,512]{2,1,0:T(8,128)(2,1)} %bitcast.19), channel_id=1, replica_groups=mesh['z'=8,'y'=4,'core'=2,'head'=8] {'head'}, dimensions={0} | all-to-all | bytes 262144 | tf_op jit(solution)/shard_map/all_to_all | solution.py:266
  178.4 0.7 shard_map.69
  (10 shorter events, 0.1 us)
Async XLA Ops:
  0.6 1.0 copy-start.1
  1.6 14.8 %copy-start.7 = (f32[128,1]{0,1:T(1,128)S(1)}, f32[128,1]{0,1:T(1,128)}, u32[]{:S(2)}) copy-start(f32[128,1]{0,1:T(1,128)} %param.5) | copy-start | bytes 1540
  17.6 33.9 %copy-start.2 = (f32[3,1,8,512]{3,2,1,0:T(8,128)S(1)}, f32[3,1,8,512]{3,2,1,0:T(8,128)}, u32[]{:S(2)}) copy-start(f32[3,1,8,512]{3,2,1,0:T(8,128)} %param.7) | copy-start | bytes 147460
  17.6 56.6 %copy-start = (bf16[128,512]{1,0:T(8,128)(2,1)S(1)}, bf16[128,512]{1,0:T(8,128)(2,1)}, u32[]{:S(2)}) copy-start(bf16[128,512]{1,0:T(8,128)(2,1)} %get-tuple-element.8.q_ref) | copy-start | bytes 393220
  49.6 34.8 %collective-permute-start = (bf16[4,264,512]{2,1,0:T(8,128)(2,1)S(1)}, bf16[4,264,512]{2,1,0:T(8,128)(2,1)S(1)}, u32[]{:S(2)}, u32[]{:S(2)}) collective-permute-start(bf16[4,264,512]{2,1,0:T(8,128)(2,1)S(1)} %all_to_all.26.own_ref), channel_id=1, source_target_pairs={{0,8},{8,0},{1,9},{9,1},{2,10},{10,2},{3,11},{11,3},{4,12},{12,4},... | collective-permute-start | bytes 3244040 | tf_op jit(solution)/shard_map/ppermute | solution.py:291
  51.5 12.8 %collective-permute-start.1 = (bf16[1,3,8,512]{3,2,1,0:T(8,128)(2,1)S(1)}, bf16[1,3,8,512]{3,2,1,0:T(8,128)(2,1)S(1)}, u32[]{:S(2)}, u32[]{:S(2)}) collective-permute-start(bf16[1,3,8,512]{3,2,1,0:T(8,128)(2,1)S(1)} %fusion), channel_id=1, source_target_pairs={{256,0},{320,64},{384,128},{448,192},{0,256},{64,320},{128,384},{1... | collective-permute-start | bytes 73736 | tf_op jit(solution)/shard_map/ppermute | solution.py:284
  64.4 9.7 %collective-permute-start.2 = (bf16[2,3,8,512]{3,2,1,0:T(8,128)(2,1)S(1)}, bf16[2,3,8,512]{3,2,1,0:T(8,128)(2,1)S(1)}, u32[]{:S(2)}, u32[]{:S(2)}) collective-permute-start(bf16[2,3,8,512]{3,2,1,0:T(8,128)(2,1)S(1)} %pad_maximum_fusion.2), channel_id=1, source_target_pairs={{128,0},{192,64},{256,128},{320,192},{384,256},{448,320},{0,384},{... | collective-permute-start | bytes 147464 | tf_op jit(solution)/shard_map/ppermute | solution.py:285
  74.2 9.6 %collective-permute-start.3 = (bf16[224,512]{1,0:T(8,128)(2,1)S(1)}, bf16[224,512]{1,0:T(8,128)(2,1)S(1)}, u32[]{:S(2)}, u32[]{:S(2)}) collective-permute-start(bf16[224,512]{1,0:T(8,128)(2,1)S(1)} %pad_maximum_fusion), channel_id=1, source_target_pairs={{64,0},{128,64},{192,128},{256,192},{320,256},{384,320},{448,384},... | collective-permute-start | bytes 688136 | tf_op jit(solution)/shard_map/ppermute | solution.py:287
  80.3 4.0 %copy-start.4 = (s32[3]{0:T(128)}, s32[3]{0:T(128)S(1)}, u32[]{:S(2)}) copy-start(s32[3]{0:T(128)S(1)} %pad_add_fusion.where_ref) | copy-start | bytes 40
  102.4 39.4 %all-to-all-start.3 = ((bf16[32,3,8,512]{3,2,1,0:T(8,128)(2,1)}), bf16[32,3,8,512]{3,2,1,0:T(8,128)(2,1)S(1)}, u32[]{:S(2)}, u32[]{:S(2)}) async-start(bf16[32,3,8,512]{3,2,1,0:T(8,128)(2,1)} %shard_map.63), calls=%async_computation.3 | async-start | bytes 1572864 | tf_op jit(solution)/shard_map/all_to_all | solution.py:266
  107.6 36.1 %collective-permute-start.7 = (bf16[8,3,8,512]{3,2,1,0:T(8,128)(2,1)S(1)}, bf16[8,3,8,512]{3,2,1,0:T(8,128)(2,1)}, u32[]{:S(2)}, u32[]{:S(2)}) collective-permute-start(bf16[8,3,8,512]{3,2,1,0:T(8,128)(2,1)S(1)} %shard_map.61.w_ref.refs_0_), channel_id=1, source_target_pairs={{0,48},{16,32},{32,16},{48,0},{1,49},{17,33},{33,17},{49,1},{2,50}... | collective-permute-start | bytes 589832 | tf_op jit(solution)/shard_map/ppermute | solution.py:314
  113.1 30.6 %collective-permute-start.6 = (bf16[8,3,8,512]{3,2,1,0:T(8,128)(2,1)S(1)}, bf16[8,3,8,512]{3,2,1,0:T(8,128)(2,1)}, u32[]{:S(2)}, u32[]{:S(2)}) collective-permute-start(bf16[8,3,8,512]{3,2,1,0:T(8,128)(2,1)S(1)} %shard_map.61.w_ref.refs_0_), channel_id=1, source_target_pairs={{0,32},{16,48},{32,0},{48,16},{1,33},{17,49},{33,1},{49,17},{2,34}... | collective-permute-start | bytes 589832 | tf_op jit(solution)/shard_map/ppermute | solution.py:314
  115.4 28.4 %collective-permute-start.5 = (bf16[8,3,8,512]{3,2,1,0:T(8,128)(2,1)S(1)}, bf16[8,3,8,512]{3,2,1,0:T(8,128)(2,1)}, u32[]{:S(2)}, u32[]{:S(2)}) collective-permute-start(bf16[8,3,8,512]{3,2,1,0:T(8,128)(2,1)S(1)} %shard_map.61.w_ref.refs_0_), channel_id=1, source_target_pairs={{0,16},{16,0},{32,48},{48,32},{1,17},{17,1},{33,49},{49,33},{2,18}... | collective-permute-start | bytes 589832 | tf_op jit(solution)/shard_map/ppermute | solution.py:314
  141.8 18.5 %collective-permute-start.4 = (bf16[32,3,8,512]{3,2,1,0:T(8,128)(2,1)S(1)}, bf16[32,3,8,512]{3,2,1,0:T(8,128)(2,1)S(1)}, u32[]{:S(2)}, u32[]{:S(2)}) collective-permute-start(bf16[32,3,8,512]{3,2,1,0:T(8,128)(2,1)S(1)} %all-to-all-done.3.g_own), channel_id=1, source_target_pairs={{0,8},{8,0},{1,9},{9,1},{2,10},{10,2},{3,11},{11,3},{4,12},{12,4},... | collective-permute-start | bytes 2359304 | tf_op jit(solution)/shard_map/ppermute | solution.py:319
  143.7 0.7 copy-start.5
  145.6 13.1 %copy-start.6 = (s32[3]{0:T(128)S(1)}, s32[3]{0:T(128)}, u32[]{:S(2)}) copy-start(s32[3]{0:T(128)} %copy-done.4) | copy-start | bytes 40
  145.6 21.5 %collective-permute-start.8 = (bf16[32,3,8,512]{3,2,1,0:T(8,128)(2,1)S(1)}, bf16[32,3,8,512]{3,2,1,0:T(8,128)(2,1)S(1)}, u32[]{:S(2)}, u32[]{:S(2)}) collective-permute-start(bf16[32,3,8,512]{3,2,1,0:T(8,128)(2,1)S(1)} %shard_map.65.old_own), channel_id=1, source_target_pairs={{0,8},{8,0},{1,9},{9,1},{2,10},{10,2},{3,11},{11,3},{4,12},{12,4},... | collective-permute-start | bytes 2359304 | tf_op jit(solution)/shard_map/ppermute | solution.py:318
  149.4 9.2 %collective-permute-start.9 = (bf16[128,640]{1,0:T(8,128)(2,1)S(1)}, bf16[128,640]{1,0:T(8,128)(2,1)S(1)}, u32[]{:S(2)}, u32[]{:S(2)}) collective-permute-start(bf16[128,640]{1,0:T(8,128)(2,1)S(1)} %shard_map.66), channel_id=1, source_target_pairs={{0,64},{64,128},{128,192},{192,256},{256,320},{320,384},{384,448},... | collective-permute-start | bytes 491528 | tf_op jit(solution)/shard_map/ppermute | solution.py:305
  160.2 6.9 %copy-start.3 = (bf16[128,512]{1,0:T(8,128)(2,1)S(1)}, bf16[128,512]{1,0:T(8,128)(2,1)}, u32[]{:S(2)}) copy-start(bf16[128,512]{1,0:T(8,128)(2,1)} %get-tuple-element.10.qn_ref) | copy-start | bytes 393220
